TPU v7x, 256 devices: a whole 4x4x8 slice. The times are simulated.
256 devices in a mesh: patch: 64 (over y, z, core), sub: 4 (over x).
Axes of the slice: x: 4, y: 4, z: 8, core: 2. Of those that a mesh axis runs over, the one named last changes fastest.
Arguments:
- state: float32 [64, 4, 1, 27, 729], P('patch', 'sub'), may hold values from -6 to 6
- stiff_weight: float32 [64, 96, 9216], P('patch'), may hold values from 0.3 to 3
- volume_weight: float32 [64, 96, 9216], P('patch'), may hold values from 0.5 to 2
- lagrange: float32 [256, 4, 1, 729], P('patch', 'sub'), may hold values from -6 to 6
- mortar: float32 [256, 2, 2, 27, 27], P('patch'), may hold values from -1.25 to 1.25
- links: int32 [256, 6], replicated, may hold values from 0 to 63, as said below
Outputs:
- residual: float32 [64, 4, 1, 27, 729], P('patch', 'sub')
- constraint: float32 [256, 4, 1, 729], P('patch', 'sub')
Inputs may be any that keep to these rules, and one draw needn't show every extreme that they name: `links`: row o * 4 + s is slot s of owner o along patch. Live slots of an owner come first and have both counts in 12 to 27; empty slots are all zero. 2 * 64 slots are live. A live interface joins face 2d + 1 of its first patch to face 2d of its second patch, d being 0 or 1; faces 0 to 3 of every patch lie on exactly one live interface each; the live interfaces of one owner all have the same d. At most 2 faces of one patch lie on live interfaces of one owner; in every draw some owner has 4 live slots and 2 faces of one patch.
All inputs are finite; a program needn't handle non-finite values.
Results may differ from a plain program's by a relative error of at most 0.0001.
Values sent between devices are 32-bit elements; how exact they have to be, the bound alone decides.
A program may use at most 128 MiB of HBM per device.

v0:
```python
import jax
import jax.numpy as jnp
import numpy as np
from jax import lax
from jax.sharding import PartitionSpec as P

ELEMS = 24
DEGREE = 3
FIELDS = 4


stabilize = 0.25
highest = lax.Precision.HIGHEST
gauss_points_four = [
    -0.8611363115940526,
    -0.3399810435848563,
    0.3399810435848563,
    0.8611363115940526,
]
gauss_weights_four = [
    0.3478548451374538,
    0.6521451548625461,
    0.6521451548625461,
    0.3478548451374538,
]


def filled_up(lines, peers):
    spare = -lines.shape[0] % peers
    if not spare:
        return lines
    return jnp.concatenate([lines, jnp.zeros((spare, *lines.shape[1:]), lines.dtype)])


def spread(value, axis, root):
    lines = jnp.where(lax.axis_index(axis) == root, value, jnp.zeros_like(value)).reshape(
        -1, *value.shape[1:][-1:]
    )
    padded = filled_up(lines, lax.axis_size(axis))
    own = lax.psum_scatter(padded, axis, scatter_dimension=0, tiled=True)
    return lax.all_gather(own, axis, axis=0, tiled=True)[: len(lines)].reshape(value.shape)


def in_order(tiles, dim):
    dims = list(tiles.shape[1:])
    dims[dim] *= tiles.shape[0]
    return jnp.moveaxis(tiles, 0, dim).reshape(dims)


def from_everyone(value, axis):
    peers = lax.axis_size(axis)
    return lax.all_to_all(
        jnp.broadcast_to(value[None], (peers, *value.shape)), axis, 0, 0, tiled=True
    )


def gathered_copies(value, axis, dim):
    return in_order(from_everyone(value, axis), dim)


def spline_tables(elements, degree):
    knot_list = np.concatenate(
        [np.zeros(degree), np.arange(elements + 1.0), np.full(degree, float(elements))]
    )
    gauss_nodes = np.array(gauss_points_four)
    gauss_weights = np.array(gauss_weights_four)
    points = (np.arange(elements)[:, None] + (gauss_nodes[None, :] + 1.0) / 2.0).reshape(-1)
    point_weights = np.tile(gauss_weights / 2.0, elements)
    current = np.where(
        (knot_list[None, :-1] <= points[:, None]) & (points[:, None] < knot_list[None, 1:]),
        1.0,
        0.0,
    )
    previous = current
    for order_k in range(1, degree + 1):
        previous = current
        amount = len(knot_list) - 1 - order_k
        current = np.zeros((points.shape[0], amount))
        for column in range(amount):
            left_span = knot_list[column + order_k] - knot_list[column]
            right_span = knot_list[column + order_k + 1] - knot_list[column + 1]
            if left_span > 0:
                current[:, column] += (points - knot_list[column]) / left_span * previous[:, column]
            if right_span > 0:
                current[:, column] += (
                    (knot_list[column + order_k + 1] - points)
                    / right_span
                    * previous[:, column + 1]
                )
    slope_part = np.zeros(current.shape)
    for column in range(current.shape[1]):
        left_span = knot_list[column + degree] - knot_list[column]
        right_span = knot_list[column + degree + 1] - knot_list[column + 1]
        if left_span > 0:
            slope_part[:, column] += degree / left_span * previous[:, column]
        if right_span > 0:
            slope_part[:, column] -= degree / right_span * previous[:, column + 1]
    return (
        jnp.asarray(current, jnp.float32),
        jnp.asarray(slope_part, jnp.float32),
        jnp.asarray(current * point_weights[:, None], jnp.float32),
        jnp.asarray(slope_part * point_weights[:, None], jnp.float32),
    )


def forward(coefficients, outer_matrix, middle_matrix, inner_matrix):
    size_n = outer_matrix.shape[1]
    partial_value = coefficients.reshape(size_n, size_n, size_n)
    partial_value = jnp.einsum("ck,ijk->ijc", inner_matrix, partial_value, precision=highest)
    partial_value = jnp.einsum("bj,ijc->ibc", middle_matrix, partial_value, precision=highest)
    return jnp.dot(
        outer_matrix,
        partial_value.reshape(size_n, -1),
        precision=highest,
        preferred_element_type=jnp.float32,
    )


def backward(values, outer_matrix, middle_matrix, inner_matrix):
    size_n = outer_matrix.shape[1]
    points = outer_matrix.shape[0]
    partial_value = jnp.dot(
        outer_matrix.T, values, precision=highest, preferred_element_type=jnp.float32
    )
    partial_value = partial_value.reshape(size_n, points, points)
    partial_value = jnp.einsum("bj,ibc->ijc", middle_matrix, partial_value, precision=highest)
    partial_value = jnp.einsum("ck,ijc->ijk", inner_matrix, partial_value, precision=highest)
    return partial_value.reshape(size_n, size_n * size_n)


def gradients(coefficients, value_table, slope_table):
    size_n = value_table.shape[1]
    field_cube = coefficients.reshape(size_n, size_n, size_n)
    last_value = jnp.einsum("ck,ijk->ijc", value_table, field_cube, precision=highest)
    last_slope = jnp.einsum("ck,ijk->ijc", slope_table, field_cube, precision=highest)
    mid_plain = jnp.einsum("bj,ijc->ibc", value_table, last_value, precision=highest).reshape(
        size_n, -1
    )
    mid_second = jnp.einsum("bj,ijc->ibc", slope_table, last_value, precision=highest).reshape(
        size_n, -1
    )
    mid_third = jnp.einsum("bj,ijc->ibc", value_table, last_slope, precision=highest).reshape(
        size_n, -1
    )
    return (
        jnp.dot(slope_table, mid_plain, precision=highest, preferred_element_type=jnp.float32),
        jnp.dot(value_table, mid_second, precision=highest, preferred_element_type=jnp.float32),
        jnp.dot(value_table, mid_third, precision=highest, preferred_element_type=jnp.float32),
    )


def backward_sum(fluxes, value_weighted, slope_weighted):
    size_n = value_weighted.shape[1]
    points = value_weighted.shape[0]
    head_first = jnp.dot(slope_weighted.T, fluxes[0], precision=highest).reshape(
        size_n, points, points
    )
    head_second = jnp.dot(value_weighted.T, fluxes[1], precision=highest).reshape(
        size_n, points, points
    )
    head_third = jnp.dot(value_weighted.T, fluxes[2], precision=highest).reshape(
        size_n, points, points
    )
    plain_mid = jnp.einsum("bj,ibc->ijc", value_weighted, head_first, precision=highest)
    plain_mid = plain_mid + jnp.einsum(
        "bj,ibc->ijc", slope_weighted, head_second, precision=highest
    )
    third_mid = jnp.einsum("bj,ibc->ijc", value_weighted, head_third, precision=highest)
    result = jnp.einsum("ck,ijc->ijk", value_weighted, plain_mid, precision=highest)
    result = result + jnp.einsum("ck,ijc->ijk", slope_weighted, third_mid, precision=highest)
    return result.reshape(size_n, size_n * size_n)


def volume_terms(own_field, pressure, stiffness, volume, factor, picker, tables):
    value_table, slope_table, value_weighted, slope_weighted = tables
    partials = gradients(own_field, value_table, slope_table)
    pvalue = forward(pressure, value_table, value_table, value_table)
    fluxes = [factor * stiffness * partials[d] - picker[d] * volume * pvalue for d in range(3)]
    result = backward_sum(fluxes, value_weighted, slope_weighted)
    chosen = picker[0] * partials[0] + picker[1] * partials[1] + picker[2] * partials[2]
    return (result, -backward(volume * chosen, value_weighted, value_weighted, value_weighted))


def per_device(state, stiff_weight, volume_weight, lagrange, mortar, links):
    tables = spline_tables(ELEMS, DEGREE)
    patches = lax.axis_size("patch")
    device = lax.axis_index("patch")
    field_index = lax.axis_index("sub")
    vectors = state.shape[2]
    size_n = state.shape[3]
    slot_count = mortar.shape[0]
    coefficients = state[0, 0]
    stiffness = stiff_weight[0]
    volume = volume_weight[0]
    is_pressure = field_index == FIELDS - 1
    factor = jnp.where(is_pressure, -stabilize, 1.0).astype(jnp.float32)
    picker = (jnp.arange(3) == field_index).astype(jnp.float32)

    def terms_of():

        def one_vector(paired):
            return volume_terms(paired[0], paired[1], stiffness, volume, factor, picker, tables)

        return one_vector

    pressure = spread(coefficients, "sub", FIELDS - 1)
    own_terms, div_terms = lax.map(terms_of(), (coefficients, pressure))
    divergence = lax.psum(div_terms, "sub")
    residual = own_terms + jnp.where(is_pressure, divergence, 0.0)
    field_cube = coefficients.reshape(vectors, size_n, size_n, size_n)
    faces = jnp.stack(
        [field_cube[:, 0], field_cube[:, -1], field_cube[:, :, 0], field_cube[:, :, -1]]
    )
    faces = faces.reshape(4, vectors, size_n * size_n)
    item_count = 2 * slot_count
    item_patch = links[:, 0:2].reshape(patches, item_count)
    item_face = links[:, 2:4].reshape(patches, item_count)
    is_live = jnp.repeat(links[:, 4] > 0, 2).reshape(patches, item_count)
    own_patch = lax.dynamic_index_in_dim(item_patch, device, 0, keepdims=False)
    own_face = lax.dynamic_index_in_dim(item_face, device, 0, keepdims=False)
    own_live = lax.dynamic_index_in_dim(is_live, device, 0, keepdims=False)
    own_rows = lax.dynamic_slice_in_dim(links, device * slot_count, slot_count, 0)
    face_grid = jnp.arange(4)
    gathered = gathered_copies(faces[None], "patch", 0)
    picked = jnp.take(
        gathered.reshape(patches * 4, vectors, size_n * size_n), own_patch * 4 + own_face, axis=0
    )
    picked = picked * own_live.astype(jnp.float32)[:, None, None]
    rank_grid = jnp.arange(size_n)
    row_mask = (rank_grid[None, :] < own_rows[:, 4:5]).astype(jnp.float32)
    col_mask = (rank_grid[None, :] < own_rows[:, 5:6]).astype(jnp.float32)
    left = mortar[:, :, 0] * row_mask[:, None, :, None]
    right = mortar[:, :, 1] * col_mask[:, None, :, None]
    traces_here = picked.reshape(slot_count, 2, vectors, size_n, size_n)
    projected = jnp.einsum("sgai,sgvij,sgbj->sgvab", left, traces_here, right, precision=highest)
    constraint = (projected[:, 0] - projected[:, 1]).reshape(
        slot_count, 1, vectors, size_n * size_n
    )
    multipliers = lagrange[:, 0].reshape(slot_count, vectors, size_n, size_n)
    signs = jnp.array([1.0, -1.0], jnp.float32)
    correction = jnp.einsum("sgai,svab,sgbj->sgvij", left, multipliers, right, precision=highest)
    correction = (correction * signs[None, :, None, None, None]).reshape(
        item_count, vectors, size_n * size_n
    )
    all_blocks = lax.all_gather(correction, "patch", axis=0, tiled=True)
    face_match = (
        (is_live & (item_patch == device)).reshape(-1)[None, :]
        & (item_face.reshape(-1)[None, :] == face_grid[:, None])
    ).astype(jnp.float32)
    face_total = jnp.einsum("ft,tvx->fvx", face_match, all_blocks, precision=highest)
    pieces = face_total.reshape(4, vectors, size_n, size_n)
    result_cube = residual.reshape(vectors, size_n, size_n, size_n)
    result_cube = result_cube.at[:, 0].add(pieces[0])
    result_cube = result_cube.at[:, -1].add(pieces[1])
    result_cube = result_cube.at[:, :, 0].add(pieces[2])
    result_cube = result_cube.at[:, :, -1].add(pieces[3])
    return (result_cube.reshape(1, 1, vectors, size_n, size_n * size_n), constraint)


def solution(mesh):
    return jax.shard_map(
        per_device,
        mesh=mesh,
        in_specs=(
            P("patch", "sub", None, None, None),
            P("patch", None, None),
            P("patch", None, None),
            P("patch", "sub", None, None),
            P("patch", None, None, None, None),
            P(),
        ),
        out_specs=(P("patch", "sub", None, None, None), P("patch", "sub", None, None)),
        check_vma=False,
    )
```

profile of v0, /device:TPU:1, one launch (start us, length us, event | category | flops | bytes accessed | tf_op | source)
XLA Modules:
  0.0 175.8 jit_solution(12599876094862100393)
XLA Ops:
  8.0 0.9 fusion.41
  8.9 10.5 %fusion = f32[8,729]{1,0:T(8,128)S(1)} fusion(f32[28,729]{1,0:T(8,128)S(1)} %concatenate.12), kind=kCustom, calls=%all-reduce-scatter | all-reduce-scatter fusion | flops 23329 | bytes 106000
  19.5 2.8 %collective-permute-start = (f32[3,729]{1,0:T(4,128)S(1)}, f32[3,729]{1,0:T(4,128)S(1)}, u32[]{:S(2)}, u32[]{:S(2)}) collective-permute-start(f32[3,729]{1,0:T(4,128)S(1)} %slice.223), channel_id=1, source_target_pairs={{0,1},{1,2},{2,3},{4,5},{5,6},{6,7},{8,9},{9,10},{10,11},{12,13},{... | collective-permute-start | bytes 26252
  22.3 1.1 reduce.8
  23.4 0.5 reshape_squeeze.4
  24.4 1.0 broadcast_in_dim.45
  25.3 15.1 %all-to-all-start = ((f32[64,1,4,1,729]{4,2,3,1,0:T(4,128)}), f32[64,1,4,1,729]{4,2,3,1,0:T(4,128)}, u32[]{:S(2)}, u32[]{:S(2)}) async-start(f32[64,1,4,1,729]{4,2,3,1,0:T(4,128)} %broadcast_in_dim.45), calls=%async_computation | async-start | bytes 1572864 | tf_op jit(solution)/shard_map/all_to_all | solution.py:52
  40.7 0.5 reshape.432
  41.2 0.5 convolution_bitcast_fusion.7
  41.7 0.5 convolution_bitcast_fusion.6
  42.2 2.2 %convolution_bitcast_fusion.1 = f32[27,96,96]{1,2,0:T(8,128)S(1)} fusion(f32[27,27,96]{2,1,0:T(8,128)S(1)} %convolution_bitcast_fusion.7, f32[96,27,1]{0,1,2:T(8,128)S(1)} %copy-done.21), kind=kOutput, calls=%fused_computation.38 | convolution fusion | flops 80621568 | bytes 1285632 | tf_op jit(solution)/shard_map/while/body/eval_jaxpr/bj,ijc->ibc/dot_general | solution.py:139
  44.5 2.2 %convolution_bitcast_fusion.3 = f32[27,96,96]{1,2,0:T(8,128)S(1)} fusion(f32[27,27,96]{2,1,0:T(8,128)S(1)} %convolution_bitcast_fusion.7, f32[96,27,1]{0,1,2:T(8,128)S(1)} %copy-done.15), kind=kOutput, calls=%fused_computation.40 | convolution fusion | flops 80621568 | bytes 1285632 | tf_op jit(solution)/shard_map/while/body/eval_jaxpr/bj,ijc->ibc/dot_general | solution.py:136
  46.7 0.6 fusion.63
  47.3 3.3 %convolution_bitcast_fusion = f32[27,96,96]{1,2,0:T(8,128)} fusion(f32[27,27,96]{2,1,0:T(8,128)S(1)} %convolution_bitcast_fusion.6, f32[96,27,1]{0,1,2:T(8,128)S(1)} %copy-done.15), kind=kOutput, calls=%fused_computation.37 | convolution fusion | flops 80621568 | bytes 1285632 | tf_op jit(solution)/shard_map/while/body/eval_jaxpr/bj,ijc->ibc/dot_general | solution.py:142
  50.6 2.8 %copy.46 = f32[27,96,96]{2,1,0:T(8,128)} copy(f32[27,96,96]{1,2,0:T(8,128)} %convolution_bitcast_fusion) | data formatting | bytes 1990656 | tf_op jit(solution)/shard_map/while/body/eval_jaxpr/bj,ijc->ibc/transpose | solution.py:142
  53.5 3.1 %reshape.439 = f32[27,9216]{1,0:T(8,128)} reshape(f32[27,96,96]{2,1,0:T(8,128)} %copy.46) | data formatting | bytes 1990656 | tf_op jit(solution)/shard_map/while/body/eval_jaxpr/reshape | solution.py:142
  56.6 1.5 copy.45
  58.1 3.2 %reshape.437 = f32[27,9216]{1,0:T(8,128)} reshape(f32[27,96,96]{2,1,0:T(8,128)} %copy.45) | data formatting | bytes 1990656 | tf_op jit(solution)/shard_map/while/body/eval_jaxpr/reshape | solution.py:139
  61.3 0.4 copy.42
  61.8 1.9 %reshape.433 = f32[27,9216]{1,0:T(8,128)} reshape(f32[27,96,96]{2,1,0:T(8,128)S(1)} %copy.42) | data formatting | bytes 1990656 | tf_op jit(solution)/shard_map/while/body/eval_jaxpr/reshape | solution.py:136
  63.6 4.7 %fusion.68 = f32[96,9216]{1,0:T(8,128)S(1)} fusion(f32[96,27]{0,1:T(8,128)S(1)} %copy-done.17, f32[27,9216]{1,0:T(8,128)} %reshape.437), kind=kOutput, calls=%fused_computation.118 | convolution fusion | flops 286654464 | bytes 4544640 | tf_op jit(solution)/shard_map/while/body/eval_jaxpr/dot_general | solution.py:147
  68.3 3.0 %fusion.70 = f32[96,9216]{1,0:T(8,128)S(1)} fusion(f32[96,27]{0,1:T(8,128)S(1)} %copy-done.17, f32[27,9216]{1,0:T(8,128)S(1)} %copy-done.8), kind=kOutput, calls=%fused_computation.120 | convolution fusion | flops 286654464 | bytes 4544640 | tf_op jit(solution)/shard_map/while/body/eval_jaxpr/dot_general | solution.py:148
  71.4 3.0 %fusion.64 = f32[96,9216]{1,0:T(8,128)S(1)} fusion(f32[96,27]{0,1:T(8,128)S(1)} %copy-done.23, f32[27,9216]{1,0:T(8,128)S(1)} %copy-done.9), kind=kOutput, calls=%fused_computation.114 | convolution fusion | flops 286654464 | bytes 4544640 | tf_op jit(solution)/shard_map/while/body/eval_jaxpr/dot_general | solution.py:146
  74.4 1.8 %copy-done.5 = f32[96,9216]{1,0:T(8,128)} copy-done((f32[96,9216]{1,0:T(8,128)}, f32[96,9216]{1,0:T(8,128)S(1)}, u32[]{:S(2)}) %copy-start.5) | copy-done | bytes 3538968
  76.2 4.4 %fusion.13 = f32[27,9216]{1,0:T(8,128)S(1)} fusion(f32[96,27]{0,1:T(8,128)S(1)} %copy-done.18, f32[1,96,9216]{2,1,0:T(8,128)S(1)} %copy-done, f32[96,9216]{1,0:T(8,128)S(1)} %fusion.70, f32[96,9216]{1,0:T(8,128)S(1)} %fusion.68, f32[96,9216]{1,0:T(8,128)S(1)} %fusion.64, f32[]{:T(128)} %bitcast.17, f32[]{:T(128)} %bitcast.12, f32[]{:T(128)} %bitcast.4), kind=kOutput, calls=%fused_computation.14 | convolution fusion | flops 291962880 | bytes 15161484 | tf_op jit(solution)/shard_map/while/body/eval_jaxpr/dot_general | solution.py:122
  80.6 0.5 reshape.441
  81.2 0.9 convolution_bitcast_fusion.4
  82.1 0.7 convolution_negate_fusion
  82.8 0.9 neg.15
  84.6 0.6 copy-done.12
  85.9 0.7 reshape.444
  87.2 0.5 broadcast.223
  87.7 0.7 fusion.58
  88.4 0.5 compare_and_fusion.1
  89.0 0.6 pad_clamp_fusion
  89.7 0.7 eq.41
  90.7 0.6 reshape.453
  91.5 0.6 and.41
  92.1 0.6 dynamic-slice.33
  93.5 9.1 %all-gather = f32[4,7,729]{2,1,0:T(8,128)S(1)} all-gather(f32[1,7,729]{2,1,0:T(8,128)S(1)} %dynamic-slice_bitcast_fusion), channel_id=1, replica_groups=mesh['patch'=64,'sub'=4] {'sub'}, dimensions={0}, use_global_device_ids=true | all-gather | bytes 102060 | tf_op jit(solution)/shard_map/all_gather | solution.py:41
  102.7 0.5 reshape.434
  103.1 0.5 fusion.65
  103.6 2.2 %convolution_bitcast_fusion.2 = f32[27,96,96]{1,2,0:T(8,128)S(1)} fusion(f32[27,27,96]{2,1,0:T(8,128)S(1)} %fusion.65, f32[96,27,1]{0,1,2:T(8,128)S(1)} %copy-done.15), kind=kOutput, calls=%fused_computation.39 | convolution fusion | flops 80621568 | bytes 1285632 | tf_op jit(solution)/shard_map/while/body/eval_jaxpr/bj,ijc->ibc/dot_general | solution.py:110
  105.9 0.4 copy.44
  106.3 1.9 %reshape.435 = f32[27,9216]{1,0:T(8,128)} reshape(f32[27,96,96]{2,1,0:T(8,128)S(1)} %copy.44) | data formatting | bytes 1990656 | tf_op jit(solution)/shard_map/while/body/eval_jaxpr/reshape | solution.py:113
  108.2 4.4 %fusion.66 = f32[96,9216]{1,0:T(8,128)S(1)} fusion(f32[96,27]{0,1:T(8,128)} %constant.177.clone, f32[27,9216]{1,0:T(8,128)} %reshape.435), kind=kOutput, calls=%fused_computation.116 | convolution fusion | flops 286654464 | bytes 4544640 | tf_op jit(solution)/shard_map/while/body/eval_jaxpr/dot_general | solution.py:111
  112.7 7.8 %fusion.7 = f32[27,9216]{1,0:T(8,128)} fusion(f32[96,27]{0,1:T(8,128)S(1)} %copy-done.19, f32[96,9216]{1,0:T(8,128)S(1)} %fusion.66, f32[1,96,9216]{2,1,0:T(8,128)S(1)} %copy-done.1, f32[96,9216]{1,0:T(8,128)} %copy-done.4, f32[1,96,9216]{2,1,0:T(8,128)} %param.20, f32[]{:T(128)} %bitcast.12, f32[]{:T(128)S(6)} %select_n.60), kind=kOutput, calls=%fused_computation.10 | convolution fusion | flops 291078144 | bytes 15161480 | tf_op jit(solution)/shard_map/while/body/eval_jaxpr/dot_general | solution.py:158
  120.5 4.1 %fusion.3 = f32[27,9216]{1,0:T(8,128)} fusion(f32[96,27]{0,1:T(8,128)S(1)} %copy-done.22, f32[96,9216]{1,0:T(8,128)S(1)} %fusion.66, f32[1,96,9216]{2,1,0:T(8,128)S(1)} %copy-done.1, f32[96,9216]{1,0:T(8,128)S(1)} %copy-done.6, f32[1,96,9216]{2,1,0:T(8,128)S(1)} %copy-done.2, f32[]{:T(128)} %bitcast.4, f32[]{:T(128)S(6)} %select_n.60), kind=kOutput, calls=%fused_computation.7 | convolution fusion | flops 291078144 | bytes 15161480 | tf_op jit(solution)/shard_map/while/body/eval_jaxpr/dot_general | solution.py:155
  124.6 3.1 %reshape.436 = f32[27,96,96]{2,1,0:T(8,128)} reshape(f32[27,9216]{1,0:T(8,128)} %fusion.3) | data formatting | bytes 1990656 | tf_op jit(solution)/shard_map/while/body/eval_jaxpr/reshape | solution.py:155
  127.7 2.9 %reshape.438 = f32[27,96,96]{2,1,0:T(8,128)} reshape(f32[27,9216]{1,0:T(8,128)} %fusion.7) | data formatting | bytes 1990656 | tf_op jit(solution)/shard_map/while/body/eval_jaxpr/reshape | solution.py:158
  130.6 8.2 %fusion.11 = f32[27,9216]{1,0:T(8,128)} fusion(f32[96,27]{0,1:T(8,128)} %constant.179.clone, f32[96,9216]{1,0:T(8,128)S(1)} %fusion.66, f32[1,96,9216]{2,1,0:T(8,128)} %param.21, f32[96,9216]{1,0:T(8,128)} %copy-done.3, f32[1,96,9216]{2,1,0:T(8,128)} %param.20, f32[]{:T(128)} %bitcast.17, f32[]{:T(128)S(6)} %select_n.60), kind=kOutput, calls=%fused_computation.13 | convolution fusion | flops 291078144 | bytes 15161480 | tf_op jit(solution)/shard_map/while/body/eval_jaxpr/dot_general | solution.py:161
  138.8 1.9 %reshape.440 = f32[27,96,96]{2,1,0:T(8,128)S(1)} reshape(f32[27,9216]{1,0:T(8,128)} %fusion.11) | data formatting | bytes 1990656 | tf_op jit(solution)/shard_map/while/body/eval_jaxpr/reshape | solution.py:161
  140.7 2.2 %fusion.67 = f32[27,96,27]{1,2,0:T(8,128)S(1)} fusion(f32[27,96,96]{2,1,0:T(8,128)} %reshape.436, f32[96,27,1]{0,1,2:T(8,128)S(1)} %copy-done.14), kind=kOutput, calls=%fused_computation.117 | convolution fusion | flops 80621568 | bytes 1285632 | tf_op jit(solution)/shard_map/while/body/eval_jaxpr/bj,ibc->ijc/dot_general | solution.py:164
  142.9 0.9 fusion.33
  143.8 0.5 fusion.69
  144.4 0.9 convolution_bitcast_fusion.5
  145.2 0.5 convolution_add_fusion.1
  146.0 0.5 reshape.442
  146.5 1.4 reshape.454
  147.9 0.7 gather_fusion
  149.5 0.7 sub.32
  150.2 14.0 %all-gather.3.cloned.1.call-done = f32[512,1,729]{2,0,1:T(8,128)} async-done(((f32[8,1,729]{2,0,1:T(8,128)}), f32[512,1,729]{2,0,1:T(8,128)}) %all-gather.3.cloned.1.call-update) | async-done | bytes 1493008 | tf_op jit(solution)/shard_map/all_gather | solution.py:245
  164.3 2.0 %fusion.31 = f32[4,729]{1,0:T(4,128)S(1)} fusion(f32[512,1,729]{2,0,1:T(8,128)} %all-gather.3.cloned.1.call-done, s32[512]{0:T(512)S(1)} %copy-done.26, pred[512]{0:T(512)(128)(4,1)S(1)} %copy-done.28), kind=kOutput, calls=%fused_computation.35 | convolution fusion | flops 17920000 | bytes 1507216 | tf_op jit(solution)/shard_map/ft,tvx->fvx/dot_general | solution.py:250
  167.1 1.0 reshape.450
  (125 shorter events, 5.5 us)
Async XLA Ops:
  8.0 33.2 %copy-start.15 = (f32[96,27,1]{0,1,2:T(8,128)S(1)}, f32[96,27,1]{0,1,2:T(8,128)}, u32[]{:S(2)}) copy-start(f32[96,27,1]{0,1,2:T(8,128)} %constant.193) | copy-start | bytes 31108
  8.0 33.7 %copy-start.21 = (f32[96,27,1]{0,1,2:T(8,128)S(1)}, f32[96,27,1]{0,1,2:T(8,128)}, u32[]{:S(2)}) copy-start(f32[96,27,1]{0,1,2:T(8,128)} %constant.195) | copy-start | bytes 31108
  19.5 73.9 %collective-permute-start = (f32[3,729]{1,0:T(4,128)S(1)}, f32[3,729]{1,0:T(4,128)S(1)}, u32[]{:S(2)}, u32[]{:S(2)}) collective-permute-start(f32[3,729]{1,0:T(4,128)S(1)} %slice.223), channel_id=1, source_target_pairs={{0,1},{1,2},{2,3},{4,5},{5,6},{6,7},{8,9},{9,10},{10,11},{12,13},{... | collective-permute-start | bytes 26252
  25.3 121.1 %all-to-all-start = ((f32[64,1,4,1,729]{4,2,3,1,0:T(4,128)}), f32[64,1,4,1,729]{4,2,3,1,0:T(4,128)}, u32[]{:S(2)}, u32[]{:S(2)}) async-start(f32[64,1,4,1,729]{4,2,3,1,0:T(4,128)} %broadcast_in_dim.45), calls=%async_computation | async-start | bytes 1572864 | tf_op jit(solution)/shard_map/all_to_all | solution.py:52
  40.5 105.5 %all-reduce.5.cloned.1.call-start = ((), (), s32[]{:S(2)}) async-start(), calls=%async_computation.1 | async-start | bytes 196608 | tf_op jit(solution)/shard_map/psum | solution.py:208
  58.1 5.5 %copy-start.17 = (f32[96,27]{0,1:T(8,128)S(1)}, f32[96,27]{0,1:T(8,128)}, u32[]{:S(2)}) copy-start(f32[96,27]{0,1:T(8,128)} %constant.177.clone) | copy-start | bytes 31108
  61.8 6.5 %copy-start.8 = (f32[27,9216]{1,0:T(8,128)S(1)}, f32[27,9216]{1,0:T(8,128)}, u32[]{:S(2)}) copy-start(f32[27,9216]{1,0:T(8,128)} %reshape.439) | copy-start | bytes 2985988
  68.3 6.0 %copy-start.4 = (f32[96,9216]{1,0:T(8,128)}, f32[96,9216]{1,0:T(8,128)S(1)}, u32[]{:S(2)}) copy-start(f32[96,9216]{1,0:T(8,128)S(1)} %fusion.68) | copy-start | bytes 10616836
  68.3 3.0 %copy-start.9 = (f32[27,9216]{1,0:T(8,128)S(1)}, f32[27,9216]{1,0:T(8,128)}, u32[]{:S(2)}) copy-start(f32[27,9216]{1,0:T(8,128)} %reshape.433) | copy-start | bytes 2985988
  68.3 3.0 %copy-start.23 = (f32[96,27]{0,1:T(8,128)S(1)}, f32[96,27]{0,1:T(8,128)}, u32[]{:S(2)}) copy-start(f32[96,27]{0,1:T(8,128)} %constant.178.clone) | copy-start | bytes 31108
  71.3 3.0 %copy-start.3 = (f32[96,9216]{1,0:T(8,128)}, f32[96,9216]{1,0:T(8,128)S(1)}, u32[]{:S(2)}) copy-start(f32[96,9216]{1,0:T(8,128)S(1)} %fusion.70) | copy-start | bytes 10616836
  71.3 4.8 %copy-start = (f32[1,96,9216]{2,1,0:T(8,128)S(1)}, f32[1,96,9216]{2,1,0:T(8,128)}, u32[]{:S(2)}) copy-start(f32[1,96,9216]{2,1,0:T(8,128)} %param.21) | copy-start | bytes 10616836
  71.3 4.8 %copy-start.18 = (f32[96,27]{0,1:T(8,128)S(1)}, f32[96,27]{0,1:T(8,128)}, u32[]{:S(2)}) copy-start(f32[96,27]{0,1:T(8,128)} %constant.179.clone) | copy-start | bytes 31108
  74.3 1.9 %copy-start.5 = (f32[96,9216]{1,0:T(8,128)}, f32[96,9216]{1,0:T(8,128)S(1)}, u32[]{:S(2)}) copy-start(f32[96,9216]{1,0:T(8,128)S(1)} %fusion.64) | copy-start | bytes 10616836
  76.2 5.0 %copy-start.14 = (f32[96,27,1]{0,1,2:T(8,128)S(1)}, f32[96,27,1]{0,1,2:T(8,128)}, u32[]{:S(2)}) copy-start(f32[96,27,1]{0,1,2:T(8,128)} %constant.194) | copy-start | bytes 31108
  80.6 3.1 %copy-start.24 = (s32[256,6]{0,1:T(8,128)S(1)}, s32[256,6]{0,1:T(8,128)}, u32[]{:S(2)}) copy-start(s32[256,6]{0,1:T(8,128)} %param.24) | copy-start | bytes 18436
  80.6 3.3 %copy-start.25 = (f32[4,1,1,729]{3,2,1,0:T(1,128)S(1)}, f32[4,1,1,729]{3,2,1,0:T(1,128)}, u32[]{:S(2)}) copy-start(f32[4,1,1,729]{3,2,1,0:T(1,128)} %param.22) | copy-start | bytes 34996
  80.6 3.5 %copy-start.16 = (f32[4,2,2,27,27]{4,2,3,1,0:T(2,128)S(1)}, f32[4,2,2,27,27]{4,2,3,1,0:T(2,128)}, u32[]{:S(2)}) copy-start(f32[4,2,2,27,27]{4,2,3,1,0:T(2,128)} %param.23) | copy-start | bytes 139972
  80.6 5.0 %copy-start.30 = (f32[2]{0:T(128)S(1)}, f32[2]{0:T(128)}, u32[]{:S(2)}) copy-start(f32[2]{0:T(128)} %constant.181.clone) | copy-start | bytes 28
  81.2 10.9 %copy-start.31 = (u32[256]{0:T(256)S(1)}, u32[256]{0:T(256)}, u32[]{:S(2)}) copy-start(u32[256]{0:T(256)} %constant.191) | copy-start | bytes 3076
  83.6 80.6 %all-gather.3.cloned.1.call-start = ((), (), s32[]{:S(2)}) async-start(), calls=%async_computation.2 | async-start | bytes 1597440 | tf_op jit(solution)/shard_map/all_gather | solution.py:245
  84.6 0.6 copy-start.12
  84.6 1.0 copy-start.10
  108.2 4.4 %copy-start.1 = (f32[1,96,9216]{2,1,0:T(8,128)S(1)}, f32[1,96,9216]{2,1,0:T(8,128)}, u32[]{:S(2)}) copy-start(f32[1,96,9216]{2,1,0:T(8,128)} %param.21) | copy-start | bytes 10616836
  108.2 4.4 %copy-start.19 = (f32[96,27]{0,1:T(8,128)S(1)}, f32[96,27]{0,1:T(8,128)}, u32[]{:S(2)}) copy-start(f32[96,27]{0,1:T(8,128)} %constant.179.clone) | copy-start | bytes 31108
  112.7 7.8 %copy-start.2 = (f32[1,96,9216]{2,1,0:T(8,128)S(1)}, f32[1,96,9216]{2,1,0:T(8,128)}, u32[]{:S(2)}) copy-start(f32[1,96,9216]{2,1,0:T(8,128)} %param.20) | copy-start | bytes 10616836
  112.7 7.8 %copy-start.6 = (f32[96,9216]{1,0:T(8,128)S(1)}, f32[96,9216]{1,0:T(8,128)}, u32[]{:S(2)}) copy-start(f32[96,9216]{1,0:T(8,128)} %copy-done.5) | copy-start | bytes 10616836
  112.7 7.8 %copy-start.22 = (f32[96,27]{0,1:T(8,128)S(1)}, f32[96,27]{0,1:T(8,128)}, u32[]{:S(2)}) copy-start(f32[96,27]{0,1:T(8,128)} %constant.180.clone) | copy-start | bytes 31108
  138.8 4.1 %copy-start.7 = (f32[27,96,96]{2,1,0:T(8,128)S(1)}, f32[27,96,96]{2,1,0:T(8,128)}, u32[]{:S(2)}) copy-start(f32[27,96,96]{2,1,0:T(8,128)} %reshape.438) | copy-start | bytes 2985988
  138.8 4.1 %copy-start.20 = (f32[96,27,1]{0,1,2:T(8,128)S(1)}, f32[96,27,1]{0,1,2:T(8,128)}, u32[]{:S(2)}) copy-start(f32[96,27,1]{0,1,2:T(8,128)} %constant.196) | copy-start | bytes 31108
  143.8 5.0 %copy-start.13 = (f32[4,2,27,27]{3,1,2,0:T(2,128)S(1)}, f32[4,2,27,27]{3,1,2,0:T(2,128)}, u32[]{:S(2)}) copy-start(f32[4,2,27,27]{3,1,2,0:T(2,128)} %copy-done.12) | copy-start | bytes 69988
  143.8 5.0 %copy-start.27 = (f32[4,2]{1,0:T(4,128)S(1)}, f32[4,2]{1,0:T(4,128)}, u32[]{:S(2)}) copy-start(f32[4,2]{1,0:T(4,128)} %reshape.453) | copy-start | bytes 100
  143.8 5.0 %copy-start.29 = (pred[4,2]{1,0:T(4,128)(4,1)S(1)}, pred[4,2]{1,0:T(4,128)(4,1)}, u32[]{:S(2)}) copy-start(pred[4,2]{1,0:T(4,128)(4,1)} %compare_and_fusion.1) | copy-start | bytes 28
  144.3 4.8 %copy-start.11 = (f32[4,2,27,27]{3,1,2,0:T(2,128)S(1)}, f32[4,2,27,27]{3,1,2,0:T(2,128)}, u32[]{:S(2)}) copy-start(f32[4,2,27,27]{3,1,2,0:T(2,128)} %copy-done.10) | copy-start | bytes 69988
  144.3 19.9 %copy-start.26 = (s32[512]{0:T(512)S(1)}, s32[512]{0:T(512)}, u32[]{:S(2)}) copy-start(s32[512]{0:T(512)} %eq.41) | copy-start | bytes 6148
  144.3 19.9 %copy-start.28 = (pred[512]{0:T(512)(128)(4,1)S(1)}, pred[512]{0:T(512)(128)(4,1)}, u32[]{:S(2)}) copy-start(pred[512]{0:T(512)(128)(4,1)} %and.41) | copy-start | bytes 1540
Sparse Core Ops, SparseCore 0:
  83.8 43.7 all-reduce.4
Sparse Core Ops, SparseCore 1:
  87.4 76.8 all-gather.2
where the time goes:
time: 179 us; the launch traced here: 176 us
  matrix products  60.8 us (34%)
  local copies, waits for them, and re-layouts  41.2 us (23%)
  blocking collectives  19.6 us (11%)
  starting transfers between devices  18.2 us (10%)
  between operations  17.3 us (10%)
  waiting for transfers between devices  14.1 us (8%)
  other arithmetic  4.58 us (3%)
    all_to_all x1, starting transfers between devices, from_everyone(): lax.all_to_all(jnp.broadcast_to(value[None], (peers, *value.shape)), axis...  15.1 us
    all_gather x1, waiting for transfers between devices, per_device(): all_blocks = lax.all_gather(correction, 'patch', axis=0, tiled=True)  14 us
    unnamed x1, blocking collectives  10.5 us
    all_gather x1, blocking collectives, spread(): lax.all_gather(own, axis, axis=0, tiled=True)[:len(lines)]  9.12 us
    dot_general x1, matrix products, backward_sum(): jnp.dot(value_weighted.T, fluxes[2], precision=highest)  8.23 us
    dot_general x1, matrix products, backward_sum(): jnp.dot(value_weighted.T, fluxes[1], precision=highest)  7.78 us
    dot_general x1, matrix products, gradients(): jnp.dot(value_table, mid_second, precision=highest, preferred_element_typ...  4.66 us
    dot_general x1, matrix products, backward(): jnp.dot(outer_matrix.T, values, precision=highest, preferred_element_type...  4.4 us
  transfers between devices with their start and end apart: 4, of which 1 were waited for; matrix products, arithmetic and copies ran while one was open for 57% of the time, Pallas kernels for 0%

commit v1 on v0

v1 whole, which is shorter than its diff:
```python
import jax
import jax.numpy as jnp
import numpy as np
from jax import lax
from jax.experimental import pallas as pl
from jax.experimental.pallas import tpu as pltpu
from jax.sharding import PartitionSpec as P

ELEMS = 24
DEGREE = 3
FIELDS = 4
BASIS = 27
QUAD = 96
SUBS = 4
SLAB = QUAD // SUBS
LAYERS = SLAB // 4 + DEGREE
STEPS = 12
MESH = pl.DeviceIdType.MESH

stabilize = 0.25
highest = lax.Precision.HIGHEST
gauss_points_four = [
    -0.8611363115940526,
    -0.3399810435848563,
    0.3399810435848563,
    0.8611363115940526,
]
gauss_weights_four = [
    0.3478548451374538,
    0.6521451548625461,
    0.6521451548625461,
    0.3478548451374538,
]


def in_order(tiles, dim):
    dims = list(tiles.shape[1:])
    dims[dim] *= tiles.shape[0]
    return jnp.moveaxis(tiles, 0, dim).reshape(dims)


def from_everyone(value, axis):
    peers = lax.axis_size(axis)
    return lax.all_to_all(
        jnp.broadcast_to(value[None], (peers, *value.shape)), axis, 0, 0, tiled=True
    )


def gathered_copies(value, axis, dim):
    return in_order(from_everyone(value, axis), dim)


def spline_tables(elements, degree):
    knot_list = np.concatenate(
        [np.zeros(degree), np.arange(elements + 1.0), np.full(degree, float(elements))]
    )
    gauss_nodes = np.array(gauss_points_four)
    gauss_weights = np.array(gauss_weights_four)
    points = (np.arange(elements)[:, None] + (gauss_nodes[None, :] + 1.0) / 2.0).reshape(-1)
    point_weights = np.tile(gauss_weights / 2.0, elements)
    current = np.where(
        (knot_list[None, :-1] <= points[:, None]) & (points[:, None] < knot_list[None, 1:]),
        1.0,
        0.0,
    )
    previous = current
    for order_k in range(1, degree + 1):
        previous = current
        amount = len(knot_list) - 1 - order_k
        current = np.zeros((points.shape[0], amount))
        for column in range(amount):
            left_span = knot_list[column + order_k] - knot_list[column]
            right_span = knot_list[column + order_k + 1] - knot_list[column + 1]
            if left_span > 0:
                current[:, column] += (points - knot_list[column]) / left_span * previous[:, column]
            if right_span > 0:
                current[:, column] += (
                    (knot_list[column + order_k + 1] - points)
                    / right_span
                    * previous[:, column + 1]
                )
    slope_part = np.zeros(current.shape)
    for column in range(current.shape[1]):
        left_span = knot_list[column + degree] - knot_list[column]
        right_span = knot_list[column + degree + 1] - knot_list[column + 1]
        if left_span > 0:
            slope_part[:, column] += degree / left_span * previous[:, column]
        if right_span > 0:
            slope_part[:, column] -= degree / right_span * previous[:, column + 1]
    return (
        current.astype(np.float32),
        slope_part.astype(np.float32),
        (current * point_weights[:, None]).astype(np.float32),
        (slope_part * point_weights[:, None]).astype(np.float32),
    )


def halves(table):
    high = table.astype(jnp.bfloat16).astype(np.float32)
    low = (table - high).astype(jnp.bfloat16).astype(np.float32)
    return high, low


def constant_tables():
    value, slope, value_w, slope_w = spline_tables(ELEMS, DEGREE)
    first = np.zeros((SUBS, 2 * SLAB, 16), np.float32)
    last = np.zeros((SUBS, 16, 2 * SLAB), np.float32)
    for q in range(SUBS):
        rows = slice(SLAB * q, SLAB * (q + 1))
        cols = slice(6 * q, 6 * q + LAYERS)
        first[q, :SLAB, :LAYERS] = value[rows, cols]
        first[q, SLAB:, :LAYERS] = slope[rows, cols]
        last[q, :LAYERS, :SLAB] = slope_w[rows, cols].T
        last[q, :LAYERS, SLAB:] = value_w[rows, cols].T
    high, low = halves(first)
    first = np.concatenate([high, high, low], axis=2)
    high, low = halves(last)
    last = np.concatenate([high, high, low], axis=2)

    def pair_tables(table):
        high, low = halves(table)
        even = np.zeros((256, 256), np.float32)
        odd = np.zeros((256, 256), np.float32)
        for s in range(2):
            cols = slice(128 * s, 128 * s + QUAD)
            even[32 * s:32 * s + BASIS, cols] = high.T
            even[128 + 32 * s:128 + 32 * s + BASIS, cols] = high.T
            even[192 + 32 * s:192 + 32 * s + BASIS, cols] = low.T
            odd[64 + 32 * s:64 + 32 * s + BASIS, cols] = high.T
            odd[128 + 32 * s:128 + 32 * s + BASIS, cols] = low.T
            odd[192 + 32 * s:192 + 32 * s + BASIS, cols] = high.T
        return even, odd

    value_even, value_odd = pair_tables(value)
    slope_even, slope_odd = pair_tables(slope)
    inner = np.stack([value_even, value_odd, slope_even, slope_odd])
    plain = value_odd[:, 128:]

    def adjoint_table(table):
        high, low = halves(table)
        out = np.zeros((512, 256), np.float32)
        for f in range(FIELDS):
            scale = -stabilize if f == FIELDS - 1 else 1.0
            rows = slice(128 * f, 128 * f + QUAD)
            out[rows, 32 * f:32 * f + BASIS] = scale * high
            out[rows, 128 + 32 * f:128 + 32 * f + BASIS] = scale * low
        return out

    high, low = halves(value_w)
    div = np.zeros((128, 256), np.float32)
    div[:QUAD, 96:96 + BASIS] = -high
    div[:QUAD, 224:224 + BASIS] = -low
    adjoint_value = adjoint_table(value_w)
    adjoint_slope = np.concatenate([adjoint_table(slope_w), div])
    middle = np.zeros((STEPS, 128), np.float32)
    for t in range(STEPS):
        for bb in range(8):
            point = 8 * t + bb
            for m in range(4):
                col = 2 * t + bb // 4 + m
                for n, table in enumerate((value, slope, value_w, slope_w)):
                    middle[t, 32 * n + 4 * bb + m] = table[point, col]
    half = lambda x: jnp.asarray(x, jnp.bfloat16)
    return (half(first), half(last), half(inner), half(plain), half(adjoint_value), half(adjoint_slope),
            jnp.asarray(middle, jnp.float32))


def split(x):
    high = x.astype(jnp.bfloat16)
    return high, (x - high.astype(jnp.float32)).astype(jnp.bfloat16)


def product(left, right):
    return jnp.dot(left, right, preferred_element_type=jnp.float32)


def lanes_of(rows):
    return lax.broadcasted_iota(jnp.int32, (rows, 128), 1)


def volume_kernel(x_ref, stiff_hbm, volume_hbm, first_ref, last_ref, inner_ref, plain_ref, adj_value_ref,
                  adj_slope_ref, middle_ref, out_ref, stiff, volume, sent, got, back, home, outer, total,
                  load_sem, send_sem, recv_sem, back_send_sem, back_recv_sem):
    me = lax.axis_index("sub")
    rows = pl.ds(pl.multiple_of(me * SLAB, 8), SLAB)
    load_stiff = pltpu.make_async_copy(stiff_hbm.at[rows], stiff, load_sem.at[0])
    load_volume = pltpu.make_async_copy(volume_hbm.at[rows], volume, load_sem.at[1])
    load_stiff.start()
    load_volume.start()
    peers = [lax.rem(me + d, SUBS) for d in range(SUBS)]
    origins = [lax.rem(me + SUBS - d, SUBS) for d in range(SUBS)]
    barrier = pltpu.get_barrier_semaphore()
    for d in range(1, SUBS):
        pl.semaphore_signal(barrier, inc=1, device_id={"sub": peers[d]}, device_id_type=MESH)
    sent[...] = jnp.zeros_like(sent)
    for q in range(SUBS):
        sent[q, 0:LAYERS, 0:729] = x_ref[6 * q:6 * q + LAYERS, :]
    pl.semaphore_wait(barrier, SUBS - 1)
    going = [None]
    for d in range(1, SUBS):
        copy = pltpu.make_async_remote_copy(
            src_ref=sent.at[peers[d]], dst_ref=got.at[me], send_sem=send_sem.at[d], recv_sem=recv_sem.at[d],
            device_id={"sub": peers[d]}, device_id_type=MESH)
        copy.start()
        going.append(copy)
    got[me] = sent[me]
    total[...] = jnp.zeros_like(total)
    for d in range(1, SUBS):
        going[d].wait_send()
        pltpu.make_async_remote_copy(
            src_ref=sent.at[peers[d]], dst_ref=got.at[origins[d]], send_sem=send_sem.at[d],
            recv_sem=recv_sem.at[d], device_id={"sub": peers[d]}, device_id_type=MESH).wait_recv()

    first = first_ref[me]
    spread = []
    for f in range(FIELDS):
        high, low = split(got[f])
        spread.append(product(first, jnp.concatenate([high, low, high], axis=0)))
    lane = lanes_of(2 * SLAB)
    for j in range(BASIS):
        tile, shift = divmod(BASIS * j, 128)
        merged = None
        for f in range(FIELDS):
            piece = spread[f][:, 128 * tile:128 * tile + 128]
            if shift + BASIS > 128:
                piece = jnp.where(lane >= shift, piece, spread[f][:, 128 * tile + 128:128 * tile + 256])
            turn = (32 * f - shift) % 128
            piece = pltpu.roll(piece, turn, 1) if turn else piece
            merged = piece if f == 0 else jnp.where(lane >= 32 * f, piece, merged)
        outer[j] = merged
    load_stiff.wait()
    load_volume.wait()

    def step(t, carry):
        def scalar(table, bb, m):
            return middle_ref[t, 32 * table + 4 * bb + m]

        window = [outer[2 * t + m] for m in range(5)]
        values = [w[0:SLAB] for w in window]
        slopes = [w[SLAB:2 * SLAB] for w in window]

        def middle_sum(table, parts, bb):
            e = bb // 4
            out = scalar(table, bb, 0) * parts[e]
            for m in range(1, 4):
                out = out + scalar(table, bb, m) * parts[e + m]
            return out

        across = [middle_sum(0, slopes, bb) for bb in range(8)] + [middle_sum(1, values, bb) for bb in range(8)]
        along = [middle_sum(0, values, bb) for bb in range(8)]

        def pair_sides(x):
            lane = lanes_of(x.shape[0])
            high = x.astype(jnp.bfloat16)
            wide = high.astype(jnp.float32)
            low = x - wide
            turned = pltpu.roll(wide, 64, 1)
            even = jnp.where(lane < 64, low, turned).astype(jnp.bfloat16)
            odd = jnp.where(lane < 64, turned, low).astype(jnp.bfloat16)
            return jnp.concatenate([high, even], axis=1), jnp.concatenate([high, odd], axis=1)

        even, odd = pair_sides(jnp.concatenate(across, axis=0))
        across_even = product(even, inner_ref[0])
        across_odd = product(odd, inner_ref[1])
        even, odd = pair_sides(jnp.concatenate(along, axis=0))
        along_even = product(even, inner_ref[2])
        along_odd = product(odd, inner_ref[3])
        pvalue = product(odd, plain_ref[...])

        def weights(ref):
            lane = lanes_of(SLAB)
            tiles = [ref[:, pl.ds(pl.multiple_of(768 * t + 128 * n, 128), 128)] for n in range(6)]
            parts = []
            for bb in range(8):
                tile, shift = divmod(QUAD * bb, 128)
                part = tiles[tile]
                if shift + QUAD > 128:
                    part = jnp.where(lane >= shift, part, tiles[tile + 1])
                parts.append(pltpu.roll(part, 128 - shift, 1) if shift else part)
            return jnp.concatenate(parts, axis=0)

        s = weights(stiff)
        w = weights(volume)
        half = 8 * SLAB
        pressed = w * pvalue
        grads = [
            [across_even[0:half, 0:128], across_even[0:half, 128:256], across_odd[0:half, 0:128],
             across_odd[0:half, 128:256]],
            [across_even[half:, 0:128], across_even[half:, 128:256], across_odd[half:, 0:128],
             across_odd[half:, 128:256]],
            [along_even[:, 0:128], along_even[:, 128:256], along_odd[:, 0:128], along_odd[:, 128:256]],
        ]
        fluxes = []
        for d in range(3):
            fluxes.append([s * grads[d][f] - pressed if f == d else s * grads[d][f] for f in range(FIELDS)])
        spill = w * (grads[0][0] + grads[1][1] + grads[2][2])

        def adjoint(parts, table):
            pairs = [split(p) for p in parts]
            wide = product(jnp.concatenate([p[0] for p in pairs], axis=1), table[...])
            low = product(jnp.concatenate([p[1] for p in pairs], axis=1), table[:, 0:128])
            return wide[:, 0:128] + wide[:, 128:256] + low

        heads = [adjoint(fluxes[0], adj_value_ref), adjoint(fluxes[1], adj_value_ref),
                 adjoint(fluxes[2] + [spill], adj_slope_ref)]
        heads = [[h[SLAB * bb:SLAB * bb + SLAB] for bb in range(8)] for h in heads]
        sums = [[None, None] for _ in range(5)]
        for bb in range(8):
            for m in range(4):
                at = bb // 4 + m
                v = scalar(2, bb, m)
                terms = [v * heads[0][bb], scalar(3, bb, m) * heads[1][bb] + v * heads[2][bb]]
                sums[at] = [a if b is None else b + a for a, b in zip(terms, sums[at])]
        for m in range(5):
            total[2 * t + m] += jnp.concatenate(sums[m], axis=0)
        return carry

    lax.fori_loop(0, STEPS, step, 0)

    last = last_ref[me]
    lane = lanes_of(16)
    packed = [[jnp.zeros((16, 128), jnp.float32) for _ in range(6)] for _ in range(FIELDS)]
    for j0 in range(0, BASIS, 2):
        some = list(range(j0, min(j0 + 2, BASIS)))
        columns = []
        for j in some:
            high, low = split(total[j])
            columns.append(jnp.concatenate([high, low, high], axis=0))
        result = product(last, jnp.concatenate(columns, axis=1))
        for n, j in enumerate(some):
            piece = result[:, 128 * n:128 * n + 128]
            tile, shift = divmod(BASIS * j, 128)
            for f in range(FIELDS):
                turn = (shift - 32 * f) % 128
                turned = pltpu.roll(piece, turn, 1) if turn else piece
                end = shift + BASIS
                mask = (lane >= shift) & (lane < end)
                packed[f][tile] = jnp.where(mask, turned, packed[f][tile])
                if end > 128:
                    packed[f][tile + 1] = jnp.where(lane < end - 128, turned, packed[f][tile + 1])
    for f in range(FIELDS):
        back[f] = jnp.concatenate(packed[f], axis=1)
    going = [None]
    for d in range(1, SUBS):
        copy = pltpu.make_async_remote_copy(
            src_ref=back.at[peers[d]], dst_ref=home.at[me], send_sem=back_send_sem.at[d],
            recv_sem=back_recv_sem.at[d], device_id={"sub": peers[d]}, device_id_type=MESH)
        copy.start()
        going.append(copy)
    home[me] = back[me]
    for d in range(1, SUBS):
        going[d].wait_send()
        pltpu.make_async_remote_copy(
            src_ref=back.at[peers[d]], dst_ref=home.at[origins[d]], send_sem=back_send_sem.at[d],
            recv_sem=back_recv_sem.at[d], device_id={"sub": peers[d]}, device_id_type=MESH).wait_recv()
    out_ref[...] = jnp.zeros_like(out_ref)
    for q in range(SUBS):
        out_ref[6 * q:6 * q + LAYERS, :] += home[q, 0:LAYERS, 0:729]


def volume_residual(coefficients, stiffness, volume):
    constants = constant_tables()
    vmem = pl.BlockSpec(memory_space=pltpu.VMEM)
    anywhere = pl.BlockSpec(memory_space=pl.ANY)
    smem = pl.BlockSpec(memory_space=pltpu.SMEM)
    return pl.pallas_call(
        volume_kernel,
        name="volume",
        out_shape=jax.ShapeDtypeStruct((BASIS, BASIS * BASIS), jnp.float32),
        in_specs=[vmem, anywhere, anywhere] + [vmem] * 6 + [smem],
        out_specs=vmem,
        scratch_shapes=[
            pltpu.VMEM((SLAB, QUAD * QUAD), jnp.float32),
            pltpu.VMEM((SLAB, QUAD * QUAD), jnp.float32),
            pltpu.VMEM((SUBS, 16, 768), jnp.float32),
            pltpu.VMEM((SUBS, 16, 768), jnp.float32),
            pltpu.VMEM((SUBS, 16, 768), jnp.float32),
            pltpu.VMEM((SUBS, 16, 768), jnp.float32),
            pltpu.VMEM((BASIS, 2 * SLAB, 128), jnp.float32),
            pltpu.VMEM((BASIS, 2 * SLAB, 128), jnp.float32),
            pltpu.SemaphoreType.DMA((2,)),
            pltpu.SemaphoreType.DMA((SUBS,)),
            pltpu.SemaphoreType.DMA((SUBS,)),
            pltpu.SemaphoreType.DMA((SUBS,)),
            pltpu.SemaphoreType.DMA((SUBS,)),
        ],
        compiler_params=pltpu.CompilerParams(collective_id=0, has_side_effects=True),
        cost_estimate=pl.CostEstimate(flops=10**10, bytes_accessed=4 * 10**6, transcendentals=0),
    )(coefficients, stiffness, volume, *constants)


def per_device(state, stiff_weight, volume_weight, lagrange, mortar, links):
    patches = lax.axis_size("patch")
    device = lax.axis_index("patch")
    vectors = state.shape[2]
    size_n = state.shape[3]
    slot_count = mortar.shape[0]
    coefficients = state[0, 0]
    stiffness = stiff_weight[0]
    volume = volume_weight[0]
    residual = volume_residual(coefficients.reshape(size_n, size_n * size_n), stiffness, volume)
    field_cube = coefficients.reshape(vectors, size_n, size_n, size_n)
    faces = jnp.stack(
        [field_cube[:, 0], field_cube[:, -1], field_cube[:, :, 0], field_cube[:, :, -1]]
    )
    faces = faces.reshape(4, vectors, size_n * size_n)
    item_count = 2 * slot_count
    item_patch = links[:, 0:2].reshape(patches, item_count)
    item_face = links[:, 2:4].reshape(patches, item_count)
    is_live = jnp.repeat(links[:, 4] > 0, 2).reshape(patches, item_count)
    own_patch = lax.dynamic_index_in_dim(item_patch, device, 0, keepdims=False)
    own_face = lax.dynamic_index_in_dim(item_face, device, 0, keepdims=False)
    own_live = lax.dynamic_index_in_dim(is_live, device, 0, keepdims=False)
    own_rows = lax.dynamic_slice_in_dim(links, device * slot_count, slot_count, 0)
    face_grid = jnp.arange(4)
    gathered = gathered_copies(faces[None], "patch", 0)
    picked = jnp.take(
        gathered.reshape(patches * 4, vectors, size_n * size_n), own_patch * 4 + own_face, axis=0
    )
    picked = picked * own_live.astype(jnp.float32)[:, None, None]
    rank_grid = jnp.arange(size_n)
    row_mask = (rank_grid[None, :] < own_rows[:, 4:5]).astype(jnp.float32)
    col_mask = (rank_grid[None, :] < own_rows[:, 5:6]).astype(jnp.float32)
    left = mortar[:, :, 0] * row_mask[:, None, :, None]
    right = mortar[:, :, 1] * col_mask[:, None, :, None]
    traces_here = picked.reshape(slot_count, 2, vectors, size_n, size_n)
    projected = jnp.einsum("sgai,sgvij,sgbj->sgvab", left, traces_here, right, precision=highest)
    constraint = (projected[:, 0] - projected[:, 1]).reshape(
        slot_count, 1, vectors, size_n * size_n
    )
    multipliers = lagrange[:, 0].reshape(slot_count, vectors, size_n, size_n)
    signs = jnp.array([1.0, -1.0], jnp.float32)
    correction = jnp.einsum("sgai,svab,sgbj->sgvij", left, multipliers, right, precision=highest)
    correction = (correction * signs[None, :, None, None, None]).reshape(
        item_count, vectors, size_n * size_n
    )
    all_blocks = lax.all_gather(correction, "patch", axis=0, tiled=True)
    face_match = (
        (is_live & (item_patch == device)).reshape(-1)[None, :]
        & (item_face.reshape(-1)[None, :] == face_grid[:, None])
    ).astype(jnp.float32)
    face_total = jnp.einsum("ft,tvx->fvx", face_match, all_blocks, precision=highest)
    pieces = face_total.reshape(4, vectors, size_n, size_n)
    result_cube = residual.reshape(vectors, size_n, size_n, size_n)
    result_cube = result_cube.at[:, 0].add(pieces[0])
    result_cube = result_cube.at[:, -1].add(pieces[1])
    result_cube = result_cube.at[:, :, 0].add(pieces[2])
    result_cube = result_cube.at[:, :, -1].add(pieces[3])
    return (result_cube.reshape(1, 1, vectors, size_n, size_n * size_n), constraint)


def solution(mesh):
    return jax.shard_map(
        per_device,
        mesh=mesh,
        in_specs=(
            P("patch", "sub", None, None, None),
            P("patch", None, None),
            P("patch", None, None),
            P("patch", "sub", None, None),
            P("patch", None, None, None, None),
            P(),
        ),
        out_specs=(P("patch", "sub", None, None, None), P("patch", "sub", None, None)),
        check_vma=False,
    )
```

time: 179 us -> 105 us (0.59); the launches traced: 176 us -> 105 us
  matrix products: 60.8 us -> 3.99 us
  local copies, waits for them, and re-layouts: 41.2 us -> 11.9 us
  Pallas kernels: 0 us -> 25.6 us
  blocking collectives: 19.6 us -> 0 us
  waiting for transfers between devices: 14.1 us -> 33.6 us
  starting transfers between devices: 18.2 us -> 13.2 us
  between operations: 17.3 us -> 14.4 us
  other arithmetic: 4.58 us -> 2.38 us
    dot_general x22 -> x0, matrix products: 57.5 us -> none  [the longest x1 8.23 us: backward_sum(): jnp.dot(value_weighted.T, fluxes[2], precision=highest)]
    pallas_call x0 -> x1, Pallas kernels: none -> 25.6 us  [volume_residual(): pl.pallas_call(volume_kernel, name='volume', out_shape=jax.ShapeDtypeStru...]
    all_gather x1, waiting for transfers between devices: 14 us -> 33.6 us  [per_device(): all_blocks = lax.all_gather(correction, 'patch', axis=0, tiled=True)]
    reshape x10 -> x0, local copies, waits for them, and re-layouts: 19.4 us -> none  [the longest x1 3.21 us: gradients(): jnp.einsum('bj,ijc->ibc', slope_table, last_value, precision=highest)]
    unnamed x1 -> x0, blocking collectives: 10.5 us -> none
    all_gather x1 -> x0, blocking collectives: 9.12 us -> none  [spread(): lax.all_gather(own, axis, axis=0, tiled=True)[:len(lines)]]
    transpose x4 -> x0, local copies, waits for them, and re-layouts: 5.18 us -> none  [the longest x1 2.83 us: gradients(): jnp.einsum('bj,ijc->ibc', value_table, last_slope, precision=highest)]
    unnamed x1 -> x0, starting transfers between devices: 2.77 us -> none
  transfers between devices with their start and end apart: 4 -> 2, of which waited for: 1 -> 1; matrix products, arithmetic and copies ran while one was open for 57% -> 9% of each run, Pallas kernels for 0% -> 24%
where the time goes in v1:
time: 105 us
  waiting for transfers between devices  33.6 us (32%)
  Pallas kernels  25.6 us (24%)
  between operations  14.4 us (14%)
  starting transfers between devices  13.2 us (13%)
  local copies, waits for them, and re-layouts  11.9 us (11%)
  matrix products  3.99 us (4%)
  other arithmetic  2.38 us (2%)
    all_gather x1, waiting for transfers between devices, per_device(): all_blocks = lax.all_gather(correction, 'patch', axis=0, tiled=True)  33.6 us
    pallas_call x1, Pallas kernels, volume_residual(): pl.pallas_call(volume_kernel, name='volume', out_shape=jax.ShapeDtypeStru...  25.6 us
    all_to_all x1, starting transfers between devices, from_everyone(): lax.all_to_all(jnp.broadcast_to(value[None], (peers, *value.shape)), axis...  13.1 us
  transfers between devices with their start and end apart: 2, of which 1 were waited for; matrix products, arithmetic and copies ran while one was open for 9% of the time, Pallas kernels for 24%

profile of v1, /device:TPU:1, one launch (start us, length us, event | category | flops | bytes accessed | tf_op | source)
XLA Modules:
  0.0 105.0 jit_solution(2385315004716129705)
XLA Ops:
  7.2 0.0 copy-start
  7.2 0.0 all-gather.2.cloned.1.call-start
  7.2 0.8 constant_dynamic-slice_fusion.2
  8.0 0.1 fusion.19
  8.1 0.1 fusion.20
  8.1 1.2 %fusion.28 = (f32[4,2,1,27,27]{4,2,3,1,0:T(1,128)S(1)}, f32[4,2,1,27,27]{4,2,3,1,0:T(1,128)S(1)}) fusion(f32[4,2,2,27,27]{4,2,3,1,0:T(2,128)} %param.26), kind=kLoop, calls=%fused_computation.61 | loop fusion | bytes 93312 | tf_op jit(solution)/shard_map/slice | solution.py:425
  9.4 0.7 reduce.9
  10.1 0.1 reshape.384
  10.2 0.3 bitcast_multiply_fusion
  10.5 0.4 convolution_bitcast_fusion.1
  10.9 0.9 convolution_multiply_fusion
  11.8 0.7 reshape.362
  12.6 0.0 all-gather.2.cloned.1.call-update
  12.6 0.0 copy-done
  12.6 0.2 reduce.15
  12.8 0.0 copy-start.1
  12.8 0.5 reshape_squeeze.8
  13.3 0.1 stack.11
  13.4 0.1 stack.12
  13.5 0.1 slice_reduce_fusion.1
  13.6 0.1 stack.13
  13.7 0.1 stack.14
  13.8 1.0 broadcast_in_dim.34
  14.8 13.1 %all-to-all-start = ((f32[64,1,4,1,729]{4,2,3,1,0:T(4,128)}), f32[64,1,4,1,729]{4,2,3,1,0:T(4,128)S(1)}, u32[]{:S(2)}, u32[]{:S(2)}) async-start(f32[64,1,4,1,729]{4,2,3,1,0:T(4,128)} %broadcast_in_dim.34), calls=%async_computation | async-start | bytes 1572864 | tf_op jit(solution)/shard_map/all_to_all | solution.py:44
  28.0 0.0 copy-done.1
  28.0 0.1 copy.37
  28.1 0.1 reshape.370
  28.2 0.1 eq.28
  28.4 0.6 copy.70
  29.0 0.1 copy.44
  29.2 0.1 reshape.369
  29.3 0.5 broadcast.199
  29.8 0.7 fusion.25
  30.4 0.1 add.80
  30.5 0.1 gt.16
  30.7 0.1 copy.46
  30.8 0.2 convert_reduce_fusion
  31.0 0.1 reshape.371
  31.1 0.2 copy.36
  31.3 0.2 and.40
  31.4 25.6 %volume.1 = f32[27,729]{1,0:T(8,128)} custom-call(f32[27,729]{1,0:T(8,128)} %bitcast.43, f32[96,9216]{1,0:T(8,128)} %bitcast.46, f32[96,9216]{1,0:T(8,128)} %bitcast.47, bf16[4,48,48]{2,1,0:T(8,128)(2,1)} %constant.160.clone.first_ref, bf16[4,16,144]{2,1,0:T(8,128)(2,1)} %constant.161.clone.last_ref, bf16[4,256,256]{2,1,0:T(8,128)(2,1)} %constant.162.clone.inner_ref, ...), custom_call_target="tpu_custom_call" | custom-call | flops 10000000000 | bytes 4000000 | tf_op jit(solution)/shard_map/volume/pallas_call | solution.py:366
  57.0 1.3 %reshape.360 = f32[1,27,27,27]{3,2,1,0:T(8,128)S(1)} reshape(f32[27,729]{1,0:T(8,128)} %volume.1) | data formatting | bytes 157464 | tf_op jit(solution)/shard_map/reshape | solution.py:444
  58.4 0.0 all-to-all-done
  58.4 0.3 reshape.372
  58.7 0.6 gather_fusion
  59.3 0.1 gather.7
  59.4 0.3 fusion.3
  59.7 0.3 convolution_bitcast_fusion
  60.1 0.7 sub.17
  60.8 33.6 %all-gather.2.cloned.1.call-done = f32[512,1,729]{2,0,1:T(8,128)} async-done(((f32[8,1,729]{2,0,1:T(8,128)}), f32[512,1,729]{2,0,1:T(8,128)}) %all-gather.2.cloned.1.call-update) | async-done | bytes 1493008 | tf_op jit(solution)/shard_map/all_gather | solution.py:437
  94.4 2.0 %fusion = f32[4,729]{1,0:T(4,128)S(1)} fusion(f32[512,1,729]{2,0,1:T(8,128)} %all-gather.2.cloned.1.call-done, s32[512]{0:T(512)S(1)} %eq.28, pred[512]{0:T(512)(128)(4,1)S(1)} %and.40), kind=kOutput, calls=%fused_computation.1 | convolution fusion | flops 17920000 | bytes 1507216 | tf_op jit(solution)/shard_map/ft,tvx->fvx/dot_general | solution.py:442
  96.5 0.1 reshape.364
  96.5 0.1 reshape.365
  96.6 0.1 reshape.386
  96.8 0.1 scatter-add.16
  96.9 0.1 reshape.387
  97.1 0.1 scatter-add.19
  97.2 1.0 reshape.368
  (18 shorter events, 0.2 us)
Async XLA Ops:
  7.2 5.4 %copy-start = (f32[1,1,1,27,729]{4,2,3,1,0:T(1,128)S(1)}, f32[1,1,1,27,729]{4,2,3,1,0:T(1,128)}, u32[]{:S(2)}) copy-start(f32[1,1,1,27,729]{4,2,3,1,0:T(1,128)} %param.22) | copy-start | bytes 236200
  7.2 87.2 %all-gather.2.cloned.1.call-start = ((), (), s32[]{:S(2)}) async-start(), calls=%async_computation.1 | async-start | bytes 1597440 | tf_op jit(solution)/shard_map/all_gather | solution.py:437
  12.8 15.2 %copy-start.1 = (s32[256,6]{0,1:T(8,128)S(1)}, s32[256,6]{0,1:T(8,128)}, u32[]{:S(2)}) copy-start(s32[256,6]{0,1:T(8,128)} %param.27) | copy-start | bytes 18436
  14.8 43.6 %all-to-all-start = ((f32[64,1,4,1,729]{4,2,3,1,0:T(4,128)}), f32[64,1,4,1,729]{4,2,3,1,0:T(4,128)S(1)}, u32[]{:S(2)}, u32[]{:S(2)}) async-start(f32[64,1,4,1,729]{4,2,3,1,0:T(4,128)} %broadcast_in_dim.34), calls=%async_computation | async-start | bytes 1572864 | tf_op jit(solution)/shard_map/all_to_all | solution.py:44
Sparse Core Ops, SparseCore 0:
  12.7 81.6 all-gather.1

commit v2 on v1

--- a/solution.py
+++ b/solution.py
@@ -31,23 +31,6 @@
     0.6521451548625461,
     0.3478548451374538,
 ]
-
-
-def in_order(tiles, dim):
-    dims = list(tiles.shape[1:])
-    dims[dim] *= tiles.shape[0]
-    return jnp.moveaxis(tiles, 0, dim).reshape(dims)
-
-
-def from_everyone(value, axis):
-    peers = lax.axis_size(axis)
-    return lax.all_to_all(
-        jnp.broadcast_to(value[None], (peers, *value.shape)), axis, 0, 0, tiled=True
-    )
-
-
-def gathered_copies(value, axis, dim):
-    return in_order(from_everyone(value, axis), dim)
 
 
 def spline_tables(elements, degree):
@@ -178,13 +161,94 @@
     return lax.broadcasted_iota(jnp.int32, (rows, 128), 1)
 
 
-def volume_kernel(x_ref, stiff_hbm, volume_hbm, first_ref, last_ref, inner_ref, plain_ref, adj_value_ref,
-                  adj_slope_ref, middle_ref, out_ref, stiff, volume, sent, got, back, home, outer, total,
-                  load_sem, send_sem, recv_sem, back_send_sem, back_recv_sem):
+def exact(left, right, dims):
+    return lax.dot_general(left, right, (dims, ((), ())), precision=highest, preferred_element_type=jnp.float32)
+
+
+def to_matrices(tiles, grid):
+    for i in range(BASIS):
+        tile, shift = divmod(BASIS * i, 128)
+        piece = tiles[tile]
+        if shift + BASIS > 128:
+            piece = jnp.where(lanes_of(piece.shape[0]) >= shift, piece, tiles[tile + 1])
+        grid[8 * i:8 * i + piece.shape[0], :] = pltpu.roll(piece, 128 - shift, 1) if shift else piece
+
+
+def to_rows(row_of, count):
+    lane = lanes_of(count)
+    tiles = [jnp.zeros((count, 128), jnp.float32) for _ in range(6)]
+    for i in range(BASIS):
+        tile, shift = divmod(BASIS * i, 128)
+        piece = row_of(i)
+        piece = pltpu.roll(piece, shift, 1) if shift else piece
+        end = shift + BASIS
+        tiles[tile] = jnp.where((lane >= shift) & (lane < end), piece, tiles[tile])
+        if end > 128:
+            tiles[tile + 1] = jnp.where(lane < end - 128, piece, tiles[tile + 1])
+    return tiles
+
+
+def routing(links_ref, y, z, core):
+    low_half = lanes_of(32) < 64
+    table = jnp.concatenate(
+        [links_ref[pl.ds(pl.multiple_of(64 * row + 8 * z, 8), 8), :] for row in range(4)], axis=0
+    ).astype(jnp.float32)
+    live = table[:, 4:5] > 0.0
+    sides = []
+    for s in range(2):
+        patch = jnp.where(live, table[:, s:s + 1], -1.0)
+        sides.append(jnp.where(low_half, patch, table[:, 2 + s:3 + s]))
+    natural = jnp.concatenate(sides, axis=0).astype(jnp.bfloat16)
+    row = lax.broadcasted_iota(jnp.int32, (128, 64), 0)
+    col = lax.broadcasted_iota(jnp.int32, (128, 64), 1)
+    source = ((row // 4) % 2) * 32 + (row // 16) * 4 + row % 4
+    order = jnp.where(col == source, 1.0, 0.0).astype(jnp.bfloat16)
+    keys = product(order, natural)
+    faces = pltpu.roll(keys, 64, 1)
+    lane = lanes_of(128)
+    row = lax.broadcasted_iota(jnp.int32, (128, 128), 0)
+    wanted = (16 * y + 2 * (lane // 8) + core).astype(jnp.float32)
+    same = (keys == wanted) & (faces == (lane % 4).astype(jnp.float32))
+    same = same & ((lane // 4) % 2 == (row // 8) % 2) & (lane < 64)
+    return jnp.where(same, 1.0, 0.0)
+
+
+def operator_kernel(x_ref, stiff_hbm, volume_hbm, lagrange_ref, mortar_ref, links_ref, counts_ref, first_ref,
+                    last_ref, inner_ref, plain_ref, adj_value_ref, adj_slope_ref, middle_ref, out_ref,
+                    jump_ref, stiff, volume, sent, got, back, home, outer, total, grid, trace_own, trace_all,
+                    trace_out, trace_in, fix_own, fix_all, fix_out, fix_in, load_sem, send_sem, recv_sem,
+                    back_send_sem, back_recv_sem, face_send_sem, face_recv_sem):
     me = lax.axis_index("sub")
+    patch = lax.axis_index("patch")
+    y, z, core = patch // 16, (patch // 2) % 8, patch % 2
+    group = 2 * y + core
+    line = [lax.rem(z + d, 8) for d in range(8)]
+    line_from = [lax.rem(z + 8 - d, 8) for d in range(8)]
+    plane = [lax.rem(group + d, 8) for d in range(8)]
+    plane_from = [lax.rem(group + 8 - d, 8) for d in range(8)]
+    line_ids = [{"patch": 16 * y + 2 * at + core} for at in line]
+    plane_ids = [{"patch": 16 * (at // 2) + 2 * z + at % 2} for at in plane]
+
+    def exchange(n, source, target, slot, slots_from, ids):
+        def one(d, at):
+            return pltpu.make_async_remote_copy(
+                src_ref=source(d), dst_ref=target.at[at], send_sem=face_send_sem.at[n, d],
+                recv_sem=face_recv_sem.at[n, d], device_id=ids[d], device_id_type=MESH)
+
+        def start():
+            for d in range(1, 8):
+                one(d, slot).start()
+
+        def finish():
+            for d in range(1, 8):
+                one(d, slot).wait_send()
+                one(d, slots_from[d]).wait_recv()
+
+        return start, finish
+
     rows = pl.ds(pl.multiple_of(me * SLAB, 8), SLAB)
-    load_stiff = pltpu.make_async_copy(stiff_hbm.at[rows], stiff, load_sem.at[0])
-    load_volume = pltpu.make_async_copy(volume_hbm.at[rows], volume, load_sem.at[1])
+    load_stiff = pltpu.make_async_copy(stiff_hbm.at[0, rows], stiff, load_sem.at[0])
+    load_volume = pltpu.make_async_copy(volume_hbm.at[0, rows], volume, load_sem.at[1])
     load_stiff.start()
     load_volume.start()
     peers = [lax.rem(me + d, SUBS) for d in range(SUBS)]
@@ -192,10 +256,30 @@
     barrier = pltpu.get_barrier_semaphore()
     for d in range(1, SUBS):
         pl.semaphore_signal(barrier, inc=1, device_id={"sub": peers[d]}, device_id_type=MESH)
+    for d in range(1, 8):
+        for ids in (line_ids, plane_ids):
+            pl.semaphore_signal(barrier, inc=1, device_id=ids[d], device_id_type=MESH)
     sent[...] = jnp.zeros_like(sent)
     for q in range(SUBS):
-        sent[q, 0:LAYERS, 0:729] = x_ref[6 * q:6 * q + LAYERS, :]
-    pl.semaphore_wait(barrier, SUBS - 1)
+        sent[q, 0:LAYERS, 0:729] = x_ref[0, 0, 0, 6 * q:6 * q + LAYERS, :]
+    trace_rows = [[x_ref[0, 0, 0, 26 * s:26 * s + 1, 128 * n:min(128 * n + 128, 729)] for n in range(6)] for s in range(2)]
+    for s in range(2):
+        tail = jnp.zeros((1, 768 - 729), jnp.float32)
+        trace_rows[s][5] = jnp.concatenate([trace_rows[s][5], tail], axis=1)
+    edge = x_ref[0, 0, 0, :, 0:128]
+    trace_rows.append(to_rows(lambda i: edge[i:i + 1, :], 1))
+    edge = jnp.concatenate([x_ref[0, 0, 0, :, 640:729], jnp.zeros((BASIS, 39), jnp.float32)], axis=1)
+    edge = pltpu.roll(edge, 128 - 62, 1)
+    trace_rows.append(to_rows(lambda i: edge[i:i + 1, :], 1))
+    for h in range(2):
+        for f in range(4):
+            for n in range(3):
+                trace_own[4 * h + f:4 * h + f + 1, 128 * n:128 * n + 128] = trace_rows[f][3 * h + n]
+    start_traces, finish_traces = exchange(0, lambda d: trace_own, trace_all, z, line_from, line_ids)
+    start_picked, finish_picked = exchange(1, lambda d: trace_out.at[plane[d]], trace_in, group, plane_from, plane_ids)
+    start_fixes, finish_fixes = exchange(2, lambda d: fix_own, fix_all, group, plane_from, plane_ids)
+    start_sums, finish_sums = exchange(3, lambda d: fix_out.at[line[d]], fix_in, z, line_from, line_ids)
+    pl.semaphore_wait(barrier, SUBS - 1 + 14)
     going = [None]
     for d in range(1, SUBS):
         copy = pltpu.make_async_remote_copy(
@@ -203,7 +287,33 @@
             device_id={"sub": peers[d]}, device_id_type=MESH)
         copy.start()
         going.append(copy)
+    start_traces()
+    trace_all[z] = trace_own[...]
     got[me] = sent[me]
+    row = lax.broadcasted_iota(jnp.int32, (BASIS, BASIS), 0)
+    lefts, rights = [], []
+    for s in range(2):
+        for slot in range(4):
+            at = 4 * patch + slot
+            lefts.append(jnp.where(row < counts_ref[at, 4], mortar_ref[slot, s, 0], 0.0))
+            rights.append(jnp.where(row < counts_ref[at, 5], mortar_ref[slot, s, 1], 0.0))
+    multipliers = jnp.concatenate([lagrange_ref[slot, 0] for slot in range(4)], axis=0)
+    multipliers = jnp.concatenate([multipliers, jnp.zeros((4, 768 - 729), jnp.float32)], axis=1)
+    to_matrices([multipliers[:, 128 * n:128 * n + 128] for n in range(6)], grid)
+    given = [grid[pl.ds(slot, BASIS, stride=8), :][:, 0:BASIS] for slot in range(4)]
+    for k in range(8):
+        fix = exact(given[k % 4], rights[k], ((1,), (0,)))
+        fix = exact(lefts[k], fix, ((0,), (0,)))
+        fix = fix if k < 4 else -fix
+        grid[pl.ds(k, BASIS, stride=8), :] = jnp.concatenate(
+            [fix, jnp.zeros((BASIS, 128 - BASIS), jnp.float32)], axis=1)
+    fix_rows = to_rows(lambda i: grid[8 * i:8 * i + 8, :], 8)
+    for h in range(2):
+        for n in range(3):
+            fix_own[8 * h:8 * h + 8, 128 * n:128 * n + 128] = fix_rows[3 * h + n]
+    start_fixes()
+    fix_all[group] = fix_own[...]
+    route = routing(links_ref, y, z, core)
     total[...] = jnp.zeros_like(total)
     for d in range(1, SUBS):
         going[d].wait_send()
@@ -315,7 +425,21 @@
             total[2 * t + m] += jnp.concatenate(sums[m], axis=0)
         return carry
 
-    lax.fori_loop(0, STEPS, step, 0)
+    lax.fori_loop(0, STEPS // 2, step, 0)
+    finish_traces()
+    high, low = split(trace_all[...].reshape(64, 384))
+    both = (route + pltpu.roll(route, 64, 1)).astype(jnp.bfloat16)
+    trace_out[...] = product(both, jnp.concatenate([high, low], axis=0)).reshape(8, 16, 384)
+    start_picked()
+    trace_in[group] = trace_out[group]
+    finish_fixes()
+    high, low = split(fix_all[...].reshape(128, 384))
+    flipped = route.T.astype(jnp.bfloat16)[0:64]
+    fix_out[...] = product(jnp.concatenate([flipped, flipped], axis=1),
+                           jnp.concatenate([high, low], axis=0)).reshape(8, 8, 384)
+    start_sums()
+    fix_in[z] = fix_out[z]
+    lax.fori_loop(STEPS // 2, STEPS, step, 0)
 
     last = last_ref[me]
     lane = lanes_of(16)
@@ -348,27 +472,57 @@
         copy.start()
         going.append(copy)
     home[me] = back[me]
+    finish_picked()
+    picked = trace_in[0]
+    for at in range(1, 8):
+        picked = picked + trace_in[at]
+    to_matrices([picked[8 * h:8 * h + 8, 128 * n:128 * n + 128] for h in range(2) for n in range(3)], grid)
+    jumps = []
+    for k in range(8):
+        jump = exact(grid[pl.ds(k, BASIS, stride=8), :][:, 0:BASIS], rights[k], ((1,), (1,)))
+        jumps.append(exact(lefts[k], jump, ((1,), (0,))))
+    for slot in range(4):
+        grid[pl.ds(slot, BASIS, stride=8), :] = jnp.concatenate(
+            [jumps[slot] - jumps[4 + slot], jnp.zeros((BASIS, 128 - BASIS), jnp.float32)], axis=1)
+    jump_rows = jnp.concatenate(to_rows(lambda i: grid[8 * i:8 * i + 8, :], 8), axis=1)
+    for slot in range(4):
+        jump_ref[slot, 0] = jump_rows[slot:slot + 1, 0:729]
+    finish_sums()
+    sums = fix_in[0]
+    for at in range(1, 8):
+        sums = sums + fix_in[at]
+    sums = [sums[4 * h:4 * h + 4, 128 * n:128 * n + 128] for h in range(2) for n in range(3)]
+    to_matrices(sums, grid)
+    lane = lanes_of(BASIS)
+    inside = lane < BASIS
+    near = jnp.where(inside, grid[pl.ds(2, BASIS, stride=8), :], 0.0)
+    far = jnp.where(inside, grid[pl.ds(3, BASIS, stride=8), :], 0.0)
+    far = pltpu.roll(far, 62, 1)
+    ends = jnp.concatenate(sums, axis=1)
     for d in range(1, SUBS):
         going[d].wait_send()
         pltpu.make_async_remote_copy(
             src_ref=back.at[peers[d]], dst_ref=home.at[origins[d]], send_sem=back_send_sem.at[d],
             recv_sem=back_recv_sem.at[d], device_id={"sub": peers[d]}, device_id_type=MESH).wait_recv()
-    out_ref[...] = jnp.zeros_like(out_ref)
+    out_ref[0, 0, 0] = jnp.zeros((BASIS, BASIS * BASIS), jnp.float32)
     for q in range(SUBS):
-        out_ref[6 * q:6 * q + LAYERS, :] += home[q, 0:LAYERS, 0:729]
-
-
-def volume_residual(coefficients, stiffness, volume):
-    constants = constant_tables()
+        out_ref[0, 0, 0, 6 * q:6 * q + LAYERS, :] += home[q, 0:LAYERS, 0:729]
+    for s in range(2):
+        out_ref[0, 0, 0, 26 * s:26 * s + 1, :] += ends[s:s + 1, 0:729]
+    out_ref[0, 0, 0, :, 0:128] += near
+    out_ref[0, 0, 0, :, 640:729] += far[:, 0:89]
+
+
+def per_device(state, stiff_weight, volume_weight, lagrange, mortar, links):
     vmem = pl.BlockSpec(memory_space=pltpu.VMEM)
     anywhere = pl.BlockSpec(memory_space=pl.ANY)
     smem = pl.BlockSpec(memory_space=pltpu.SMEM)
     return pl.pallas_call(
-        volume_kernel,
-        name="volume",
-        out_shape=jax.ShapeDtypeStruct((BASIS, BASIS * BASIS), jnp.float32),
-        in_specs=[vmem, anywhere, anywhere] + [vmem] * 6 + [smem],
-        out_specs=vmem,
+        operator_kernel,
+        name="operator",
+        out_shape=(jax.ShapeDtypeStruct(state.shape, jnp.float32), jax.ShapeDtypeStruct(lagrange.shape, jnp.float32)),
+        in_specs=[vmem, anywhere, anywhere, vmem, vmem, vmem, smem] + [vmem] * 6 + [smem],
+        out_specs=(vmem, vmem),
         scratch_shapes=[
             pltpu.VMEM((SLAB, QUAD * QUAD), jnp.float32),
             pltpu.VMEM((SLAB, QUAD * QUAD), jnp.float32),
@@ -378,75 +532,26 @@
             pltpu.VMEM((SUBS, 16, 768), jnp.float32),
             pltpu.VMEM((BASIS, 2 * SLAB, 128), jnp.float32),
             pltpu.VMEM((BASIS, 2 * SLAB, 128), jnp.float32),
+            pltpu.VMEM((BASIS * 8, 128), jnp.float32),
+            pltpu.VMEM((8, 384), jnp.float32),
+            pltpu.VMEM((8, 8, 384), jnp.float32),
+            pltpu.VMEM((8, 16, 384), jnp.float32),
+            pltpu.VMEM((8, 16, 384), jnp.float32),
+            pltpu.VMEM((16, 384), jnp.float32),
+            pltpu.VMEM((8, 16, 384), jnp.float32),
+            pltpu.VMEM((8, 8, 384), jnp.float32),
+            pltpu.VMEM((8, 8, 384), jnp.float32),
             pltpu.SemaphoreType.DMA((2,)),
             pltpu.SemaphoreType.DMA((SUBS,)),
             pltpu.SemaphoreType.DMA((SUBS,)),
             pltpu.SemaphoreType.DMA((SUBS,)),
             pltpu.SemaphoreType.DMA((SUBS,)),
+            pltpu.SemaphoreType.DMA((4, 8)),
+            pltpu.SemaphoreType.DMA((4, 8)),
         ],
         compiler_params=pltpu.CompilerParams(collective_id=0, has_side_effects=True),
         cost_estimate=pl.CostEstimate(flops=10**10, bytes_accessed=4 * 10**6, transcendentals=0),
-    )(coefficients, stiffness, volume, *constants)
-
-
-def per_device(state, stiff_weight, volume_weight, lagrange, mortar, links):
-    patches = lax.axis_size("patch")
-    device = lax.axis_index("patch")
-    vectors = state.shape[2]
-    size_n = state.shape[3]
-    slot_count = mortar.shape[0]
-    coefficients = state[0, 0]
-    stiffness = stiff_weight[0]
-    volume = volume_weight[0]
-    residual = volume_residual(coefficients.reshape(size_n, size_n * size_n), stiffness, volume)
-    field_cube = coefficients.reshape(vectors, size_n, size_n, size_n)
-    faces = jnp.stack(
-        [field_cube[:, 0], field_cube[:, -1], field_cube[:, :, 0], field_cube[:, :, -1]]
-    )
-    faces = faces.reshape(4, vectors, size_n * size_n)
-    item_count = 2 * slot_count
-    item_patch = links[:, 0:2].reshape(patches, item_count)
-    item_face = links[:, 2:4].reshape(patches, item_count)
-    is_live = jnp.repeat(links[:, 4] > 0, 2).reshape(patches, item_count)
-    own_patch = lax.dynamic_index_in_dim(item_patch, device, 0, keepdims=False)
-    own_face = lax.dynamic_index_in_dim(item_face, device, 0, keepdims=False)
-    own_live = lax.dynamic_index_in_dim(is_live, device, 0, keepdims=False)
-    own_rows = lax.dynamic_slice_in_dim(links, device * slot_count, slot_count, 0)
-    face_grid = jnp.arange(4)
-    gathered = gathered_copies(faces[None], "patch", 0)
-    picked = jnp.take(
-        gathered.reshape(patches * 4, vectors, size_n * size_n), own_patch * 4 + own_face, axis=0
-    )
-    picked = picked * own_live.astype(jnp.float32)[:, None, None]
-    rank_grid = jnp.arange(size_n)
-    row_mask = (rank_grid[None, :] < own_rows[:, 4:5]).astype(jnp.float32)
-    col_mask = (rank_grid[None, :] < own_rows[:, 5:6]).astype(jnp.float32)
-    left = mortar[:, :, 0] * row_mask[:, None, :, None]
-    right = mortar[:, :, 1] * col_mask[:, None, :, None]
-    traces_here = picked.reshape(slot_count, 2, vectors, size_n, size_n)
-    projected = jnp.einsum("sgai,sgvij,sgbj->sgvab", left, traces_here, right, precision=highest)
-    constraint = (projected[:, 0] - projected[:, 1]).reshape(
-        slot_count, 1, vectors, size_n * size_n
-    )
-    multipliers = lagrange[:, 0].reshape(slot_count, vectors, size_n, size_n)
-    signs = jnp.array([1.0, -1.0], jnp.float32)
-    correction = jnp.einsum("sgai,svab,sgbj->sgvij", left, multipliers, right, precision=highest)
-    correction = (correction * signs[None, :, None, None, None]).reshape(
-        item_count, vectors, size_n * size_n
-    )
-    all_blocks = lax.all_gather(correction, "patch", axis=0, tiled=True)
-    face_match = (
-        (is_live & (item_patch == device)).reshape(-1)[None, :]
-        & (item_face.reshape(-1)[None, :] == face_grid[:, None])
-    ).astype(jnp.float32)
-    face_total = jnp.einsum("ft,tvx->fvx", face_match, all_blocks, precision=highest)
-    pieces = face_total.reshape(4, vectors, size_n, size_n)
-    result_cube = residual.reshape(vectors, size_n, size_n, size_n)
-    result_cube = result_cube.at[:, 0].add(pieces[0])
-    result_cube = result_cube.at[:, -1].add(pieces[1])
-    result_cube = result_cube.at[:, :, 0].add(pieces[2])
-    result_cube = result_cube.at[:, :, -1].add(pieces[3])
-    return (result_cube.reshape(1, 1, vectors, size_n, size_n * size_n), constraint)
+    )(state, stiff_weight, volume_weight, lagrange, mortar, links, links, *constant_tables())
 
 
 def solution(mesh):

time: 105 us -> 42.8 us (0.41)
  the two profiles are of different devices: /device:TPU:1 before, /device:TPU:8 now
where the time goes in v2:
time: 42.8 us; the launch traced here: 42.5 us
  Pallas kernels  34.3 us (80%)
  local copies, waits for them, and re-layouts  7.61 us (18%)
  between operations  0.64 us (1%)
    pallas_call x1, Pallas kernels, per_device(): pl.pallas_call(operator_kernel, name='operator', out_shape=(jax.ShapeDtyp...  34.3 us
    unnamed x4, local copies, waits for them, and re-layouts  5.99 us
    pallas_call x1, local copies, waits for them, and re-layouts, per_device(): pl.pallas_call(operator_kernel, name='operator', out_shape=(jax.ShapeDtyp...  1.61 us

profile of v2, /device:TPU:8, one launch (start us, length us, event | category | flops | bytes accessed | tf_op | source)
XLA Modules:
  0.0 42.5 jit_solution(12788428821473048187)
XLA Ops:
  0.6 1.5 %copy.15.x_ref = f32[1,1,1,27,729]{4,3,2,1,0:T(8,128)} copy(f32[1,1,1,27,729]{4,2,3,1,0:T(1,128)} %param.13) | data formatting | bytes 157464 | tf_op args[0]
  2.2 1.5 %copy.17.links_ref.counts_ref = s32[256,6]{1,0:T(8,128)} copy(s32[256,6]{0,1:T(8,128)} %param.18) | data formatting | bytes 12288 | tf_op args[5]
  3.7 1.7 %copy.16.mortar_ref = f32[4,2,2,27,27]{4,3,2,1,0:T(8,128)} copy(f32[4,2,2,27,27]{4,2,3,1,0:T(2,128)} %param.17) | data formatting | bytes 93312 | tf_op args[4]
  5.3 34.3 %operator.1 = (f32[1,1,1,27,729]{4,3,2,1,0:T(8,128)}, f32[4,1,1,729]{3,2,1,0:T(1,128)}) custom-call(f32[1,1,1,27,729]{4,3,2,1,0:T(8,128)} %copy.15.x_ref, f32[1,96,9216]{2,1,0:T(8,128)} %stiff_hbm.1, f32[1,96,9216]{2,1,0:T(8,128)} %volume_hbm.1, f32[4,1,1,729]{3,2,1,0:T(1,128)} %lagrange_ref.1, f32[4,2,2,27,27]{4,3,2,1,0:T(8,128)} %copy.16.mortar_ref, ...), custom_call_target="tpu_custom_call" | custom-call | flops 10000000000 | bytes 4000000 | tf_op jit(solution)/shard_map/operator/pallas_call | solution.py:520
  39.6 1.6 %copy.19 = f32[1,1,1,27,729]{4,2,3,1,0:T(1,128)} copy(f32[1,1,1,27,729]{4,3,2,1,0:T(8,128)} %get-tuple-element.2) | data formatting | bytes 157464 | tf_op jit(solution)/shard_map/operator/pallas_call | solution.py:520
  41.2 1.3 %copy.21 = f32[4,1,1,729]{3,2,1,0:T(1,128)} copy(f32[4,1,1,729]{3,2,1,0:T(1,128)} %get-tuple-element.7) | data formatting | bytes 23328

commit v3 on v2

--- a/solution.py
+++ b/solution.py
@@ -188,34 +188,36 @@
     return tiles
 
 
+def ninth_layer(ref, at):
+    first = lax.broadcasted_iota(jnp.int32, (8, 768), 0) == 0
+    line = jnp.concatenate([ref[at, n:n + 1, 768:896] for n in range(6)], axis=1)
+    return jnp.where(first, line, 0.0)
+
+
 def routing(links_ref, y, z, core):
-    low_half = lanes_of(32) < 64
-    table = jnp.concatenate(
-        [links_ref[pl.ds(pl.multiple_of(64 * row + 8 * z, 8), 8), :] for row in range(4)], axis=0
-    ).astype(jnp.float32)
-    live = table[:, 4:5] > 0.0
-    sides = []
-    for s in range(2):
-        patch = jnp.where(live, table[:, s:s + 1], -1.0)
-        sides.append(jnp.where(low_half, patch, table[:, 2 + s:3 + s]))
-    natural = jnp.concatenate(sides, axis=0).astype(jnp.bfloat16)
-    row = lax.broadcasted_iota(jnp.int32, (128, 64), 0)
-    col = lax.broadcasted_iota(jnp.int32, (128, 64), 1)
-    source = ((row // 4) % 2) * 32 + (row // 16) * 4 + row % 4
+    row = lax.broadcasted_iota(jnp.int32, (128, 256), 0)
+    col = lax.broadcasted_iota(jnp.int32, (128, 256), 1)
+    source = ((row // 32) * 16 + 2 * z + (row // 16) % 2) * 4 + row % 4
     order = jnp.where(col == source, 1.0, 0.0).astype(jnp.bfloat16)
-    keys = product(order, natural)
-    faces = pltpu.roll(keys, 64, 1)
+    table = links_ref[...].astype(jnp.float32).astype(jnp.bfloat16)
+    found = lax.dot_general(order, table, (((1,), (1,)), ((), ())), preferred_element_type=jnp.float32)
+    row = lax.broadcasted_iota(jnp.int32, (128, 1), 0)
+    second = (row // 4) % 2 == 1
+    patch = jnp.where(second, found[:, 1:2], found[:, 0:1])
+    face = jnp.where(second, found[:, 3:4], found[:, 2:3])
+    patch = jnp.where(found[:, 4:5] > 0.0, patch, -1.0)
     lane = lanes_of(128)
     row = lax.broadcasted_iota(jnp.int32, (128, 128), 0)
     wanted = (16 * y + 2 * (lane // 8) + core).astype(jnp.float32)
-    same = (keys == wanted) & (faces == (lane % 4).astype(jnp.float32))
+    same = (patch == wanted) & (face == (lane % 4).astype(jnp.float32))
     same = same & ((lane // 4) % 2 == (row // 8) % 2) & (lane < 64)
     return jnp.where(same, 1.0, 0.0)
 
 
-def operator_kernel(x_ref, stiff_hbm, volume_hbm, lagrange_ref, mortar_ref, links_ref, counts_ref, first_ref,
-                    last_ref, inner_ref, plain_ref, adj_value_ref, adj_slope_ref, middle_ref, out_ref,
-                    jump_ref, stiff, volume, sent, got, back, home, outer, total, grid, trace_own, trace_all,
+def operator_kernel(x_hbm, stiff_hbm, volume_hbm, lagrange_hbm, mortar_hbm, links_hbm, first_hbm, last_hbm,
+                    inner_hbm, plain_hbm, adj_value_hbm, adj_slope_hbm, middle_hbm, out_ref, jump_ref,
+                    x_ref, lagrange_ref, mortar_ref, links_ref, counts_ref, first_ref, last_ref, inner_ref,
+                    plain_ref, adj_value_ref, adj_slope_ref, middle_ref, stiff, volume, sent, got, back, home, outer, total, grid, trace_own, trace_all,
                     trace_out, trace_in, fix_own, fix_all, fix_out, fix_in, load_sem, send_sem, recv_sem,
                     back_send_sem, back_recv_sem, face_send_sem, face_recv_sem):
     me = lax.axis_index("sub")
@@ -247,10 +249,30 @@
         return start, finish
 
     rows = pl.ds(pl.multiple_of(me * SLAB, 8), SLAB)
-    load_stiff = pltpu.make_async_copy(stiff_hbm.at[0, rows], stiff, load_sem.at[0])
-    load_volume = pltpu.make_async_copy(volume_hbm.at[0, rows], volume, load_sem.at[1])
-    load_stiff.start()
-    load_volume.start()
+    pairs = [(slot, s, n) for slot in range(4) for s in range(2) for n in range(2)]
+    loads = [
+        [(x_hbm.at[0, 0, :, 0, :], x_ref)],
+        [(links_hbm, links_ref)],
+        [(links_hbm, counts_ref)],
+        [(lagrange_hbm, lagrange_ref)],
+        [(mortar_hbm.at[slot, s, :, n, :], mortar_ref.at[slot, s, n]) for slot, s, n in pairs],
+        [(first_hbm.at[me], first_ref)],
+        [(middle_hbm, middle_ref)],
+        [(inner_hbm, inner_ref), (plain_hbm, plain_ref)],
+        [(stiff_hbm.at[0, rows], stiff), (volume_hbm.at[0, rows], volume)],
+        [(adj_value_hbm, adj_value_ref), (adj_slope_hbm, adj_slope_ref)],
+        [(last_hbm.at[me], last_ref)],
+    ]
+    loads = [[pltpu.make_async_copy(a, b, load_sem.at[n]) for a, b in some] for n, some in enumerate(loads)]
+    for some in loads:
+        for copy in some:
+            copy.start()
+
+    def loaded(*which):
+        for n in which:
+            for copy in loads[n]:
+                copy.wait()
+
     peers = [lax.rem(me + d, SUBS) for d in range(SUBS)]
     origins = [lax.rem(me + SUBS - d, SUBS) for d in range(SUBS)]
     barrier = pltpu.get_barrier_semaphore()
@@ -259,16 +281,20 @@
     for d in range(1, 8):
         for ids in (line_ids, plane_ids):
             pl.semaphore_signal(barrier, inc=1, device_id=ids[d], device_id_type=MESH)
+    loaded(0)
     sent[...] = jnp.zeros_like(sent)
     for q in range(SUBS):
-        sent[q, 0:LAYERS, 0:729] = x_ref[0, 0, 0, 6 * q:6 * q + LAYERS, :]
-    trace_rows = [[x_ref[0, 0, 0, 26 * s:26 * s + 1, 128 * n:min(128 * n + 128, 729)] for n in range(6)] for s in range(2)]
+        sent[q, :, 0:729] = x_ref[6 * q:6 * q + 8, :]
+        for n in range(6):
+            width = min(128, 729 - 128 * n)
+            sent[q, n:n + 1, 768:768 + width] = x_ref[6 * q + 8:6 * q + 9, 128 * n:128 * n + width]
+    trace_rows = [[x_ref[26 * s:26 * s + 1, 128 * n:min(128 * n + 128, 729)] for n in range(6)] for s in range(2)]
     for s in range(2):
         tail = jnp.zeros((1, 768 - 729), jnp.float32)
         trace_rows[s][5] = jnp.concatenate([trace_rows[s][5], tail], axis=1)
-    edge = x_ref[0, 0, 0, :, 0:128]
+    edge = x_ref[:, 0:128]
     trace_rows.append(to_rows(lambda i: edge[i:i + 1, :], 1))
-    edge = jnp.concatenate([x_ref[0, 0, 0, :, 640:729], jnp.zeros((BASIS, 39), jnp.float32)], axis=1)
+    edge = jnp.concatenate([x_ref[:, 640:729], jnp.zeros((BASIS, 39), jnp.float32)], axis=1)
     edge = pltpu.roll(edge, 128 - 62, 1)
     trace_rows.append(to_rows(lambda i: edge[i:i + 1, :], 1))
     for h in range(2):
@@ -290,13 +316,14 @@
     start_traces()
     trace_all[z] = trace_own[...]
     got[me] = sent[me]
+    loaded(1, 2, 3, 4)
     row = lax.broadcasted_iota(jnp.int32, (BASIS, BASIS), 0)
     lefts, rights = [], []
     for s in range(2):
         for slot in range(4):
             at = 4 * patch + slot
-            lefts.append(jnp.where(row < counts_ref[at, 4], mortar_ref[slot, s, 0], 0.0))
-            rights.append(jnp.where(row < counts_ref[at, 5], mortar_ref[slot, s, 1], 0.0))
+            lefts.append(jnp.where(row < counts_ref[4, at], mortar_ref[slot, s, 0], 0.0))
+            rights.append(jnp.where(row < counts_ref[5, at], mortar_ref[slot, s, 1], 0.0))
     multipliers = jnp.concatenate([lagrange_ref[slot, 0] for slot in range(4)], axis=0)
     multipliers = jnp.concatenate([multipliers, jnp.zeros((4, 768 - 729), jnp.float32)], axis=1)
     to_matrices([multipliers[:, 128 * n:128 * n + 128] for n in range(6)], grid)
@@ -321,10 +348,11 @@
             src_ref=sent.at[peers[d]], dst_ref=got.at[origins[d]], send_sem=send_sem.at[d],
             recv_sem=recv_sem.at[d], device_id={"sub": peers[d]}, device_id_type=MESH).wait_recv()
 
-    first = first_ref[me]
+    loaded(5)
+    first = first_ref[...]
     spread = []
     for f in range(FIELDS):
-        high, low = split(got[f])
+        high, low = split(jnp.concatenate([got[f, :, 0:768], ninth_layer(got, f)], axis=0))
         spread.append(product(first, jnp.concatenate([high, low, high], axis=0)))
     lane = lanes_of(2 * SLAB)
     for j in range(BASIS):
@@ -338,8 +366,7 @@
             piece = pltpu.roll(piece, turn, 1) if turn else piece
             merged = piece if f == 0 else jnp.where(lane >= 32 * f, piece, merged)
         outer[j] = merged
-    load_stiff.wait()
-    load_volume.wait()
+    loaded(6, 7, 8, 9, 10)
 
     def step(t, carry):
         def scalar(table, bb, m):
@@ -441,7 +468,7 @@
     fix_in[z] = fix_out[z]
     lax.fori_loop(STEPS // 2, STEPS, step, 0)
 
-    last = last_ref[me]
+    last = last_ref[...]
     lane = lanes_of(16)
     packed = [[jnp.zeros((16, 128), jnp.float32) for _ in range(6)] for _ in range(FIELDS)]
     for j0 in range(0, BASIS, 2):
@@ -463,7 +490,9 @@
                 if end > 128:
                     packed[f][tile + 1] = jnp.where(lane < end - 128, turned, packed[f][tile + 1])
     for f in range(FIELDS):
-        back[f] = jnp.concatenate(packed[f], axis=1)
+        for n in range(6):
+            back[f, :, 128 * n:128 * n + 128] = packed[f][n][0:8]
+            back[f, n:n + 1, 768:896] = packed[f][n][8:9]
     going = [None]
     for d in range(1, SUBS):
         copy = pltpu.make_async_remote_copy(
@@ -504,32 +533,43 @@
         pltpu.make_async_remote_copy(
             src_ref=back.at[peers[d]], dst_ref=home.at[origins[d]], send_sem=back_send_sem.at[d],
             recv_sem=back_recv_sem.at[d], device_id={"sub": peers[d]}, device_id_type=MESH).wait_recv()
-    out_ref[0, 0, 0] = jnp.zeros((BASIS, BASIS * BASIS), jnp.float32)
+    x_ref[...] = jnp.zeros((BASIS, BASIS * BASIS), jnp.float32)
     for q in range(SUBS):
-        out_ref[0, 0, 0, 6 * q:6 * q + LAYERS, :] += home[q, 0:LAYERS, 0:729]
+        x_ref[6 * q:6 * q + 8, :] += home[q, :, 0:729]
+        x_ref[6 * q + 8:6 * q + 9, :] += ninth_layer(home, q)[0:1, 0:729]
     for s in range(2):
-        out_ref[0, 0, 0, 26 * s:26 * s + 1, :] += ends[s:s + 1, 0:729]
-    out_ref[0, 0, 0, :, 0:128] += near
-    out_ref[0, 0, 0, :, 640:729] += far[:, 0:89]
+        x_ref[26 * s:26 * s + 1, :] += ends[s:s + 1, 0:729]
+    x_ref[:, 0:128] += near
+    x_ref[:, 640:729] += far[:, 0:89]
+    out_ref[0, 0, :, 0, :] = x_ref[...]
 
 
 def per_device(state, stiff_weight, volume_weight, lagrange, mortar, links):
     vmem = pl.BlockSpec(memory_space=pltpu.VMEM)
     anywhere = pl.BlockSpec(memory_space=pl.ANY)
-    smem = pl.BlockSpec(memory_space=pltpu.SMEM)
-    return pl.pallas_call(
+    constants = constant_tables()
+    local = [x.shape[1:] if n < 2 else x.shape for n, x in enumerate(constants)]
+    result, jumps = pl.pallas_call(
         operator_kernel,
         name="operator",
-        out_shape=(jax.ShapeDtypeStruct(state.shape, jnp.float32), jax.ShapeDtypeStruct(lagrange.shape, jnp.float32)),
-        in_specs=[vmem, anywhere, anywhere, vmem, vmem, vmem, smem] + [vmem] * 6 + [smem],
+        out_shape=(jax.ShapeDtypeStruct((1, 1, BASIS, 1, BASIS * BASIS), jnp.float32),
+                   jax.ShapeDtypeStruct(lagrange.shape, jnp.float32)),
+        in_specs=[anywhere] * 13,
         out_specs=(vmem, vmem),
         scratch_shapes=[
+            pltpu.VMEM((BASIS, BASIS * BASIS), jnp.float32),
+            pltpu.VMEM(lagrange.shape, jnp.float32),
+            pltpu.VMEM(mortar.shape, jnp.float32),
+            pltpu.VMEM((6, 256), jnp.int32),
+            pltpu.SMEM((6, 256), jnp.int32),
+            *[pltpu.VMEM(shape, jnp.bfloat16) for shape in local[:-1]],
+            pltpu.SMEM(local[-1], jnp.float32),
             pltpu.VMEM((SLAB, QUAD * QUAD), jnp.float32),
             pltpu.VMEM((SLAB, QUAD * QUAD), jnp.float32),
-            pltpu.VMEM((SUBS, 16, 768), jnp.float32),
-            pltpu.VMEM((SUBS, 16, 768), jnp.float32),
-            pltpu.VMEM((SUBS, 16, 768), jnp.float32),
-            pltpu.VMEM((SUBS, 16, 768), jnp.float32),
+            pltpu.VMEM((SUBS, 8, 896), jnp.float32),
+            pltpu.VMEM((SUBS, 8, 896), jnp.float32),
+            pltpu.VMEM((SUBS, 8, 896), jnp.float32),
+            pltpu.VMEM((SUBS, 8, 896), jnp.float32),
             pltpu.VMEM((BASIS, 2 * SLAB, 128), jnp.float32),
             pltpu.VMEM((BASIS, 2 * SLAB, 128), jnp.float32),
             pltpu.VMEM((BASIS * 8, 128), jnp.float32),
@@ -541,7 +581,7 @@
             pltpu.VMEM((8, 16, 384), jnp.float32),
             pltpu.VMEM((8, 8, 384), jnp.float32),
             pltpu.VMEM((8, 8, 384), jnp.float32),
-            pltpu.SemaphoreType.DMA((2,)),
+            pltpu.SemaphoreType.DMA((11,)),
             pltpu.SemaphoreType.DMA((SUBS,)),
             pltpu.SemaphoreType.DMA((SUBS,)),
             pltpu.SemaphoreType.DMA((SUBS,)),
@@ -551,7 +591,9 @@
         ],
         compiler_params=pltpu.CompilerParams(collective_id=0, has_side_effects=True),
         cost_estimate=pl.CostEstimate(flops=10**10, bytes_accessed=4 * 10**6, transcendentals=0),
-    )(state, stiff_weight, volume_weight, lagrange, mortar, links, links, *constant_tables())
+    )(jnp.transpose(state, (0, 1, 3, 2, 4)), stiff_weight, volume_weight, lagrange,
+      jnp.transpose(mortar, (0, 1, 3, 2, 4)), links.T, *constants)
+    return jnp.transpose(result, (0, 1, 3, 2, 4)), jumps
 
 
 def solution(mesh):

time: 42.8 us -> 34.3 us (0.80)
  the two profiles are of different devices: /device:TPU:8 before, /device:TPU:16 now
where the time goes in v3:
time: 34.3 us; the launch traced here: 34.1 us
  Pallas kernels  30.6 us (89%)
  local copies, waits for them, and re-layouts  2.85 us (8%)
  between operations  0.64 us (2%)
    pallas_call x1, Pallas kernels, per_device(): pl.pallas_call(operator_kernel, name='operator', out_shape=(jax.ShapeDtyp...  30.6 us
    unnamed x2, local copies, waits for them, and re-layouts  2.85 us

profile of v3, /device:TPU:16, one launch (start us, length us, event | category | flops | bytes accessed | tf_op | source)
XLA Modules:
  0.0 34.1 jit_solution(12542574308552254725)
XLA Ops:
  0.6 30.6 %operator.1 = (f32[1,1,27,1,729]{4,3,2,1,0:T(1,128)}, f32[4,1,1,729]{3,2,1,0:T(1,128)}) custom-call(f32[1,1,27,1,729]{4,3,2,1,0:T(1,128)} %bitcast.8, f32[1,96,9216]{2,1,0:T(8,128)} %stiff_hbm.1, f32[1,96,9216]{2,1,0:T(8,128)} %volume_hbm.1, f32[4,1,1,729]{3,2,1,0:T(1,128)} %lagrange_hbm.1, f32[4,2,27,2,27]{4,3,2,1,0:T(2,128)} %bitcast.7, s32[6,256]{1,0:T(8,128)} %bitcast.9, ...), custom_call_target="tpu_custom_call" | custom-call | flops 10000000000 | bytes 4000000 | tf_op jit(solution)/shard_map/operator/pallas_call | solution.py:552
  31.3 1.5 %copy.18 = f32[1,1,1,27,729]{4,2,3,1,0:T(1,128)} copy(f32[1,1,1,27,729]{4,2,3,1,0:T(1,128)} %bitcast.6) | data formatting | bytes 157464
  32.8 1.3 %copy.19 = f32[4,1,1,729]{3,2,1,0:T(1,128)} copy(f32[4,1,1,729]{3,2,1,0:T(1,128)} %get-tuple-element.11) | data formatting | bytes 23328

commit v4 on v3

--- a/solution.py
+++ b/solution.py
@@ -119,22 +119,26 @@
     inner = np.stack([value_even, value_odd, slope_even, slope_odd])
     plain = value_odd[:, 128:]
 
-    def adjoint_table(table):
+    def adjoint_table(table, spilled=None):
         high, low = halves(table)
-        out = np.zeros((512, 256), np.float32)
+        out = np.zeros((1024, 256), np.float32)
         for f in range(FIELDS):
             scale = -stabilize if f == FIELDS - 1 else 1.0
             rows = slice(128 * f, 128 * f + QUAD)
             out[rows, 32 * f:32 * f + BASIS] = scale * high
             out[rows, 128 + 32 * f:128 + 32 * f + BASIS] = scale * low
-        return out
-
-    high, low = halves(value_w)
-    div = np.zeros((128, 256), np.float32)
-    div[:QUAD, 96:96 + BASIS] = -high
-    div[:QUAD, 224:224 + BASIS] = -low
+            out[512 + 128 * f:512 + 128 * f + QUAD, 32 * f:32 * f + BASIS] = scale * high
+        if spilled is None:
+            return out
+        high, low = halves(spilled)
+        more = np.zeros((256, 256), np.float32)
+        more[:QUAD, 96:96 + BASIS] = -high
+        more[:QUAD, 224:224 + BASIS] = -low
+        more[128:128 + QUAD, 96:96 + BASIS] = -high
+        return np.concatenate([out, more])
+
     adjoint_value = adjoint_table(value_w)
-    adjoint_slope = np.concatenate([adjoint_table(slope_w), div])
+    adjoint_slope = adjoint_table(slope_w, value_w)
     middle = np.zeros((STEPS, 128), np.float32)
     for t in range(STEPS):
         for bb in range(8):
@@ -214,80 +218,48 @@
     return jnp.where(same, 1.0, 0.0)
 
 
-def operator_kernel(x_hbm, stiff_hbm, volume_hbm, lagrange_hbm, mortar_hbm, links_hbm, first_hbm, last_hbm,
-                    inner_hbm, plain_hbm, adj_value_hbm, adj_slope_hbm, middle_hbm, out_ref, jump_ref,
-                    x_ref, lagrange_ref, mortar_ref, links_ref, counts_ref, first_ref, last_ref, inner_ref,
-                    plain_ref, adj_value_ref, adj_slope_ref, middle_ref, stiff, volume, sent, got, back, home, outer, total, grid, trace_own, trace_all,
-                    trace_out, trace_in, fix_own, fix_all, fix_out, fix_in, load_sem, send_sem, recv_sem,
-                    back_send_sem, back_recv_sem, face_send_sem, face_recv_sem):
+def masked_mortar(mortar_ref, counts_ref, patch):
+    row = lax.broadcasted_iota(jnp.int32, (BASIS, BASIS), 0)
+    lefts, rights = [], []
+    for s in range(2):
+        for slot in range(4):
+            at = 4 * patch + slot
+            lefts.append(jnp.where(row < counts_ref[4, at], mortar_ref[slot, s, :, 0, :], 0.0))
+            rights.append(jnp.where(row < counts_ref[5, at], mortar_ref[slot, s, :, 1, :], 0.0))
+    return lefts, rights
+
+
+def spread_kernel(x_in, lagrange_ref, mortar_ref, links_ref, counts_ref, stiff_hbm, volume_hbm, got_out, trace_own,
+                  fix_own, route_out, stiff, volume, x_ref, sent, got, grid, load_sem, send_sem, recv_sem):
     me = lax.axis_index("sub")
+    rows = pl.ds(pl.multiple_of(me * SLAB, 8), SLAB)
     patch = lax.axis_index("patch")
     y, z, core = patch // 16, (patch // 2) % 8, patch % 2
-    group = 2 * y + core
-    line = [lax.rem(z + d, 8) for d in range(8)]
-    line_from = [lax.rem(z + 8 - d, 8) for d in range(8)]
-    plane = [lax.rem(group + d, 8) for d in range(8)]
-    plane_from = [lax.rem(group + 8 - d, 8) for d in range(8)]
-    line_ids = [{"patch": 16 * y + 2 * at + core} for at in line]
-    plane_ids = [{"patch": 16 * (at // 2) + 2 * z + at % 2} for at in plane]
-
-    def exchange(n, source, target, slot, slots_from, ids):
-        def one(d, at):
-            return pltpu.make_async_remote_copy(
-                src_ref=source(d), dst_ref=target.at[at], send_sem=face_send_sem.at[n, d],
-                recv_sem=face_recv_sem.at[n, d], device_id=ids[d], device_id_type=MESH)
-
-        def start():
-            for d in range(1, 8):
-                one(d, slot).start()
-
-        def finish():
-            for d in range(1, 8):
-                one(d, slot).wait_send()
-                one(d, slots_from[d]).wait_recv()
-
-        return start, finish
-
-    rows = pl.ds(pl.multiple_of(me * SLAB, 8), SLAB)
-    pairs = [(slot, s, n) for slot in range(4) for s in range(2) for n in range(2)]
-    loads = [
-        [(x_hbm.at[0, 0, :, 0, :], x_ref)],
-        [(links_hbm, links_ref)],
-        [(links_hbm, counts_ref)],
-        [(lagrange_hbm, lagrange_ref)],
-        [(mortar_hbm.at[slot, s, :, n, :], mortar_ref.at[slot, s, n]) for slot, s, n in pairs],
-        [(first_hbm.at[me], first_ref)],
-        [(middle_hbm, middle_ref)],
-        [(inner_hbm, inner_ref), (plain_hbm, plain_ref)],
-        [(stiff_hbm.at[0, rows], stiff), (volume_hbm.at[0, rows], volume)],
-        [(adj_value_hbm, adj_value_ref), (adj_slope_hbm, adj_slope_ref)],
-        [(last_hbm.at[me], last_ref)],
-    ]
-    loads = [[pltpu.make_async_copy(a, b, load_sem.at[n]) for a, b in some] for n, some in enumerate(loads)]
-    for some in loads:
-        for copy in some:
-            copy.start()
-
-    def loaded(*which):
-        for n in which:
-            for copy in loads[n]:
-                copy.wait()
-
     peers = [lax.rem(me + d, SUBS) for d in range(SUBS)]
     origins = [lax.rem(me + SUBS - d, SUBS) for d in range(SUBS)]
     barrier = pltpu.get_barrier_semaphore()
     for d in range(1, SUBS):
         pl.semaphore_signal(barrier, inc=1, device_id={"sub": peers[d]}, device_id_type=MESH)
-    for d in range(1, 8):
-        for ids in (line_ids, plane_ids):
-            pl.semaphore_signal(barrier, inc=1, device_id=ids[d], device_id_type=MESH)
-    loaded(0)
+    loads = [pltpu.make_async_copy(stiff_hbm.at[0, rows], stiff, load_sem.at[0]),
+             pltpu.make_async_copy(volume_hbm.at[0, rows], volume, load_sem.at[1])]
+    for copy in loads:
+        copy.start()
+    x_ref[...] = x_in[0, 0, :, 0, :]
     sent[...] = jnp.zeros_like(sent)
     for q in range(SUBS):
         sent[q, :, 0:729] = x_ref[6 * q:6 * q + 8, :]
         for n in range(6):
             width = min(128, 729 - 128 * n)
             sent[q, n:n + 1, 768:768 + width] = x_ref[6 * q + 8:6 * q + 9, 128 * n:128 * n + width]
+    pl.semaphore_wait(barrier, SUBS - 1)
+    going = [None]
+    for d in range(1, SUBS):
+        copy = pltpu.make_async_remote_copy(
+            src_ref=sent.at[peers[d]], dst_ref=got.at[me], send_sem=send_sem.at[d], recv_sem=recv_sem.at[d],
+            device_id={"sub": peers[d]}, device_id_type=MESH)
+        copy.start()
+        going.append(copy)
+    got[me] = sent[me]
     trace_rows = [[x_ref[26 * s:26 * s + 1, 128 * n:min(128 * n + 128, 729)] for n in range(6)] for s in range(2)]
     for s in range(2):
         tail = jnp.zeros((1, 768 - 729), jnp.float32)
@@ -301,29 +273,7 @@
         for f in range(4):
             for n in range(3):
                 trace_own[4 * h + f:4 * h + f + 1, 128 * n:128 * n + 128] = trace_rows[f][3 * h + n]
-    start_traces, finish_traces = exchange(0, lambda d: trace_own, trace_all, z, line_from, line_ids)
-    start_picked, finish_picked = exchange(1, lambda d: trace_out.at[plane[d]], trace_in, group, plane_from, plane_ids)
-    start_fixes, finish_fixes = exchange(2, lambda d: fix_own, fix_all, group, plane_from, plane_ids)
-    start_sums, finish_sums = exchange(3, lambda d: fix_out.at[line[d]], fix_in, z, line_from, line_ids)
-    pl.semaphore_wait(barrier, SUBS - 1 + 14)
-    going = [None]
-    for d in range(1, SUBS):
-        copy = pltpu.make_async_remote_copy(
-            src_ref=sent.at[peers[d]], dst_ref=got.at[me], send_sem=send_sem.at[d], recv_sem=recv_sem.at[d],
-            device_id={"sub": peers[d]}, device_id_type=MESH)
-        copy.start()
-        going.append(copy)
-    start_traces()
-    trace_all[z] = trace_own[...]
-    got[me] = sent[me]
-    loaded(1, 2, 3, 4)
-    row = lax.broadcasted_iota(jnp.int32, (BASIS, BASIS), 0)
-    lefts, rights = [], []
-    for s in range(2):
-        for slot in range(4):
-            at = 4 * patch + slot
-            lefts.append(jnp.where(row < counts_ref[4, at], mortar_ref[slot, s, 0], 0.0))
-            rights.append(jnp.where(row < counts_ref[5, at], mortar_ref[slot, s, 1], 0.0))
+    lefts, rights = masked_mortar(mortar_ref, counts_ref, patch)
     multipliers = jnp.concatenate([lagrange_ref[slot, 0] for slot in range(4)], axis=0)
     multipliers = jnp.concatenate([multipliers, jnp.zeros((4, 768 - 729), jnp.float32)], axis=1)
     to_matrices([multipliers[:, 128 * n:128 * n + 128] for n in range(6)], grid)
@@ -338,35 +288,86 @@
     for h in range(2):
         for n in range(3):
             fix_own[8 * h:8 * h + 8, 128 * n:128 * n + 128] = fix_rows[3 * h + n]
-    start_fixes()
-    fix_all[group] = fix_own[...]
-    route = routing(links_ref, y, z, core)
-    total[...] = jnp.zeros_like(total)
+    route_out[...] = routing(links_ref, y, z, core)
     for d in range(1, SUBS):
         going[d].wait_send()
         pltpu.make_async_remote_copy(
             src_ref=sent.at[peers[d]], dst_ref=got.at[origins[d]], send_sem=send_sem.at[d],
             recv_sem=recv_sem.at[d], device_id={"sub": peers[d]}, device_id_type=MESH).wait_recv()
 
-    loaded(5)
-    first = first_ref[...]
-    spread = []
-    for f in range(FIELDS):
-        high, low = split(jnp.concatenate([got[f, :, 0:768], ninth_layer(got, f)], axis=0))
-        spread.append(product(first, jnp.concatenate([high, low, high], axis=0)))
-    lane = lanes_of(2 * SLAB)
+    got_out[...] = got[...]
+    for copy in loads:
+        copy.wait()
+
+
+def operator_kernel(got, stiff, volume, mortar_ref, counts_ref, trace_own, fix_own, route_ref, first_ref, last_ref,
+                    inner_ref, plain_ref, adj_value_ref, adj_slope_ref, middle_hbm, out_ref, jump_ref, x_ref,
+                    middle_ref, back, home, outer, total, grid, trace_all, trace_out, trace_in, fix_all, fix_out,
+                    fix_in, load_sem, back_send_sem, back_recv_sem, face_send_sem, face_recv_sem):
+    load_middle = pltpu.make_async_copy(middle_hbm, middle_ref, load_sem)
+    load_middle.start()
+    me = lax.axis_index("sub")
+    patch = lax.axis_index("patch")
+    y, z, core = patch // 16, (patch // 2) % 8, patch % 2
+    group = 2 * y + core
+    line = [lax.rem(z + d, 8) for d in range(8)]
+    line_from = [lax.rem(z + 8 - d, 8) for d in range(8)]
+    plane = [lax.rem(group + d, 8) for d in range(8)]
+    plane_from = [lax.rem(group + 8 - d, 8) for d in range(8)]
+    line_ids = [{"patch": 16 * y + 2 * at + core} for at in line]
+    plane_ids = [{"patch": 16 * (at // 2) + 2 * z + at % 2} for at in plane]
+
+    def exchange(n, source, target, slot, slots_from, ids):
+        def one(d, at):
+            return pltpu.make_async_remote_copy(
+                src_ref=source(d), dst_ref=target.at[at], send_sem=face_send_sem.at[n, d],
+                recv_sem=face_recv_sem.at[n, d], device_id=ids[d], device_id_type=MESH)
+
+        def start():
+            for d in range(1, 8):
+                one(d, slot).start()
+
+        def finish():
+            for d in range(1, 8):
+                one(d, slot).wait_send()
+                one(d, slots_from[d]).wait_recv()
+
+        return start, finish
+
+    peers = [lax.rem(me + d, SUBS) for d in range(SUBS)]
+    origins = [lax.rem(me + SUBS - d, SUBS) for d in range(SUBS)]
+    barrier = pltpu.get_barrier_semaphore()
+    for d in range(1, SUBS):
+        pl.semaphore_signal(barrier, inc=1, device_id={"sub": peers[d]}, device_id_type=MESH)
+    for d in range(1, 8):
+        for ids in (line_ids, plane_ids):
+            pl.semaphore_signal(barrier, inc=1, device_id=ids[d], device_id_type=MESH)
+    start_traces, finish_traces = exchange(0, lambda d: trace_own, trace_all, z, line_from, line_ids)
+    start_picked, finish_picked = exchange(1, lambda d: trace_out.at[plane[d]], trace_in, group, plane_from, plane_ids)
+    start_fixes, finish_fixes = exchange(2, lambda d: fix_own, fix_all, group, plane_from, plane_ids)
+    start_sums, finish_sums = exchange(3, lambda d: fix_out.at[line[d]], fix_in, z, line_from, line_ids)
+    total[...] = jnp.zeros_like(total)
+    first = first_ref[me]
+    slabs = [jnp.concatenate([got[f, :, 0:768], ninth_layer(got, f)], axis=0) for f in range(FIELDS)]
+    lane = lanes_of(16)
+    columns = []
     for j in range(BASIS):
         tile, shift = divmod(BASIS * j, 128)
         merged = None
         for f in range(FIELDS):
-            piece = spread[f][:, 128 * tile:128 * tile + 128]
+            piece = slabs[f][:, 128 * tile:128 * tile + 128]
             if shift + BASIS > 128:
-                piece = jnp.where(lane >= shift, piece, spread[f][:, 128 * tile + 128:128 * tile + 256])
+                piece = jnp.where(lane >= shift, piece, slabs[f][:, 128 * tile + 128:128 * tile + 256])
             turn = (32 * f - shift) % 128
             piece = pltpu.roll(piece, turn, 1) if turn else piece
             merged = piece if f == 0 else jnp.where(lane >= 32 * f, piece, merged)
-        outer[j] = merged
-    loaded(6, 7, 8, 9, 10)
+        high, low = split(merged)
+        columns.append(jnp.concatenate([high, low, high], axis=0))
+    for j in range(0, BASIS, 2):
+        result = product(first, jnp.concatenate(columns[j:j + 2], axis=1))
+        for n in range(min(2, BASIS - j)):
+            outer[j + n] = result[:, 128 * n:128 * n + 128]
+    load_middle.wait()
 
     def step(t, carry):
         def scalar(table, bb, m):
@@ -382,9 +383,6 @@
             for m in range(1, 4):
                 out = out + scalar(table, bb, m) * parts[e + m]
             return out
-
-        across = [middle_sum(0, slopes, bb) for bb in range(8)] + [middle_sum(1, values, bb) for bb in range(8)]
-        along = [middle_sum(0, values, bb) for bb in range(8)]
 
         def pair_sides(x):
             lane = lanes_of(x.shape[0])
@@ -395,14 +393,6 @@
             even = jnp.where(lane < 64, low, turned).astype(jnp.bfloat16)
             odd = jnp.where(lane < 64, turned, low).astype(jnp.bfloat16)
             return jnp.concatenate([high, even], axis=1), jnp.concatenate([high, odd], axis=1)
-
-        even, odd = pair_sides(jnp.concatenate(across, axis=0))
-        across_even = product(even, inner_ref[0])
-        across_odd = product(odd, inner_ref[1])
-        even, odd = pair_sides(jnp.concatenate(along, axis=0))
-        along_even = product(even, inner_ref[2])
-        along_odd = product(odd, inner_ref[3])
-        pvalue = product(odd, plain_ref[...])
 
         def weights(ref):
             lane = lanes_of(SLAB)
@@ -418,28 +408,29 @@
 
         s = weights(stiff)
         w = weights(volume)
-        half = 8 * SLAB
-        pressed = w * pvalue
-        grads = [
-            [across_even[0:half, 0:128], across_even[0:half, 128:256], across_odd[0:half, 0:128],
-             across_odd[0:half, 128:256]],
-            [across_even[half:, 0:128], across_even[half:, 128:256], across_odd[half:, 0:128],
-             across_odd[half:, 128:256]],
-            [along_even[:, 0:128], along_even[:, 128:256], along_odd[:, 0:128], along_odd[:, 128:256]],
-        ]
-        fluxes = []
-        for d in range(3):
-            fluxes.append([s * grads[d][f] - pressed if f == d else s * grads[d][f] for f in range(FIELDS)])
-        spill = w * (grads[0][0] + grads[1][1] + grads[2][2])
-
         def adjoint(parts, table):
             pairs = [split(p) for p in parts]
-            wide = product(jnp.concatenate([p[0] for p in pairs], axis=1), table[...])
-            low = product(jnp.concatenate([p[1] for p in pairs], axis=1), table[:, 0:128])
-            return wide[:, 0:128] + wide[:, 128:256] + low
-
-        heads = [adjoint(fluxes[0], adj_value_ref), adjoint(fluxes[1], adj_value_ref),
-                 adjoint(fluxes[2] + [spill], adj_slope_ref)]
+            sides = [p[0] for p in pairs[:FIELDS]] + [p[1] for p in pairs[:FIELDS]]
+            for pair in pairs[FIELDS:]:
+                sides.extend(pair)
+            wide = product(jnp.concatenate(sides, axis=1), table[...])
+            return wide[:, 0:128] + wide[:, 128:256]
+
+        def gradient(table, parts, at):
+            even, odd = pair_sides(jnp.concatenate([middle_sum(table, parts, bb) for bb in range(8)], axis=0))
+            first, second = product(even, inner_ref[at]), product(odd, inner_ref[at + 1])
+            return [first[:, 0:128], first[:, 128:256], second[:, 0:128], second[:, 128:256]], odd
+
+        along, odd = gradient(0, values, 2)
+        pressed = w * product(odd, plain_ref[...])
+        spill = along[2]
+        heads = [None] * 3
+        for d in range(2):
+            grads, _ = gradient(d, values if d else slopes, 0)
+            spill = spill + grads[d]
+            heads[d] = adjoint([s * g - pressed if f == d else s * g for f, g in enumerate(grads)], adj_value_ref)
+        heads[2] = adjoint([s * g - pressed if f == 2 else s * g for f, g in enumerate(along)] + [w * spill],
+                           adj_slope_ref)
         heads = [[h[SLAB * bb:SLAB * bb + SLAB] for bb in range(8)] for h in heads]
         sums = [[None, None] for _ in range(5)]
         for bb in range(8):
@@ -452,23 +443,29 @@
             total[2 * t + m] += jnp.concatenate(sums[m], axis=0)
         return carry
 
-    lax.fori_loop(0, STEPS // 2, step, 0)
+    lax.fori_loop(0, STEPS // 2, step, 0, unroll=2)
+    pl.semaphore_wait(barrier, SUBS - 1 + 14)
+    start_traces()
+    trace_all[z] = trace_own[...]
+    start_fixes()
+    fix_all[group] = fix_own[...]
+    lax.fori_loop(STEPS // 2, STEPS - 2, step, 0, unroll=2)
     finish_traces()
     high, low = split(trace_all[...].reshape(64, 384))
-    both = (route + pltpu.roll(route, 64, 1)).astype(jnp.bfloat16)
+    both = (route_ref[...] + pltpu.roll(route_ref[...], 64, 1)).astype(jnp.bfloat16)
     trace_out[...] = product(both, jnp.concatenate([high, low], axis=0)).reshape(8, 16, 384)
     start_picked()
     trace_in[group] = trace_out[group]
     finish_fixes()
     high, low = split(fix_all[...].reshape(128, 384))
-    flipped = route.T.astype(jnp.bfloat16)[0:64]
+    flipped = route_ref[...].T.astype(jnp.bfloat16)[0:64]
     fix_out[...] = product(jnp.concatenate([flipped, flipped], axis=1),
                            jnp.concatenate([high, low], axis=0)).reshape(8, 8, 384)
     start_sums()
     fix_in[z] = fix_out[z]
-    lax.fori_loop(STEPS // 2, STEPS, step, 0)
-
-    last = last_ref[...]
+    lax.fori_loop(STEPS - 2, STEPS, step, 0, unroll=2)
+
+    last = last_ref[me]
     lane = lanes_of(16)
     packed = [[jnp.zeros((16, 128), jnp.float32) for _ in range(6)] for _ in range(FIELDS)]
     for j0 in range(0, BASIS, 2):
@@ -506,6 +503,7 @@
     for at in range(1, 8):
         picked = picked + trace_in[at]
     to_matrices([picked[8 * h:8 * h + 8, 128 * n:128 * n + 128] for h in range(2) for n in range(3)], grid)
+    lefts, rights = masked_mortar(mortar_ref, counts_ref, patch)
     jumps = []
     for k in range(8):
         jump = exact(grid[pl.ds(k, BASIS, stride=8), :][:, 0:BASIS], rights[k], ((1,), (1,)))
@@ -547,52 +545,60 @@
 def per_device(state, stiff_weight, volume_weight, lagrange, mortar, links):
     vmem = pl.BlockSpec(memory_space=pltpu.VMEM)
     anywhere = pl.BlockSpec(memory_space=pl.ANY)
+    smem = pl.BlockSpec(memory_space=pltpu.SMEM)
+    f32 = lambda *shape: jax.ShapeDtypeStruct(shape, jnp.float32)
     constants = constant_tables()
-    local = [x.shape[1:] if n < 2 else x.shape for n, x in enumerate(constants)]
+    mortar = jnp.transpose(mortar, (0, 1, 3, 2, 4))
+    links = links.T
+    spread = pl.pallas_call(
+        spread_kernel,
+        name="spread",
+        out_shape=(f32(SUBS, 8, 896), f32(8, 384), f32(16, 384), f32(128, 128),
+                   f32(SLAB, QUAD * QUAD), f32(SLAB, QUAD * QUAD)),
+        in_specs=[vmem, vmem, vmem, vmem, smem, anywhere, anywhere],
+        out_specs=(vmem,) * 6,
+        scratch_shapes=[
+            pltpu.VMEM((BASIS, BASIS * BASIS), jnp.float32),
+            pltpu.VMEM((SUBS, 8, 896), jnp.float32),
+            pltpu.VMEM((SUBS, 8, 896), jnp.float32),
+            pltpu.VMEM((BASIS * 8, 128), jnp.float32),
+            pltpu.SemaphoreType.DMA((2,)),
+            pltpu.SemaphoreType.DMA((SUBS,)),
+            pltpu.SemaphoreType.DMA((SUBS,)),
+        ],
+        compiler_params=pltpu.CompilerParams(collective_id=0, has_side_effects=True, vmem_limit_bytes=52 * 10**6),
+        cost_estimate=pl.CostEstimate(flops=10**9, bytes_accessed=10**5, transcendentals=0),
+    )(jnp.transpose(state, (0, 1, 3, 2, 4)), lagrange, mortar, links, links,
+      stiff_weight, volume_weight)
     result, jumps = pl.pallas_call(
         operator_kernel,
         name="operator",
-        out_shape=(jax.ShapeDtypeStruct((1, 1, BASIS, 1, BASIS * BASIS), jnp.float32),
-                   jax.ShapeDtypeStruct(lagrange.shape, jnp.float32)),
-        in_specs=[anywhere] * 13,
+        out_shape=(f32(1, 1, BASIS, 1, BASIS * BASIS), f32(*lagrange.shape)),
+        in_specs=[vmem] * 4 + [smem] + [vmem] * 9 + [anywhere],
         out_specs=(vmem, vmem),
         scratch_shapes=[
             pltpu.VMEM((BASIS, BASIS * BASIS), jnp.float32),
-            pltpu.VMEM(lagrange.shape, jnp.float32),
-            pltpu.VMEM(mortar.shape, jnp.float32),
-            pltpu.VMEM((6, 256), jnp.int32),
-            pltpu.SMEM((6, 256), jnp.int32),
-            *[pltpu.VMEM(shape, jnp.bfloat16) for shape in local[:-1]],
-            pltpu.SMEM(local[-1], jnp.float32),
-            pltpu.VMEM((SLAB, QUAD * QUAD), jnp.float32),
-            pltpu.VMEM((SLAB, QUAD * QUAD), jnp.float32),
-            pltpu.VMEM((SUBS, 8, 896), jnp.float32),
-            pltpu.VMEM((SUBS, 8, 896), jnp.float32),
+            pltpu.SMEM(constants[-1].shape, jnp.float32),
             pltpu.VMEM((SUBS, 8, 896), jnp.float32),
             pltpu.VMEM((SUBS, 8, 896), jnp.float32),
             pltpu.VMEM((BASIS, 2 * SLAB, 128), jnp.float32),
             pltpu.VMEM((BASIS, 2 * SLAB, 128), jnp.float32),
             pltpu.VMEM((BASIS * 8, 128), jnp.float32),
-            pltpu.VMEM((8, 384), jnp.float32),
             pltpu.VMEM((8, 8, 384), jnp.float32),
             pltpu.VMEM((8, 16, 384), jnp.float32),
             pltpu.VMEM((8, 16, 384), jnp.float32),
-            pltpu.VMEM((16, 384), jnp.float32),
             pltpu.VMEM((8, 16, 384), jnp.float32),
             pltpu.VMEM((8, 8, 384), jnp.float32),
             pltpu.VMEM((8, 8, 384), jnp.float32),
-            pltpu.SemaphoreType.DMA((11,)),
-            pltpu.SemaphoreType.DMA((SUBS,)),
-            pltpu.SemaphoreType.DMA((SUBS,)),
+            pltpu.SemaphoreType.DMA,
             pltpu.SemaphoreType.DMA((SUBS,)),
             pltpu.SemaphoreType.DMA((SUBS,)),
             pltpu.SemaphoreType.DMA((4, 8)),
             pltpu.SemaphoreType.DMA((4, 8)),
         ],
-        compiler_params=pltpu.CompilerParams(collective_id=0, has_side_effects=True),
+        compiler_params=pltpu.CompilerParams(collective_id=1, has_side_effects=True, vmem_limit_bytes=52 * 10**6),
         cost_estimate=pl.CostEstimate(flops=10**10, bytes_accessed=4 * 10**6, transcendentals=0),
-    )(jnp.transpose(state, (0, 1, 3, 2, 4)), stiff_weight, volume_weight, lagrange,
-      jnp.transpose(mortar, (0, 1, 3, 2, 4)), links.T, *constants)
+    )(spread[0], *spread[4:], mortar, links, *spread[1:4], *constants)
     return jnp.transpose(result, (0, 1, 3, 2, 4)), jumps
 
 

time: 34.3 us -> 38.9 us (1.13)
  the two profiles are of different devices: /device:TPU:16 before, /device:TPU:1 now
where the time goes in v4:
time: 38.9 us; the launch traced here: 38.6 us
  Pallas kernels  33.3 us (86%)
  local copies, waits for them, and re-layouts  4.5 us (12%)
  between operations  0.77 us (2%)
    pallas_call x1, Pallas kernels, per_device(): pl.pallas_call(operator_kernel, name='operator', out_shape=(f32(1, 1, BAS...  26.3 us
    pallas_call x1, Pallas kernels, per_device(): pl.pallas_call(spread_kernel, name='spread', out_shape=(f32(SUBS, 8, 896)...  7 us
    unnamed x28, local copies, waits for them, and re-layouts  4.5 us

profile of v4, /device:TPU:1, one launch (start us, length us, event | category | flops | bytes accessed | tf_op | source)
XLA Modules:
  0.0 38.6 jit_solution(8200622299711957171)
XLA Ops:
  0.6 0.0 copy-start
  0.6 0.9 %copy-done = f32[4,2,2,27,27]{4,2,3,1,0:T(2,128)S(1)} copy-done((f32[4,2,2,27,27]{4,2,3,1,0:T(2,128)S(1)}, f32[4,2,2,27,27]{4,2,3,1,0:T(2,128)}, u32[]{:S(2)}) %copy-start) | copy-done | bytes 46680
  1.6 0.0 copy-start.2
  1.6 0.9 %copy-done.2 = f32[1,1,1,27,729]{4,2,3,1,0:T(1,128)S(1)} copy-done((f32[1,1,1,27,729]{4,2,3,1,0:T(1,128)S(1)}, f32[1,1,1,27,729]{4,2,3,1,0:T(1,128)}, u32[]{:S(2)}) %copy-start.2) | copy-done | bytes 78756
  2.5 0.0 copy-start.3
  2.5 0.7 %copy-done.3 = s32[256,6]{0,1:T(8,128)S(1)} copy-done((s32[256,6]{0,1:T(8,128)S(1)}, s32[256,6]{0,1:T(8,128)}, u32[]{:S(2)}) %copy-start.3) | copy-done | bytes 6168
  3.2 0.0 copy-start.5
  3.2 0.7 %copy-done.5 = f32[4,1,1,729]{3,2,1,0:T(1,128)S(1)} copy-done((f32[4,1,1,729]{3,2,1,0:T(1,128)S(1)}, f32[4,1,1,729]{3,2,1,0:T(1,128)}, u32[]{:S(2)}) %copy-start.5) | copy-done | bytes 11688
  3.9 0.0 copy-start.1
  3.9 0.0 copy-start.4
  3.9 0.0 copy-start.6
  3.9 0.0 copy-start.7
  3.9 0.0 copy-start.8
  3.9 0.0 copy-start.9
  3.9 0.0 copy-start.10
  3.9 0.0 copy-start.11
  3.9 0.0 copy-start.12
  3.9 7.0 %spread.1 = (f32[4,8,896]{2,1,0:T(8,128)S(1)}, f32[8,384]{1,0:T(8,128)S(1)}, f32[16,384]{1,0:T(8,128)S(1)}, f32[128,128]{1,0:T(8,128)S(1)}, f32[24,9216]{1,0:T(8,128)S(1)}, /*index=5*/f32[24,9216]{1,0:T(8,128)S(1)}) custom-call(f32[1,1,27,1,729]{4,3,2,1,0:T(1,128)S(1)} %bitcast.8, f32[4,1,1,729]{3,2,1,0:T(1,128)S(1)} %copy-done.5, ...), custom_call_target="tpu_custom_call" | custom-call | flops 1000000000 | bytes 100000 | tf_op jit(solution)/shard_map/spread/pallas_call | solution.py:553
  10.9 0.0 copy-done.1
  11.0 0.0 copy-done.4
  11.0 0.0 copy-done.6
  11.0 0.0 copy-done.7
  11.0 0.0 copy-done.8
  11.0 0.0 copy-done.9
  11.0 0.0 copy-done.10
  11.0 0.0 copy-done.11
  11.0 0.0 copy-done.12
  11.0 26.3 %operator.1 = (f32[1,1,27,1,729]{4,3,2,1,0:T(1,128)S(1)}, f32[4,1,1,729]{3,2,1,0:T(1,128)S(1)}) custom-call(f32[4,8,896]{2,1,0:T(8,128)S(1)} %get-tuple-element.10.got, f32[24,9216]{1,0:T(8,128)S(1)} %get-tuple-element.11.stiff, f32[24,9216]{1,0:T(8,128)S(1)} %get-tuple-element.12.volume, f32[4,2,27,2,27]{4,3,2,1,0:T(2,128)S(1)} %bitcast.7, ...), custom_call_target="tpu_custom_call" | custom-call | flops 10000000000 | bytes 4000000 | tf_op jit(solution)/shard_map/operator/pallas_call | solution.py:573
  37.4 0.6 %copy.18 = f32[1,1,1,27,729]{4,2,3,1,0:T(1,128)} copy(f32[1,1,1,27,729]{4,2,3,1,0:T(1,128)S(1)} %bitcast.9) | data formatting | bytes 157464
  38.0 0.6 %copy.19 = f32[4,1,1,729]{3,2,1,0:T(1,128)} copy(f32[4,1,1,729]{3,2,1,0:T(1,128)S(1)} %get-tuple-element.23) | data formatting | bytes 23328
Async XLA Ops:
  0.6 0.9 %copy-start = (f32[4,2,2,27,27]{4,2,3,1,0:T(2,128)S(1)}, f32[4,2,2,27,27]{4,2,3,1,0:T(2,128)}, u32[]{:S(2)}) copy-start(f32[4,2,2,27,27]{4,2,3,1,0:T(2,128)} %param.17) | copy-start | bytes 139972
  1.6 0.9 %copy-start.2 = (f32[1,1,1,27,729]{4,2,3,1,0:T(1,128)S(1)}, f32[1,1,1,27,729]{4,2,3,1,0:T(1,128)}, u32[]{:S(2)}) copy-start(f32[1,1,1,27,729]{4,2,3,1,0:T(1,128)} %param.13) | copy-start | bytes 236200
  2.5 0.7 %copy-start.3 = (s32[256,6]{0,1:T(8,128)S(1)}, s32[256,6]{0,1:T(8,128)}, u32[]{:S(2)}) copy-start(s32[256,6]{0,1:T(8,128)} %param.18) | copy-start | bytes 18436
  3.2 0.7 %copy-start.5 = (f32[4,1,1,729]{3,2,1,0:T(1,128)S(1)}, f32[4,1,1,729]{3,2,1,0:T(1,128)}, u32[]{:S(2)}) copy-start(f32[4,1,1,729]{3,2,1,0:T(1,128)} %lagrange_ref.1) | copy-start | bytes 34996
  3.9 7.1 %copy-start.1 = (f32[4,2,2,27,27]{4,2,3,1,0:T(2,128)S(1)}, f32[4,2,2,27,27]{4,2,3,1,0:T(2,128)}, u32[]{:S(2)}) copy-start(f32[4,2,2,27,27]{4,2,3,1,0:T(2,128)} %param.17) | copy-start | bytes 139972
  3.9 7.1 %copy-start.4 = (s32[256,6]{0,1:T(8,128)S(1)}, s32[256,6]{0,1:T(8,128)}, u32[]{:S(2)}) copy-start(s32[256,6]{0,1:T(8,128)} %param.18) | copy-start | bytes 18436
  3.9 7.1 %copy-start.6 = (bf16[1280,256]{1,0:T(8,128)(2,1)S(1)}, bf16[1280,256]{1,0:T(8,128)(2,1)}, u32[]{:S(2)}) copy-start(bf16[1280,256]{1,0:T(8,128)(2,1)} %constant.19.clone.adj_slope_ref) | copy-start | bytes 1966084
  3.9 7.1 %copy-start.7 = (bf16[1024,256]{1,0:T(8,128)(2,1)S(1)}, bf16[1024,256]{1,0:T(8,128)(2,1)}, u32[]{:S(2)}) copy-start(bf16[1024,256]{1,0:T(8,128)(2,1)} %constant.18.clone.adj_value_ref) | copy-start | bytes 1572868
  3.9 7.1 %copy-start.8 = (bf16[4,256,256]{2,1,0:T(8,128)(2,1)S(1)}, bf16[4,256,256]{2,1,0:T(8,128)(2,1)}, u32[]{:S(2)}) copy-start(bf16[4,256,256]{2,1,0:T(8,128)(2,1)} %constant.16.clone.inner_ref) | copy-start | bytes 1572868
  3.9 7.1 %copy-start.9 = (bf16[256,128]{1,0:T(8,128)(2,1)S(1)}, bf16[256,128]{1,0:T(8,128)(2,1)}, u32[]{:S(2)}) copy-start(bf16[256,128]{1,0:T(8,128)(2,1)} %constant.17.clone.plain_ref) | copy-start | bytes 196612
  3.9 7.1 %copy-start.10 = (bf16[4,48,48]{2,1,0:T(8,128)(2,1)S(1)}, bf16[4,48,48]{2,1,0:T(8,128)(2,1)}, u32[]{:S(2)}) copy-start(bf16[4,48,48]{2,1,0:T(8,128)(2,1)} %constant.14.clone.first_ref) | copy-start | bytes 55300
  3.9 7.1 %copy-start.11 = (bf16[4,16,144]{2,1,0:T(8,128)(2,1)S(1)}, bf16[4,16,144]{2,1,0:T(8,128)(2,1)}, u32[]{:S(2)}) copy-start(bf16[4,16,144]{2,1,0:T(8,128)(2,1)} %constant.15.clone.last_ref) | copy-start | bytes 55300
  3.9 7.1 %copy-start.12 = (f32[12,128]{1,0:T(8,128)S(1)}, f32[12,128]{1,0:T(8,128)}, u32[]{:S(2)}) copy-start(f32[12,128]{1,0:T(8,128)} %constant.20.clone.middle_hbm) | copy-start | bytes 18436

commit v5 on v3

--- a/solution.py
+++ b/solution.py
@@ -119,22 +119,26 @@
     inner = np.stack([value_even, value_odd, slope_even, slope_odd])
     plain = value_odd[:, 128:]
 
-    def adjoint_table(table):
+    def adjoint_table(table, spilled=None):
         high, low = halves(table)
-        out = np.zeros((512, 256), np.float32)
+        out = np.zeros((1024, 256), np.float32)
         for f in range(FIELDS):
             scale = -stabilize if f == FIELDS - 1 else 1.0
             rows = slice(128 * f, 128 * f + QUAD)
             out[rows, 32 * f:32 * f + BASIS] = scale * high
             out[rows, 128 + 32 * f:128 + 32 * f + BASIS] = scale * low
-        return out
-
-    high, low = halves(value_w)
-    div = np.zeros((128, 256), np.float32)
-    div[:QUAD, 96:96 + BASIS] = -high
-    div[:QUAD, 224:224 + BASIS] = -low
+            out[512 + 128 * f:512 + 128 * f + QUAD, 32 * f:32 * f + BASIS] = scale * high
+        if spilled is None:
+            return out
+        high, low = halves(spilled)
+        more = np.zeros((256, 256), np.float32)
+        more[:QUAD, 96:96 + BASIS] = -high
+        more[:QUAD, 224:224 + BASIS] = -low
+        more[128:128 + QUAD, 96:96 + BASIS] = -high
+        return np.concatenate([out, more])
+
     adjoint_value = adjoint_table(value_w)
-    adjoint_slope = np.concatenate([adjoint_table(slope_w), div])
+    adjoint_slope = adjoint_table(slope_w, value_w)
     middle = np.zeros((STEPS, 128), np.float32)
     for t in range(STEPS):
         for bb in range(8):
@@ -248,6 +252,14 @@
 
         return start, finish
 
+    peers = [lax.rem(me + d, SUBS) for d in range(SUBS)]
+    origins = [lax.rem(me + SUBS - d, SUBS) for d in range(SUBS)]
+    barrier = pltpu.get_barrier_semaphore()
+    for d in range(1, SUBS):
+        pl.semaphore_signal(barrier, inc=1, device_id={"sub": peers[d]}, device_id_type=MESH)
+    for d in range(1, 8):
+        for ids in (line_ids, plane_ids):
+            pl.semaphore_signal(barrier, inc=1, device_id=ids[d], device_id_type=MESH)
     rows = pl.ds(pl.multiple_of(me * SLAB, 8), SLAB)
     pairs = [(slot, s, n) for slot in range(4) for s in range(2) for n in range(2)]
     loads = [
@@ -273,14 +285,6 @@
             for copy in loads[n]:
                 copy.wait()
 
-    peers = [lax.rem(me + d, SUBS) for d in range(SUBS)]
-    origins = [lax.rem(me + SUBS - d, SUBS) for d in range(SUBS)]
-    barrier = pltpu.get_barrier_semaphore()
-    for d in range(1, SUBS):
-        pl.semaphore_signal(barrier, inc=1, device_id={"sub": peers[d]}, device_id_type=MESH)
-    for d in range(1, 8):
-        for ids in (line_ids, plane_ids):
-            pl.semaphore_signal(barrier, inc=1, device_id=ids[d], device_id_type=MESH)
     loaded(0)
     sent[...] = jnp.zeros_like(sent)
     for q in range(SUBS):
@@ -350,22 +354,25 @@
 
     loaded(5)
     first = first_ref[...]
-    spread = []
-    for f in range(FIELDS):
-        high, low = split(jnp.concatenate([got[f, :, 0:768], ninth_layer(got, f)], axis=0))
-        spread.append(product(first, jnp.concatenate([high, low, high], axis=0)))
-    lane = lanes_of(2 * SLAB)
+    slabs = [jnp.concatenate([got[f, :, 0:768], ninth_layer(got, f)], axis=0) for f in range(FIELDS)]
+    lane = lanes_of(16)
+    columns = []
     for j in range(BASIS):
         tile, shift = divmod(BASIS * j, 128)
         merged = None
         for f in range(FIELDS):
-            piece = spread[f][:, 128 * tile:128 * tile + 128]
+            piece = slabs[f][:, 128 * tile:128 * tile + 128]
             if shift + BASIS > 128:
-                piece = jnp.where(lane >= shift, piece, spread[f][:, 128 * tile + 128:128 * tile + 256])
+                piece = jnp.where(lane >= shift, piece, slabs[f][:, 128 * tile + 128:128 * tile + 256])
             turn = (32 * f - shift) % 128
             piece = pltpu.roll(piece, turn, 1) if turn else piece
             merged = piece if f == 0 else jnp.where(lane >= 32 * f, piece, merged)
-        outer[j] = merged
+        high, low = split(merged)
+        columns.append(jnp.concatenate([high, low, high], axis=0))
+    for j in range(0, BASIS, 2):
+        result = product(first, jnp.concatenate(columns[j:j + 2], axis=1))
+        for n in range(min(2, BASIS - j)):
+            outer[j + n] = result[:, 128 * n:128 * n + 128]
     loaded(6, 7, 8, 9, 10)
 
     def step(t, carry):
@@ -382,9 +389,6 @@
             for m in range(1, 4):
                 out = out + scalar(table, bb, m) * parts[e + m]
             return out
-
-        across = [middle_sum(0, slopes, bb) for bb in range(8)] + [middle_sum(1, values, bb) for bb in range(8)]
-        along = [middle_sum(0, values, bb) for bb in range(8)]
 
         def pair_sides(x):
             lane = lanes_of(x.shape[0])
@@ -395,14 +399,6 @@
             even = jnp.where(lane < 64, low, turned).astype(jnp.bfloat16)
             odd = jnp.where(lane < 64, turned, low).astype(jnp.bfloat16)
             return jnp.concatenate([high, even], axis=1), jnp.concatenate([high, odd], axis=1)
-
-        even, odd = pair_sides(jnp.concatenate(across, axis=0))
-        across_even = product(even, inner_ref[0])
-        across_odd = product(odd, inner_ref[1])
-        even, odd = pair_sides(jnp.concatenate(along, axis=0))
-        along_even = product(even, inner_ref[2])
-        along_odd = product(odd, inner_ref[3])
-        pvalue = product(odd, plain_ref[...])
 
         def weights(ref):
             lane = lanes_of(SLAB)
@@ -418,28 +414,29 @@
 
         s = weights(stiff)
         w = weights(volume)
-        half = 8 * SLAB
-        pressed = w * pvalue
-        grads = [
-            [across_even[0:half, 0:128], across_even[0:half, 128:256], across_odd[0:half, 0:128],
-             across_odd[0:half, 128:256]],
-            [across_even[half:, 0:128], across_even[half:, 128:256], across_odd[half:, 0:128],
-             across_odd[half:, 128:256]],
-            [along_even[:, 0:128], along_even[:, 128:256], along_odd[:, 0:128], along_odd[:, 128:256]],
-        ]
-        fluxes = []
-        for d in range(3):
-            fluxes.append([s * grads[d][f] - pressed if f == d else s * grads[d][f] for f in range(FIELDS)])
-        spill = w * (grads[0][0] + grads[1][1] + grads[2][2])
-
         def adjoint(parts, table):
             pairs = [split(p) for p in parts]
-            wide = product(jnp.concatenate([p[0] for p in pairs], axis=1), table[...])
-            low = product(jnp.concatenate([p[1] for p in pairs], axis=1), table[:, 0:128])
-            return wide[:, 0:128] + wide[:, 128:256] + low
-
-        heads = [adjoint(fluxes[0], adj_value_ref), adjoint(fluxes[1], adj_value_ref),
-                 adjoint(fluxes[2] + [spill], adj_slope_ref)]
+            sides = [p[0] for p in pairs[:FIELDS]] + [p[1] for p in pairs[:FIELDS]]
+            for pair in pairs[FIELDS:]:
+                sides.extend(pair)
+            wide = product(jnp.concatenate(sides, axis=1), table[...])
+            return wide[:, 0:128] + wide[:, 128:256]
+
+        def gradient(table, parts, at):
+            even, odd = pair_sides(jnp.concatenate([middle_sum(table, parts, bb) for bb in range(8)], axis=0))
+            first, second = product(even, inner_ref[at]), product(odd, inner_ref[at + 1])
+            return [first[:, 0:128], first[:, 128:256], second[:, 0:128], second[:, 128:256]], odd
+
+        along, odd = gradient(0, values, 2)
+        pressed = w * product(odd, plain_ref[...])
+        spill = along[2]
+        heads = [None] * 3
+        for d in range(2):
+            grads, _ = gradient(d, values if d else slopes, 0)
+            spill = spill + grads[d]
+            heads[d] = adjoint([s * g - pressed if f == d else s * g for f, g in enumerate(grads)], adj_value_ref)
+        heads[2] = adjoint([s * g - pressed if f == 2 else s * g for f, g in enumerate(along)] + [w * spill],
+                           adj_slope_ref)
         heads = [[h[SLAB * bb:SLAB * bb + SLAB] for bb in range(8)] for h in heads]
         sums = [[None, None] for _ in range(5)]
         for bb in range(8):
@@ -452,7 +449,7 @@
             total[2 * t + m] += jnp.concatenate(sums[m], axis=0)
         return carry
 
-    lax.fori_loop(0, STEPS // 2, step, 0)
+    lax.fori_loop(0, STEPS // 2, step, 0, unroll=2)
     finish_traces()
     high, low = split(trace_all[...].reshape(64, 384))
     both = (route + pltpu.roll(route, 64, 1)).astype(jnp.bfloat16)
@@ -466,7 +463,7 @@
                            jnp.concatenate([high, low], axis=0)).reshape(8, 8, 384)
     start_sums()
     fix_in[z] = fix_out[z]
-    lax.fori_loop(STEPS // 2, STEPS, step, 0)
+    lax.fori_loop(STEPS // 2, STEPS, step, 0, unroll=2)
 
     last = last_ref[...]
     lane = lanes_of(16)
@@ -589,10 +586,11 @@
             pltpu.SemaphoreType.DMA((4, 8)),
             pltpu.SemaphoreType.DMA((4, 8)),
         ],
-        compiler_params=pltpu.CompilerParams(collective_id=0, has_side_effects=True),
+        compiler_params=pltpu.CompilerParams(collective_id=0, has_side_effects=True, vmem_limit_bytes=54 * 10**6),
         cost_estimate=pl.CostEstimate(flops=10**10, bytes_accessed=4 * 10**6, transcendentals=0),
-    )(jnp.transpose(state, (0, 1, 3, 2, 4)), stiff_weight, volume_weight, lagrange,
-      jnp.transpose(mortar, (0, 1, 3, 2, 4)), links.T, *constants)
+    )(*[pltpu.with_memory_space_constraint(x, pltpu.HBM) for x in (
+        jnp.transpose(state, (0, 1, 3, 2, 4)), stiff_weight, volume_weight, lagrange,
+        jnp.transpose(mortar, (0, 1, 3, 2, 4)), links.T, *constants)])
     return jnp.transpose(result, (0, 1, 3, 2, 4)), jumps
 
 

time: 34.3 us -> 30.1 us (0.88)
  the two profiles are of different devices: /device:TPU:16 before, /device:TPU:1 now
where the time goes in v5:
time: 30.1 us; the launch traced here: 30 us
  Pallas kernels  28.1 us (93%)
  local copies, waits for them, and re-layouts  1.24 us (4%)
  between operations  0.64 us (2%)
    pallas_call x1, Pallas kernels, per_device(): pl.pallas_call(operator_kernel, name='operator', out_shape=(jax.ShapeDtyp...  28.1 us
    unnamed x2, local copies, waits for them, and re-layouts  1.24 us

profile of v5, /device:TPU:1, one launch (start us, length us, event | category | flops | bytes accessed | tf_op | source)
XLA Modules:
  0.0 30.0 jit_solution(12380484216210491149)
XLA Ops:
  0.6 28.1 %operator.1 = (f32[1,1,27,1,729]{4,3,2,1,0:T(1,128)S(1)}, f32[4,1,1,729]{3,2,1,0:T(1,128)S(1)}) custom-call(f32[1,1,27,1,729]{4,3,2,1,0:T(1,128)} %bitcast.8, f32[1,96,9216]{2,1,0:T(8,128)} %stiff_hbm.1, f32[1,96,9216]{2,1,0:T(8,128)} %volume_hbm.1, f32[4,1,1,729]{3,2,1,0:T(1,128)} %lagrange_hbm.1, f32[4,2,27,2,27]{4,3,2,1,0:T(2,128)} %bitcast.7, ...), custom_call_target="tpu_custom_call" | custom-call | flops 10000000000 | bytes 4000000 | tf_op jit(solution)/shard_map/operator/pallas_call | solution.py:549
  28.8 0.6 %copy.18 = f32[1,1,1,27,729]{4,2,3,1,0:T(1,128)} copy(f32[1,1,1,27,729]{4,2,3,1,0:T(1,128)S(1)} %bitcast.6) | data formatting | bytes 157464
  29.4 0.6 %copy.19 = f32[4,1,1,729]{3,2,1,0:T(1,128)} copy(f32[4,1,1,729]{3,2,1,0:T(1,128)S(1)} %get-tuple-element.11) | data formatting | bytes 23328

commit v6 on v4

--- a/solution.py
+++ b/solution.py
@@ -224,14 +224,18 @@
     for s in range(2):
         for slot in range(4):
             at = 4 * patch + slot
-            lefts.append(jnp.where(row < counts_ref[4, at], mortar_ref[slot, s, :, 0, :], 0.0))
-            rights.append(jnp.where(row < counts_ref[5, at], mortar_ref[slot, s, :, 1, :], 0.0))
+            lefts.append(jnp.where(row < counts_ref[4, at], mortar_ref[slot, s, 0], 0.0))
+            rights.append(jnp.where(row < counts_ref[5, at], mortar_ref[slot, s, 1], 0.0))
     return lefts, rights
 
 
-def spread_kernel(x_in, lagrange_ref, mortar_ref, links_ref, counts_ref, stiff_hbm, volume_hbm, got_out, trace_own,
-                  fix_own, route_out, stiff, volume, x_ref, sent, got, grid, load_sem, send_sem, recv_sem):
+def spread_kernel(x_hbm, lagrange_hbm, mortar_hbm, links_hbm, stiff_hbm, volume_hbm, first_hbm, last_hbm, inner_hbm,
+                  plain_hbm, adj_value_hbm, adj_slope_hbm, got_out, trace_own, fix_own, route_out, mortar_ref, stiff,
+                  volume, first_ref, last_ref, inner_ref, plain_ref, adj_value_ref, adj_slope_ref, x_ref,
+                  lagrange_ref, links_ref, counts_ref, sent, got, grid, load_sem, send_sem, recv_sem):
     me = lax.axis_index("sub")
+    load_x = pltpu.make_async_copy(x_hbm.at[0, 0, :, 0, :], x_ref, load_sem.at[0])
+    load_x.start()
     rows = pl.ds(pl.multiple_of(me * SLAB, 8), SLAB)
     patch = lax.axis_index("patch")
     y, z, core = patch // 16, (patch // 2) % 8, patch % 2
@@ -240,11 +244,25 @@
     barrier = pltpu.get_barrier_semaphore()
     for d in range(1, SUBS):
         pl.semaphore_signal(barrier, inc=1, device_id={"sub": peers[d]}, device_id_type=MESH)
-    loads = [pltpu.make_async_copy(stiff_hbm.at[0, rows], stiff, load_sem.at[0]),
-             pltpu.make_async_copy(volume_hbm.at[0, rows], volume, load_sem.at[1])]
-    for copy in loads:
+    pairs = [(slot, s, n) for slot in range(4) for s in range(2) for n in range(2)]
+    early = [
+        [(links_hbm, links_ref)],
+        [(links_hbm, counts_ref)],
+        [(lagrange_hbm, lagrange_ref)],
+        [(mortar_hbm.at[slot, s, :, n, :], mortar_ref.at[slot, s, n]) for slot, s, n in pairs],
+    ]
+    late = [
+        [(stiff_hbm.at[0, rows], stiff), (volume_hbm.at[0, rows], volume)],
+        [(first_hbm.at[me], first_ref)],
+        [(inner_hbm, inner_ref), (plain_hbm, plain_ref), (adj_value_hbm, adj_value_ref),
+         (adj_slope_hbm, adj_slope_ref)],
+        [(last_hbm.at[me], last_ref)],
+    ]
+    early = [pltpu.make_async_copy(a, b, load_sem.at[1 + n]) for n, some in enumerate(early) for a, b in some]
+    late = [pltpu.make_async_copy(a, b, load_sem.at[5 + n]) for n, some in enumerate(late) for a, b in some]
+    for copy in early + late:
         copy.start()
-    x_ref[...] = x_in[0, 0, :, 0, :]
+    load_x.wait()
     sent[...] = jnp.zeros_like(sent)
     for q in range(SUBS):
         sent[q, :, 0:729] = x_ref[6 * q:6 * q + 8, :]
@@ -273,6 +291,8 @@
         for f in range(4):
             for n in range(3):
                 trace_own[4 * h + f:4 * h + f + 1, 128 * n:128 * n + 128] = trace_rows[f][3 * h + n]
+    for copy in early:
+        copy.wait()
     lefts, rights = masked_mortar(mortar_ref, counts_ref, patch)
     multipliers = jnp.concatenate([lagrange_ref[slot, 0] for slot in range(4)], axis=0)
     multipliers = jnp.concatenate([multipliers, jnp.zeros((4, 768 - 729), jnp.float32)], axis=1)
@@ -296,16 +316,18 @@
             recv_sem=recv_sem.at[d], device_id={"sub": peers[d]}, device_id_type=MESH).wait_recv()
 
     got_out[...] = got[...]
-    for copy in loads:
+    for copy in late:
         copy.wait()
 
 
-def operator_kernel(got, stiff, volume, mortar_ref, counts_ref, trace_own, fix_own, route_ref, first_ref, last_ref,
-                    inner_ref, plain_ref, adj_value_ref, adj_slope_ref, middle_hbm, out_ref, jump_ref, x_ref,
-                    middle_ref, back, home, outer, total, grid, trace_all, trace_out, trace_in, fix_all, fix_out,
-                    fix_in, load_sem, back_send_sem, back_recv_sem, face_send_sem, face_recv_sem):
-    load_middle = pltpu.make_async_copy(middle_hbm, middle_ref, load_sem)
+def operator_kernel(got, trace_own, fix_own, route_ref, mortar_ref, stiff, volume, first_ref, last_ref, inner_ref,
+                    plain_ref, adj_value_ref, adj_slope_ref, middle_hbm, links_hbm, out_ref, jump_ref, x_ref,
+                    middle_ref, counts_ref, back, home, outer, total, grid, trace_all, trace_out, trace_in, fix_all,
+                    fix_out, fix_in, load_sem, back_send_sem, back_recv_sem, face_send_sem, face_recv_sem):
+    load_middle = pltpu.make_async_copy(middle_hbm, middle_ref, load_sem.at[0])
+    load_counts = pltpu.make_async_copy(links_hbm, counts_ref, load_sem.at[1])
     load_middle.start()
+    load_counts.start()
     me = lax.axis_index("sub")
     patch = lax.axis_index("patch")
     y, z, core = patch // 16, (patch // 2) % 8, patch % 2
@@ -347,7 +369,7 @@
     start_fixes, finish_fixes = exchange(2, lambda d: fix_own, fix_all, group, plane_from, plane_ids)
     start_sums, finish_sums = exchange(3, lambda d: fix_out.at[line[d]], fix_in, z, line_from, line_ids)
     total[...] = jnp.zeros_like(total)
-    first = first_ref[me]
+    first = first_ref[...]
     slabs = [jnp.concatenate([got[f, :, 0:768], ninth_layer(got, f)], axis=0) for f in range(FIELDS)]
     lane = lanes_of(16)
     columns = []
@@ -449,23 +471,9 @@
     trace_all[z] = trace_own[...]
     start_fixes()
     fix_all[group] = fix_own[...]
-    lax.fori_loop(STEPS // 2, STEPS - 2, step, 0, unroll=2)
-    finish_traces()
-    high, low = split(trace_all[...].reshape(64, 384))
-    both = (route_ref[...] + pltpu.roll(route_ref[...], 64, 1)).astype(jnp.bfloat16)
-    trace_out[...] = product(both, jnp.concatenate([high, low], axis=0)).reshape(8, 16, 384)
-    start_picked()
-    trace_in[group] = trace_out[group]
-    finish_fixes()
-    high, low = split(fix_all[...].reshape(128, 384))
-    flipped = route_ref[...].T.astype(jnp.bfloat16)[0:64]
-    fix_out[...] = product(jnp.concatenate([flipped, flipped], axis=1),
-                           jnp.concatenate([high, low], axis=0)).reshape(8, 8, 384)
-    start_sums()
-    fix_in[z] = fix_out[z]
-    lax.fori_loop(STEPS - 2, STEPS, step, 0, unroll=2)
-
-    last = last_ref[me]
+    lax.fori_loop(STEPS // 2, STEPS, step, 0, unroll=2)
+
+    last = last_ref[...]
     lane = lanes_of(16)
     packed = [[jnp.zeros((16, 128), jnp.float32) for _ in range(6)] for _ in range(FIELDS)]
     for j0 in range(0, BASIS, 2):
@@ -498,11 +506,34 @@
         copy.start()
         going.append(copy)
     home[me] = back[me]
+    finish_traces()
+    high, low = split(trace_all[...].reshape(64, 384))
+    both = (route_ref[...] + pltpu.roll(route_ref[...], 64, 1)).astype(jnp.bfloat16)
+    trace_out[...] = product(both, jnp.concatenate([high, low], axis=0)).reshape(8, 16, 384)
+    start_picked()
+    trace_in[group] = trace_out[group]
+    finish_fixes()
+    high, low = split(fix_all[...].reshape(128, 384))
+    flipped = route_ref[...].T.astype(jnp.bfloat16)[0:64]
+    fix_out[...] = product(jnp.concatenate([flipped, flipped], axis=1),
+                           jnp.concatenate([high, low], axis=0)).reshape(8, 8, 384)
+    start_sums()
+    fix_in[z] = fix_out[z]
+    for d in range(1, SUBS):
+        going[d].wait_send()
+        pltpu.make_async_remote_copy(
+            src_ref=back.at[peers[d]], dst_ref=home.at[origins[d]], send_sem=back_send_sem.at[d],
+            recv_sem=back_recv_sem.at[d], device_id={"sub": peers[d]}, device_id_type=MESH).wait_recv()
+    x_ref[...] = jnp.zeros((BASIS, BASIS * BASIS), jnp.float32)
+    for q in range(SUBS):
+        x_ref[6 * q:6 * q + 8, :] += home[q, :, 0:729]
+        x_ref[6 * q + 8:6 * q + 9, :] += ninth_layer(home, q)[0:1, 0:729]
     finish_picked()
     picked = trace_in[0]
     for at in range(1, 8):
         picked = picked + trace_in[at]
     to_matrices([picked[8 * h:8 * h + 8, 128 * n:128 * n + 128] for h in range(2) for n in range(3)], grid)
+    load_counts.wait()
     lefts, rights = masked_mortar(mortar_ref, counts_ref, patch)
     jumps = []
     for k in range(8):
@@ -526,15 +557,6 @@
     far = jnp.where(inside, grid[pl.ds(3, BASIS, stride=8), :], 0.0)
     far = pltpu.roll(far, 62, 1)
     ends = jnp.concatenate(sums, axis=1)
-    for d in range(1, SUBS):
-        going[d].wait_send()
-        pltpu.make_async_remote_copy(
-            src_ref=back.at[peers[d]], dst_ref=home.at[origins[d]], send_sem=back_send_sem.at[d],
-            recv_sem=back_recv_sem.at[d], device_id={"sub": peers[d]}, device_id_type=MESH).wait_recv()
-    x_ref[...] = jnp.zeros((BASIS, BASIS * BASIS), jnp.float32)
-    for q in range(SUBS):
-        x_ref[6 * q:6 * q + 8, :] += home[q, :, 0:729]
-        x_ref[6 * q + 8:6 * q + 9, :] += ninth_layer(home, q)[0:1, 0:729]
     for s in range(2):
         x_ref[26 * s:26 * s + 1, :] += ends[s:s + 1, 0:729]
     x_ref[:, 0:128] += near
@@ -545,40 +567,47 @@
 def per_device(state, stiff_weight, volume_weight, lagrange, mortar, links):
     vmem = pl.BlockSpec(memory_space=pltpu.VMEM)
     anywhere = pl.BlockSpec(memory_space=pl.ANY)
-    smem = pl.BlockSpec(memory_space=pltpu.SMEM)
     f32 = lambda *shape: jax.ShapeDtypeStruct(shape, jnp.float32)
     constants = constant_tables()
     mortar = jnp.transpose(mortar, (0, 1, 3, 2, 4))
     links = links.T
+    local = [f32(*(x.shape[1:] if n < 2 else x.shape)) for n, x in enumerate(constants[:-1])]
+    local = [jax.ShapeDtypeStruct(x.shape, jnp.bfloat16) for x in local]
+    pinned = lambda xs: [pltpu.with_memory_space_constraint(x, pltpu.HBM) for x in xs]
+    staged = (f32(SUBS, 8, 896), f32(8, 384), f32(16, 384), f32(128, 128), f32(4, 2, 2, BASIS, BASIS),
+              f32(SLAB, QUAD * QUAD), f32(SLAB, QUAD * QUAD), *local)
     spread = pl.pallas_call(
         spread_kernel,
         name="spread",
-        out_shape=(f32(SUBS, 8, 896), f32(8, 384), f32(16, 384), f32(128, 128),
-                   f32(SLAB, QUAD * QUAD), f32(SLAB, QUAD * QUAD)),
-        in_specs=[vmem, vmem, vmem, vmem, smem, anywhere, anywhere],
-        out_specs=(vmem,) * 6,
+        out_shape=staged,
+        in_specs=[anywhere] * 12,
+        out_specs=(vmem,) * len(staged),
         scratch_shapes=[
             pltpu.VMEM((BASIS, BASIS * BASIS), jnp.float32),
+            pltpu.VMEM(lagrange.shape, jnp.float32),
+            pltpu.VMEM((6, 256), jnp.int32),
+            pltpu.SMEM((6, 256), jnp.int32),
             pltpu.VMEM((SUBS, 8, 896), jnp.float32),
             pltpu.VMEM((SUBS, 8, 896), jnp.float32),
             pltpu.VMEM((BASIS * 8, 128), jnp.float32),
-            pltpu.SemaphoreType.DMA((2,)),
+            pltpu.SemaphoreType.DMA((9,)),
             pltpu.SemaphoreType.DMA((SUBS,)),
             pltpu.SemaphoreType.DMA((SUBS,)),
         ],
-        compiler_params=pltpu.CompilerParams(collective_id=0, has_side_effects=True, vmem_limit_bytes=52 * 10**6),
+        compiler_params=pltpu.CompilerParams(collective_id=0, has_side_effects=True, vmem_limit_bytes=40 * 10**6),
         cost_estimate=pl.CostEstimate(flops=10**9, bytes_accessed=10**5, transcendentals=0),
-    )(jnp.transpose(state, (0, 1, 3, 2, 4)), lagrange, mortar, links, links,
-      stiff_weight, volume_weight)
+    )(*pinned((jnp.transpose(state, (0, 1, 3, 2, 4)), lagrange, mortar, links, stiff_weight, volume_weight,
+               *constants[:-1])))
     result, jumps = pl.pallas_call(
         operator_kernel,
         name="operator",
         out_shape=(f32(1, 1, BASIS, 1, BASIS * BASIS), f32(*lagrange.shape)),
-        in_specs=[vmem] * 4 + [smem] + [vmem] * 9 + [anywhere],
+        in_specs=[vmem] * 13 + [anywhere] * 2,
         out_specs=(vmem, vmem),
         scratch_shapes=[
             pltpu.VMEM((BASIS, BASIS * BASIS), jnp.float32),
             pltpu.SMEM(constants[-1].shape, jnp.float32),
+            pltpu.SMEM((6, 256), jnp.int32),
             pltpu.VMEM((SUBS, 8, 896), jnp.float32),
             pltpu.VMEM((SUBS, 8, 896), jnp.float32),
             pltpu.VMEM((BASIS, 2 * SLAB, 128), jnp.float32),
@@ -590,15 +619,15 @@
             pltpu.VMEM((8, 16, 384), jnp.float32),
             pltpu.VMEM((8, 8, 384), jnp.float32),
             pltpu.VMEM((8, 8, 384), jnp.float32),
-            pltpu.SemaphoreType.DMA,
+            pltpu.SemaphoreType.DMA((2,)),
             pltpu.SemaphoreType.DMA((SUBS,)),
             pltpu.SemaphoreType.DMA((SUBS,)),
             pltpu.SemaphoreType.DMA((4, 8)),
             pltpu.SemaphoreType.DMA((4, 8)),
         ],
-        compiler_params=pltpu.CompilerParams(collective_id=1, has_side_effects=True, vmem_limit_bytes=52 * 10**6),
+        compiler_params=pltpu.CompilerParams(collective_id=1, has_side_effects=True, vmem_limit_bytes=40 * 10**6),
         cost_estimate=pl.CostEstimate(flops=10**10, bytes_accessed=4 * 10**6, transcendentals=0),
-    )(spread[0], *spread[4:], mortar, links, *spread[1:4], *constants)
+    )(*spread, *pinned((constants[-1], links)))
     return jnp.transpose(result, (0, 1, 3, 2, 4)), jumps
 
 

time: 38.9 us -> 33.9 us (0.87)
  local copies, waits for them, and re-layouts: 4.5 us -> 1.24 us
  Pallas kernels: 33.3 us -> 31.9 us
    unnamed x28 -> x2, local copies, waits for them, and re-layouts: 4.5 us -> 1.24 us
    pallas_call x1, Pallas kernels: 26.3 us -> 25.4 us  [per_device(): pl.pallas_call(operator_kernel, name='operator', out_shape=(f32(1, 1, BAS...]
    pallas_call x1, Pallas kernels: 7 us -> 6.42 us  [per_device(): pl.pallas_call(spread_kernel, name='spread', out_shape=staged, in_specs=[...]
where the time goes in v6:
time: 33.9 us; the launch traced here: 33.8 us
  Pallas kernels  31.9 us (94%)
  local copies, waits for them, and re-layouts  1.24 us (4%)
  between operations  0.65 us (2%)
    pallas_call x1, Pallas kernels, per_device(): pl.pallas_call(operator_kernel, name='operator', out_shape=(f32(1, 1, BAS...  25.4 us
    pallas_call x1, Pallas kernels, per_device(): pl.pallas_call(spread_kernel, name='spread', out_shape=staged, in_specs=[...  6.42 us
    unnamed x2, local copies, waits for them, and re-layouts  1.24 us

profile of v6, /device:TPU:1, one launch (start us, length us, event | category | flops | bytes accessed | tf_op | source)
XLA Modules:
  0.0 33.8 jit_solution(14634891064478970047)
XLA Ops:
  0.6 6.4 %spread.1 = (f32[4,8,896]{2,1,0:T(8,128)S(1)}, f32[8,384]{1,0:T(8,128)S(1)}, f32[16,384]{1,0:T(8,128)S(1)}, f32[128,128]{1,0:T(8,128)S(1)}, f32[4,2,2,27,27]{4,3...) custom-call(f32[1,1,27,1,729]{4,3,2,1,0:T(1,128)} %bitcast.8, ...), custom_call_target="tpu_custom_call" | custom-call | flops 1000000000 | bytes 100000 | tf_op jit(solution)/shard_map/spread/pallas_call | solution.py:579
  7.1 25.4 %operator.1 = (f32[1,1,27,1,729]{4,3,2,1,0:T(1,128)S(1)}, f32[4,1,1,729]{3,2,1,0:T(1,128)S(1)}) custom-call(f32[4,8,896]{2,1,0:T(8,128)S(1)} %get-tuple-element.17.got, f32[8,384]{1,0:T(8,128)S(1)} %get-tuple-element.18.trace_own, f32[16,384]{1,0:T(8,128)S(1)} %get-tuple-element.19.fix_own, f32[128,128]{1,0:T(8,128)S(1)} %get-tuple-element.20.route_ref, ...), custom_call_target="tpu_custom_call" | custom-call | flops 10000000000 | bytes 4000000 | tf_op jit(solution)/shard_map/operator/pallas_call | solution.py:601
  32.5 0.6 %copy.18 = f32[1,1,1,27,729]{4,2,3,1,0:T(1,128)} copy(f32[1,1,1,27,729]{4,2,3,1,0:T(1,128)S(1)} %bitcast.6) | data formatting | bytes 157464
  33.2 0.6 %copy.19 = f32[4,1,1,729]{3,2,1,0:T(1,128)} copy(f32[4,1,1,729]{3,2,1,0:T(1,128)S(1)} %get-tuple-element.37) | data formatting | bytes 23328

commit v7 on v5

--- a/solution.py
+++ b/solution.py
@@ -192,10 +192,10 @@
     return tiles
 
 
-def ninth_layer(ref, at):
-    first = lax.broadcasted_iota(jnp.int32, (8, 768), 0) == 0
-    line = jnp.concatenate([ref[at, n:n + 1, 768:896] for n in range(6)], axis=1)
-    return jnp.where(first, line, 0.0)
+def slab_layers(ref, half, at):
+    first = lax.broadcasted_iota(jnp.int32, (8, 384), 0) == 0
+    line = jnp.concatenate([ref[half, at, n:n + 1, 384:512] for n in range(3)], axis=1)
+    return jnp.concatenate([ref[half, at, :, 0:384], jnp.where(first, line, 0.0)], axis=0)
 
 
 def routing(links_ref, y, z, core):
@@ -252,6 +252,8 @@
 
         return start, finish
 
+    load_x = pltpu.make_async_copy(x_hbm.at[0, 0, :, 0, :], x_ref, load_sem.at[0])
+    load_x.start()
     peers = [lax.rem(me + d, SUBS) for d in range(SUBS)]
     origins = [lax.rem(me + SUBS - d, SUBS) for d in range(SUBS)]
     barrier = pltpu.get_barrier_semaphore()
@@ -263,7 +265,6 @@
     rows = pl.ds(pl.multiple_of(me * SLAB, 8), SLAB)
     pairs = [(slot, s, n) for slot in range(4) for s in range(2) for n in range(2)]
     loads = [
-        [(x_hbm.at[0, 0, :, 0, :], x_ref)],
         [(links_hbm, links_ref)],
         [(links_hbm, counts_ref)],
         [(lagrange_hbm, lagrange_ref)],
@@ -275,7 +276,7 @@
         [(adj_value_hbm, adj_value_ref), (adj_slope_hbm, adj_slope_ref)],
         [(last_hbm.at[me], last_ref)],
     ]
-    loads = [[pltpu.make_async_copy(a, b, load_sem.at[n]) for a, b in some] for n, some in enumerate(loads)]
+    loads = [[pltpu.make_async_copy(a, b, load_sem.at[1 + n]) for a, b in some] for n, some in enumerate(loads)]
     for some in loads:
         for copy in some:
             copy.start()
@@ -285,13 +286,16 @@
             for copy in loads[n]:
                 copy.wait()
 
-    loaded(0)
+    load_x.wait()
     sent[...] = jnp.zeros_like(sent)
-    for q in range(SUBS):
-        sent[q, :, 0:729] = x_ref[6 * q:6 * q + 8, :]
-        for n in range(6):
-            width = min(128, 729 - 128 * n)
-            sent[q, n:n + 1, 768:768 + width] = x_ref[6 * q + 8:6 * q + 9, 128 * n:128 * n + width]
+    for half in range(2):
+        for q in range(SUBS):
+            width = min(384, 729 - 384 * half)
+            sent[half, q, :, 0:width] = x_ref[6 * q:6 * q + 8, 384 * half:384 * half + width]
+            for n in range(3):
+                lane = 384 * half + 128 * n
+                width = min(128, 729 - lane)
+                sent[half, q, n:n + 1, 384:384 + width] = x_ref[6 * q + 8:6 * q + 9, lane:lane + width]
     trace_rows = [[x_ref[26 * s:26 * s + 1, 128 * n:min(128 * n + 128, 729)] for n in range(6)] for s in range(2)]
     for s in range(2):
         tail = jnp.zeros((1, 768 - 729), jnp.float32)
@@ -310,17 +314,31 @@
     start_fixes, finish_fixes = exchange(2, lambda d: fix_own, fix_all, group, plane_from, plane_ids)
     start_sums, finish_sums = exchange(3, lambda d: fix_out.at[line[d]], fix_in, z, line_from, line_ids)
     pl.semaphore_wait(barrier, SUBS - 1 + 14)
-    going = [None]
-    for d in range(1, SUBS):
-        copy = pltpu.make_async_remote_copy(
-            src_ref=sent.at[peers[d]], dst_ref=got.at[me], send_sem=send_sem.at[d], recv_sem=recv_sem.at[d],
-            device_id={"sub": peers[d]}, device_id_type=MESH)
-        copy.start()
-        going.append(copy)
+    def sub_exchange(half, source, target, send, recv):
+        def one(d, at):
+            return pltpu.make_async_remote_copy(
+                src_ref=source.at[half, peers[d]], dst_ref=target.at[half, at], send_sem=send.at[half, d],
+                recv_sem=recv.at[half, d], device_id={"sub": peers[d]}, device_id_type=MESH)
+
+        def start():
+            for d in range(1, SUBS):
+                one(d, me).start()
+            target[half, me] = source[half, me]
+
+        def finish():
+            for d in range(1, SUBS):
+                one(d, me).wait_send()
+                one(d, origins[d]).wait_recv()
+
+        return start, finish
+
+    layers = [sub_exchange(half, sent, got, send_sem, recv_sem) for half in range(2)]
+    sums_home = [sub_exchange(half, back, home, back_send_sem, back_recv_sem) for half in range(2)]
+    layers[0][0]()
+    layers[1][0]()
     start_traces()
     trace_all[z] = trace_own[...]
-    got[me] = sent[me]
-    loaded(1, 2, 3, 4)
+    loaded(0, 1, 2, 3)
     row = lax.broadcasted_iota(jnp.int32, (BASIS, BASIS), 0)
     lefts, rights = [], []
     for s in range(2):
@@ -346,34 +364,34 @@
     fix_all[group] = fix_own[...]
     route = routing(links_ref, y, z, core)
     total[...] = jnp.zeros_like(total)
-    for d in range(1, SUBS):
-        going[d].wait_send()
-        pltpu.make_async_remote_copy(
-            src_ref=sent.at[peers[d]], dst_ref=got.at[origins[d]], send_sem=send_sem.at[d],
-            recv_sem=recv_sem.at[d], device_id={"sub": peers[d]}, device_id_type=MESH).wait_recv()
-
-    loaded(5)
+    layers[0][1]()
+    loaded(4)
     first = first_ref[...]
-    slabs = [jnp.concatenate([got[f, :, 0:768], ninth_layer(got, f)], axis=0) for f in range(FIELDS)]
-    lane = lanes_of(16)
-    columns = []
-    for j in range(BASIS):
-        tile, shift = divmod(BASIS * j, 128)
-        merged = None
-        for f in range(FIELDS):
-            piece = slabs[f][:, 128 * tile:128 * tile + 128]
-            if shift + BASIS > 128:
-                piece = jnp.where(lane >= shift, piece, slabs[f][:, 128 * tile + 128:128 * tile + 256])
-            turn = (32 * f - shift) % 128
-            piece = pltpu.roll(piece, turn, 1) if turn else piece
-            merged = piece if f == 0 else jnp.where(lane >= 32 * f, piece, merged)
-        high, low = split(merged)
-        columns.append(jnp.concatenate([high, low, high], axis=0))
-    for j in range(0, BASIS, 2):
-        result = product(first, jnp.concatenate(columns[j:j + 2], axis=1))
-        for n in range(min(2, BASIS - j)):
-            outer[j + n] = result[:, 128 * n:128 * n + 128]
-    loaded(6, 7, 8, 9, 10)
+
+    def first_stage(begin, end):
+        slabs = [jnp.concatenate([slab_layers(got, half, f) for half in range(1 + (end > 14))], axis=1)
+                 for f in range(FIELDS)]
+        lane = lanes_of(16)
+        columns = []
+        for j in range(begin, end):
+            tile, shift = divmod(BASIS * j, 128)
+            merged = None
+            for f in range(FIELDS):
+                piece = slabs[f][:, 128 * tile:128 * tile + 128]
+                if shift + BASIS > 128:
+                    piece = jnp.where(lane >= shift, piece, slabs[f][:, 128 * tile + 128:128 * tile + 256])
+                turn = (32 * f - shift) % 128
+                piece = pltpu.roll(piece, turn, 1) if turn else piece
+                merged = piece if f == 0 else jnp.where(lane >= 32 * f, piece, merged)
+            high, low = split(merged)
+            columns.append(jnp.concatenate([high, low, high], axis=0))
+        for j in range(begin, end, 2):
+            result = product(first, jnp.concatenate(columns[j - begin:j - begin + 2], axis=1))
+            for n in range(min(2, end - j)):
+                outer[j + n] = result[:, 128 * n:128 * n + 128]
+
+    first_stage(0, 14)
+    loaded(5, 6, 7, 8, 9)
 
     def step(t, carry):
         def scalar(table, bb, m):
@@ -449,7 +467,40 @@
             total[2 * t + m] += jnp.concatenate(sums[m], axis=0)
         return carry
 
-    lax.fori_loop(0, STEPS // 2, step, 0, unroll=2)
+    last = last_ref[...]
+
+    def last_stage(half):
+        lane = lanes_of(16)
+        packed = [[jnp.zeros((16, 128), jnp.float32) for _ in range(3)] for _ in range(FIELDS)]
+        begin, end = (0, 15) if half == 0 else (14, BASIS)
+        for j0 in range(begin, end, 2):
+            some = list(range(j0, min(j0 + 2, end)))
+            columns = []
+            for j in some:
+                high, low = split(total[j])
+                columns.append(jnp.concatenate([high, low, high], axis=0))
+            result = product(last, jnp.concatenate(columns, axis=1))
+            for n, j in enumerate(some):
+                piece = result[:, 128 * n:128 * n + 128]
+                tile, shift = divmod(BASIS * j, 128)
+                stop = shift + BASIS
+                at = tile - 3 * half
+                for f in range(FIELDS):
+                    turn = (shift - 32 * f) % 128
+                    turned = pltpu.roll(piece, turn, 1) if turn else piece
+                    if 0 <= at < 3:
+                        packed[f][at] = jnp.where((lane >= shift) & (lane < stop), turned, packed[f][at])
+                    if stop > 128 and 0 <= at + 1 < 3:
+                        packed[f][at + 1] = jnp.where(lane < stop - 128, turned, packed[f][at + 1])
+        for f in range(FIELDS):
+            for n in range(3):
+                back[half, f, :, 128 * n:128 * n + 128] = packed[f][n][0:8]
+                back[half, f, n:n + 1, 384:512] = packed[f][n][8:9]
+        sums_home[half][0]()
+
+    lax.fori_loop(0, 4, step, 0, unroll=4)
+    layers[1][1]()
+    first_stage(14, BASIS)
     finish_traces()
     high, low = split(trace_all[...].reshape(64, 384))
     both = (route + pltpu.roll(route, 64, 1)).astype(jnp.bfloat16)
@@ -463,41 +514,10 @@
                            jnp.concatenate([high, low], axis=0)).reshape(8, 8, 384)
     start_sums()
     fix_in[z] = fix_out[z]
-    lax.fori_loop(STEPS // 2, STEPS, step, 0, unroll=2)
-
-    last = last_ref[...]
-    lane = lanes_of(16)
-    packed = [[jnp.zeros((16, 128), jnp.float32) for _ in range(6)] for _ in range(FIELDS)]
-    for j0 in range(0, BASIS, 2):
-        some = list(range(j0, min(j0 + 2, BASIS)))
-        columns = []
-        for j in some:
-            high, low = split(total[j])
-            columns.append(jnp.concatenate([high, low, high], axis=0))
-        result = product(last, jnp.concatenate(columns, axis=1))
-        for n, j in enumerate(some):
-            piece = result[:, 128 * n:128 * n + 128]
-            tile, shift = divmod(BASIS * j, 128)
-            for f in range(FIELDS):
-                turn = (shift - 32 * f) % 128
-                turned = pltpu.roll(piece, turn, 1) if turn else piece
-                end = shift + BASIS
-                mask = (lane >= shift) & (lane < end)
-                packed[f][tile] = jnp.where(mask, turned, packed[f][tile])
-                if end > 128:
-                    packed[f][tile + 1] = jnp.where(lane < end - 128, turned, packed[f][tile + 1])
-    for f in range(FIELDS):
-        for n in range(6):
-            back[f, :, 128 * n:128 * n + 128] = packed[f][n][0:8]
-            back[f, n:n + 1, 768:896] = packed[f][n][8:9]
-    going = [None]
-    for d in range(1, SUBS):
-        copy = pltpu.make_async_remote_copy(
-            src_ref=back.at[peers[d]], dst_ref=home.at[me], send_sem=back_send_sem.at[d],
-            recv_sem=back_recv_sem.at[d], device_id={"sub": peers[d]}, device_id_type=MESH)
-        copy.start()
-        going.append(copy)
-    home[me] = back[me]
+    lax.fori_loop(4, 8, step, 0, unroll=4)
+    last_stage(0)
+    lax.fori_loop(8, STEPS, step, 0, unroll=4)
+    last_stage(1)
     finish_picked()
     picked = trace_in[0]
     for at in range(1, 8):
@@ -525,20 +545,25 @@
     far = jnp.where(inside, grid[pl.ds(3, BASIS, stride=8), :], 0.0)
     far = pltpu.roll(far, 62, 1)
     ends = jnp.concatenate(sums, axis=1)
-    for d in range(1, SUBS):
-        going[d].wait_send()
-        pltpu.make_async_remote_copy(
-            src_ref=back.at[peers[d]], dst_ref=home.at[origins[d]], send_sem=back_send_sem.at[d],
-            recv_sem=back_recv_sem.at[d], device_id={"sub": peers[d]}, device_id_type=MESH).wait_recv()
+    sums_home[0][1]()
+    sums_home[1][1]()
     x_ref[...] = jnp.zeros((BASIS, BASIS * BASIS), jnp.float32)
     for q in range(SUBS):
-        x_ref[6 * q:6 * q + 8, :] += home[q, :, 0:729]
-        x_ref[6 * q + 8:6 * q + 9, :] += ninth_layer(home, q)[0:1, 0:729]
+        layers_q = jnp.concatenate([slab_layers(home, half, q) for half in range(2)], axis=1)
+        x_ref[6 * q:6 * q + LAYERS, :] += layers_q[0:LAYERS, 0:729]
     for s in range(2):
         x_ref[26 * s:26 * s + 1, :] += ends[s:s + 1, 0:729]
     x_ref[:, 0:128] += near
     x_ref[:, 640:729] += far[:, 0:89]
     out_ref[0, 0, :, 0, :] = x_ref[...]
+
+
+def store_kernel(result, jumps, result_hbm, jumps_hbm, sems):
+    copies = [pltpu.make_async_copy(result, result_hbm, sems.at[0]), pltpu.make_async_copy(jumps, jumps_hbm, sems.at[1])]
+    for copy in copies:
+        copy.start()
+    for copy in copies:
+        copy.wait()
 
 
 def per_device(state, stiff_weight, volume_weight, lagrange, mortar, links):
@@ -563,10 +588,10 @@
             pltpu.SMEM(local[-1], jnp.float32),
             pltpu.VMEM((SLAB, QUAD * QUAD), jnp.float32),
             pltpu.VMEM((SLAB, QUAD * QUAD), jnp.float32),
-            pltpu.VMEM((SUBS, 8, 896), jnp.float32),
-            pltpu.VMEM((SUBS, 8, 896), jnp.float32),
-            pltpu.VMEM((SUBS, 8, 896), jnp.float32),
-            pltpu.VMEM((SUBS, 8, 896), jnp.float32),
+            pltpu.VMEM((2, SUBS, 8, 512), jnp.float32),
+            pltpu.VMEM((2, SUBS, 8, 512), jnp.float32),
+            pltpu.VMEM((2, SUBS, 8, 512), jnp.float32),
+            pltpu.VMEM((2, SUBS, 8, 512), jnp.float32),
             pltpu.VMEM((BASIS, 2 * SLAB, 128), jnp.float32),
             pltpu.VMEM((BASIS, 2 * SLAB, 128), jnp.float32),
             pltpu.VMEM((BASIS * 8, 128), jnp.float32),
@@ -579,10 +604,10 @@
             pltpu.VMEM((8, 8, 384), jnp.float32),
             pltpu.VMEM((8, 8, 384), jnp.float32),
             pltpu.SemaphoreType.DMA((11,)),
-            pltpu.SemaphoreType.DMA((SUBS,)),
-            pltpu.SemaphoreType.DMA((SUBS,)),
-            pltpu.SemaphoreType.DMA((SUBS,)),
-            pltpu.SemaphoreType.DMA((SUBS,)),
+            pltpu.SemaphoreType.DMA((2, SUBS)),
+            pltpu.SemaphoreType.DMA((2, SUBS)),
+            pltpu.SemaphoreType.DMA((2, SUBS)),
+            pltpu.SemaphoreType.DMA((2, SUBS)),
             pltpu.SemaphoreType.DMA((4, 8)),
             pltpu.SemaphoreType.DMA((4, 8)),
         ],
@@ -591,6 +616,15 @@
     )(*[pltpu.with_memory_space_constraint(x, pltpu.HBM) for x in (
         jnp.transpose(state, (0, 1, 3, 2, 4)), stiff_weight, volume_weight, lagrange,
         jnp.transpose(mortar, (0, 1, 3, 2, 4)), links.T, *constants)])
+    result, jumps = pl.pallas_call(
+        store_kernel,
+        name="store",
+        out_shape=(jax.ShapeDtypeStruct(result.shape, jnp.float32), jax.ShapeDtypeStruct(jumps.shape, jnp.float32)),
+        in_specs=[vmem, vmem],
+        out_specs=(anywhere, anywhere),
+        scratch_shapes=[pltpu.SemaphoreType.DMA((2,))],
+        compiler_params=pltpu.CompilerParams(vmem_limit_bytes=2 * 10**6),
+    )(result, jumps)
     return jnp.transpose(result, (0, 1, 3, 2, 4)), jumps
 
 

time: 30.1 us -> 27.9 us (0.927)
  local copies, waits for them, and re-layouts: 1.24 us -> 0 us
  Pallas kernels: 28.1 us -> 27 us
    pallas_call x1, Pallas kernels: 28.1 us -> 26.3 us  [per_device(): pl.pallas_call(operator_kernel, name='operator', out_shape=(jax.ShapeDtyp...]
    unnamed x2 -> x0, local copies, waits for them, and re-layouts: 1.24 us -> none
    pallas_call x0 -> x1, Pallas kernels: none -> 0.66 us  [per_device(): pl.pallas_call(store_kernel, name='store', out_shape=(jax.ShapeDtypeStruc...]
where the time goes in v7:
time: 27.9 us; the launch traced here: 27.6 us
  Pallas kernels  27 us (97%)
  between operations  0.64 us (2%)
    pallas_call x1, Pallas kernels, per_device(): pl.pallas_call(operator_kernel, name='operator', out_shape=(jax.ShapeDtyp...  26.3 us
    pallas_call x1, Pallas kernels, per_device(): pl.pallas_call(store_kernel, name='store', out_shape=(jax.ShapeDtypeStruc...  0.66 us

profile of v7, /device:TPU:1, one launch (start us, length us, event | category | flops | bytes accessed | tf_op | source)
XLA Modules:
  0.0 27.6 jit_solution(17671874767503736567)
XLA Ops:
  0.6 26.3 %operator.1 = (f32[1,1,27,1,729]{4,3,2,1,0:T(1,128)S(1)}, f32[4,1,1,729]{3,2,1,0:T(1,128)S(1)}) custom-call(f32[1,1,27,1,729]{4,3,2,1,0:T(1,128)} %bitcast.7, f32[1,96,9216]{2,1,0:T(8,128)} %stiff_hbm.1, f32[1,96,9216]{2,1,0:T(8,128)} %volume_hbm.1, f32[4,1,1,729]{3,2,1,0:T(1,128)} %lagrange_hbm.1, f32[4,2,27,2,27]{4,3,2,1,0:T(2,128)} %bitcast.6, ...), custom_call_target="tpu_custom_call" | custom-call | flops 10000000000 | bytes 4000000 | tf_op jit(solution)/shard_map/operator/pallas_call | solution.py:574
  27.0 0.7 %store.1 = (f32[1,1,27,1,729]{4,3,2,1,0:T(1,128)}, f32[4,1,1,729]{3,2,1,0:T(1,128)}) custom-call(f32[1,1,27,1,729]{4,3,2,1,0:T(1,128)S(1)} %get-tuple-element.6.result, f32[4,1,1,729]{3,2,1,0:T(1,128)S(1)} %get-tuple-element.7.jumps), custom_call_target="tpu_custom_call" | custom-call | tf_op jit(solution)/shard_map/store/pallas_call | solution.py:619

commit v8 on v7

--- a/solution.py
+++ b/solution.py
@@ -221,9 +221,11 @@
 def operator_kernel(x_hbm, stiff_hbm, volume_hbm, lagrange_hbm, mortar_hbm, links_hbm, first_hbm, last_hbm,
                     inner_hbm, plain_hbm, adj_value_hbm, adj_slope_hbm, middle_hbm, out_ref, jump_ref,
                     x_ref, lagrange_ref, mortar_ref, links_ref, counts_ref, first_ref, last_ref, inner_ref,
-                    plain_ref, adj_value_ref, adj_slope_ref, middle_ref, stiff, volume, sent, got, back, home, outer, total, grid, trace_own, trace_all,
+                    plain_ref, adj_value_ref, adj_slope_ref, middle_ref, stiff, volume, sent, got, back, home, outer, total, picks, grid, trace_own, trace_all,
                     trace_out, trace_in, fix_own, fix_all, fix_out, fix_in, load_sem, send_sem, recv_sem,
                     back_send_sem, back_recv_sem, face_send_sem, face_recv_sem):
+    load_x = pltpu.make_async_copy(x_hbm.at[0, 0, :, 0, :], x_ref, load_sem.at[0])
+    load_x.start()
     me = lax.axis_index("sub")
     patch = lax.axis_index("patch")
     y, z, core = patch // 16, (patch // 2) % 8, patch % 2
@@ -252,16 +254,15 @@
 
         return start, finish
 
-    load_x = pltpu.make_async_copy(x_hbm.at[0, 0, :, 0, :], x_ref, load_sem.at[0])
-    load_x.start()
     peers = [lax.rem(me + d, SUBS) for d in range(SUBS)]
     origins = [lax.rem(me + SUBS - d, SUBS) for d in range(SUBS)]
     barrier = pltpu.get_barrier_semaphore()
+    for d in (4, 3, 5, 2, 6, 1, 7):
+        pl.semaphore_signal(barrier, inc=1, device_id=line_ids[d], device_id_type=MESH)
     for d in range(1, SUBS):
         pl.semaphore_signal(barrier, inc=1, device_id={"sub": peers[d]}, device_id_type=MESH)
     for d in range(1, 8):
-        for ids in (line_ids, plane_ids):
-            pl.semaphore_signal(barrier, inc=1, device_id=ids[d], device_id_type=MESH)
+        pl.semaphore_signal(barrier, inc=1, device_id=plane_ids[d], device_id_type=MESH)
     rows = pl.ds(pl.multiple_of(me * SLAB, 8), SLAB)
     pairs = [(slot, s, n) for slot in range(4) for s in range(2) for n in range(2)]
     loads = [
@@ -363,6 +364,10 @@
     start_fixes()
     fix_all[group] = fix_own[...]
     route = routing(links_ref, y, z, core)
+    picks[0] = (route + pltpu.roll(route, 64, 1)).astype(jnp.bfloat16)
+    flipped = route.T.astype(jnp.bfloat16)[0:64]
+    flipped = jnp.concatenate([flipped, flipped], axis=1)
+    picks[1] = jnp.concatenate([flipped[:, 0:128], flipped[:, 128:256]], axis=0)
     total[...] = jnp.zeros_like(total)
     layers[0][1]()
     loaded(4)
@@ -500,20 +505,18 @@
 
     lax.fori_loop(0, 4, step, 0, unroll=4)
     layers[1][1]()
-    first_stage(14, BASIS)
     finish_traces()
     high, low = split(trace_all[...].reshape(64, 384))
-    both = (route + pltpu.roll(route, 64, 1)).astype(jnp.bfloat16)
-    trace_out[...] = product(both, jnp.concatenate([high, low], axis=0)).reshape(8, 16, 384)
+    trace_out[...] = product(picks[0], jnp.concatenate([high, low], axis=0)).reshape(8, 16, 384)
     start_picked()
     trace_in[group] = trace_out[group]
     finish_fixes()
     high, low = split(fix_all[...].reshape(128, 384))
-    flipped = route.T.astype(jnp.bfloat16)[0:64]
-    fix_out[...] = product(jnp.concatenate([flipped, flipped], axis=1),
+    fix_out[...] = product(jnp.concatenate([picks[1, 0:64], picks[1, 64:128]], axis=1),
                            jnp.concatenate([high, low], axis=0)).reshape(8, 8, 384)
     start_sums()
     fix_in[z] = fix_out[z]
+    first_stage(14, BASIS)
     lax.fori_loop(4, 8, step, 0, unroll=4)
     last_stage(0)
     lax.fori_loop(8, STEPS, step, 0, unroll=4)
@@ -594,6 +597,7 @@
             pltpu.VMEM((2, SUBS, 8, 512), jnp.float32),
             pltpu.VMEM((BASIS, 2 * SLAB, 128), jnp.float32),
             pltpu.VMEM((BASIS, 2 * SLAB, 128), jnp.float32),
+            pltpu.VMEM((2, 128, 128), jnp.bfloat16),
             pltpu.VMEM((BASIS * 8, 128), jnp.float32),
             pltpu.VMEM((8, 384), jnp.float32),
             pltpu.VMEM((8, 8, 384), jnp.float32),

time: 27.9 us -> 28.3 us (1.014)
  Pallas kernels: 27 us -> 27.6 us
    pallas_call x1, Pallas kernels: 26.3 us -> 26.9 us  [per_device(): pl.pallas_call(operator_kernel, name='operator', out_shape=(jax.ShapeDtyp...]
where the time goes in v8:
time: 28.3 us; the launch traced here: 28.2 us
  Pallas kernels  27.6 us (98%)
  between operations  0.64 us (2%)
    pallas_call x1, Pallas kernels, per_device(): pl.pallas_call(operator_kernel, name='operator', out_shape=(jax.ShapeDtyp...  26.9 us
    pallas_call x1, Pallas kernels, per_device(): pl.pallas_call(store_kernel, name='store', out_shape=(jax.ShapeDtypeStruc...  0.66 us

profile of v8, /device:TPU:1, one launch (start us, length us, event | category | flops | bytes accessed | tf_op | source)
XLA Modules:
  0.0 28.2 jit_solution(6884448315994649574)
XLA Ops:
  0.6 26.9 %operator.1 = (f32[1,1,27,1,729]{4,3,2,1,0:T(1,128)S(1)}, f32[4,1,1,729]{3,2,1,0:T(1,128)S(1)}) custom-call(f32[1,1,27,1,729]{4,3,2,1,0:T(1,128)} %bitcast.7, f32[1,96,9216]{2,1,0:T(8,128)} %stiff_hbm.1, f32[1,96,9216]{2,1,0:T(8,128)} %volume_hbm.1, f32[4,1,1,729]{3,2,1,0:T(1,128)} %lagrange_hbm.1, f32[4,2,27,2,27]{4,3,2,1,0:T(2,128)} %bitcast.6, ...), custom_call_target="tpu_custom_call" | custom-call | flops 10000000000 | bytes 4000000 | tf_op jit(solution)/shard_map/operator/pallas_call | solution.py:577
  27.6 0.7 %store.1 = (f32[1,1,27,1,729]{4,3,2,1,0:T(1,128)}, f32[4,1,1,729]{3,2,1,0:T(1,128)}) custom-call(f32[1,1,27,1,729]{4,3,2,1,0:T(1,128)S(1)} %get-tuple-element.6.result, f32[4,1,1,729]{3,2,1,0:T(1,128)S(1)} %get-tuple-element.7.jumps), custom_call_target="tpu_custom_call" | custom-call | tf_op jit(solution)/shard_map/store/pallas_call | solution.py:623

commit v9 on v7

--- a/solution.py
+++ b/solution.py
@@ -224,6 +224,8 @@
                     plain_ref, adj_value_ref, adj_slope_ref, middle_ref, stiff, volume, sent, got, back, home, outer, total, grid, trace_own, trace_all,
                     trace_out, trace_in, fix_own, fix_all, fix_out, fix_in, load_sem, send_sem, recv_sem,
                     back_send_sem, back_recv_sem, face_send_sem, face_recv_sem):
+    load_x = pltpu.make_async_copy(x_hbm.at[0, 0, :, 0, :], x_ref, load_sem.at[0])
+    load_x.start()
     me = lax.axis_index("sub")
     patch = lax.axis_index("patch")
     y, z, core = patch // 16, (patch // 2) % 8, patch % 2
@@ -242,7 +244,7 @@
                 recv_sem=face_recv_sem.at[n, d], device_id=ids[d], device_id_type=MESH)
 
         def start():
-            for d in range(1, 8):
+            for d in (4, 3, 5, 2, 6, 1, 7):
                 one(d, slot).start()
 
         def finish():
@@ -252,8 +254,6 @@
 
         return start, finish
 
-    load_x = pltpu.make_async_copy(x_hbm.at[0, 0, :, 0, :], x_ref, load_sem.at[0])
-    load_x.start()
     peers = [lax.rem(me + d, SUBS) for d in range(SUBS)]
     origins = [lax.rem(me + SUBS - d, SUBS) for d in range(SUBS)]
     barrier = pltpu.get_barrier_semaphore()
@@ -321,7 +321,7 @@
                 recv_sem=recv.at[half, d], device_id={"sub": peers[d]}, device_id_type=MESH)
 
         def start():
-            for d in range(1, SUBS):
+            for d in (2, 1, 3):
                 one(d, me).start()
             target[half, me] = source[half, me]
 

time: 27.9 us -> 27.7 us (level)
  the two profiles are of different devices: /device:TPU:1 before, /device:TPU:16 now
where the time goes in v9:
time: 27.7 us; the launch traced here: 27.6 us
  Pallas kernels  27 us (97%)
  between operations  0.64 us (2%)
    pallas_call x1, Pallas kernels, per_device(): pl.pallas_call(operator_kernel, name='operator', out_shape=(jax.ShapeDtyp...  26.4 us
    pallas_call x1, Pallas kernels, per_device(): pl.pallas_call(store_kernel, name='store', out_shape=(jax.ShapeDtypeStruc...  0.66 us

profile of v9, /device:TPU:16, one launch (start us, length us, event | category | flops | bytes accessed | tf_op | source)
XLA Modules:
  0.0 27.6 jit_solution(2597375314422178790)
XLA Ops:
  0.6 26.4 %operator.1 = (f32[1,1,27,1,729]{4,3,2,1,0:T(1,128)S(1)}, f32[4,1,1,729]{3,2,1,0:T(1,128)S(1)}) custom-call(f32[1,1,27,1,729]{4,3,2,1,0:T(1,128)} %bitcast.7, f32[1,96,9216]{2,1,0:T(8,128)} %stiff_hbm.1, f32[1,96,9216]{2,1,0:T(8,128)} %volume_hbm.1, f32[4,1,1,729]{3,2,1,0:T(1,128)} %lagrange_hbm.1, f32[4,2,27,2,27]{4,3,2,1,0:T(2,128)} %bitcast.6, ...), custom_call_target="tpu_custom_call" | custom-call | flops 10000000000 | bytes 4000000 | tf_op jit(solution)/shard_map/operator/pallas_call | solution.py:574
  27.0 0.7 %store.1 = (f32[1,1,27,1,729]{4,3,2,1,0:T(1,128)}, f32[4,1,1,729]{3,2,1,0:T(1,128)}) custom-call(f32[1,1,27,1,729]{4,3,2,1,0:T(1,128)S(1)} %get-tuple-element.6.result, f32[4,1,1,729]{3,2,1,0:T(1,128)S(1)} %get-tuple-element.7.jumps), custom_call_target="tpu_custom_call" | custom-call | tf_op jit(solution)/shard_map/store/pallas_call | solution.py:619

commit v10 on v9

--- a/solution.py
+++ b/solution.py
@@ -555,11 +555,11 @@
         x_ref[26 * s:26 * s + 1, :] += ends[s:s + 1, 0:729]
     x_ref[:, 0:128] += near
     x_ref[:, 640:729] += far[:, 0:89]
-    out_ref[0, 0, :, 0, :] = x_ref[...]
+    out_ref[...] = x_ref[...]
 
 
 def store_kernel(result, jumps, result_hbm, jumps_hbm, sems):
-    copies = [pltpu.make_async_copy(result, result_hbm, sems.at[0]), pltpu.make_async_copy(jumps, jumps_hbm, sems.at[1])]
+    copies = [pltpu.make_async_copy(result, result_hbm.at[0, 0, :, 0, :], sems.at[0]), pltpu.make_async_copy(jumps, jumps_hbm, sems.at[1])]
     for copy in copies:
         copy.start()
     for copy in copies:
@@ -574,7 +574,7 @@
     result, jumps = pl.pallas_call(
         operator_kernel,
         name="operator",
-        out_shape=(jax.ShapeDtypeStruct((1, 1, BASIS, 1, BASIS * BASIS), jnp.float32),
+        out_shape=(jax.ShapeDtypeStruct((BASIS, BASIS * BASIS), jnp.float32),
                    jax.ShapeDtypeStruct(lagrange.shape, jnp.float32)),
         in_specs=[anywhere] * 13,
         out_specs=(vmem, vmem),
@@ -594,7 +594,7 @@
             pltpu.VMEM((2, SUBS, 8, 512), jnp.float32),
             pltpu.VMEM((BASIS, 2 * SLAB, 128), jnp.float32),
             pltpu.VMEM((BASIS, 2 * SLAB, 128), jnp.float32),
-            pltpu.VMEM((BASIS * 8, 128), jnp.float32),
+            pltpu.VMEM((256, 128), jnp.float32),
             pltpu.VMEM((8, 384), jnp.float32),
             pltpu.VMEM((8, 8, 384), jnp.float32),
             pltpu.VMEM((8, 16, 384), jnp.float32),
@@ -619,7 +619,7 @@
     result, jumps = pl.pallas_call(
         store_kernel,
         name="store",
-        out_shape=(jax.ShapeDtypeStruct(result.shape, jnp.float32), jax.ShapeDtypeStruct(jumps.shape, jnp.float32)),
+        out_shape=(jax.ShapeDtypeStruct((1, 1, BASIS, 1, BASIS * BASIS), jnp.float32), jax.ShapeDtypeStruct(jumps.shape, jnp.float32)),
         in_specs=[vmem, vmem],
         out_specs=(anywhere, anywhere),
         scratch_shapes=[pltpu.SemaphoreType.DMA((2,))],

time: 27.7 us -> 27.7 us (level)
  no operation moved by 1% of the time
where the time goes in v10:
time: 27.7 us; the launch traced here: 27.6 us
  Pallas kernels  27 us (97%)
  between operations  0.64 us (2%)
    pallas_call x1, Pallas kernels, per_device(): pl.pallas_call(operator_kernel, name='operator', out_shape=(jax.ShapeDtyp...  26.3 us
    pallas_call x1, Pallas kernels, per_device(): pl.pallas_call(store_kernel, name='store', out_shape=(jax.ShapeDtypeStruc...  0.66 us

profile of v10, /device:TPU:16, one launch (start us, length us, event | category | flops | bytes accessed | tf_op | source)
XLA Modules:
  0.0 27.6 jit_solution(16882743547794242410)
XLA Ops:
  0.6 26.3 %operator.1 = (f32[27,729]{1,0:T(8,128)S(1)}, f32[4,1,1,729]{3,2,1,0:T(1,128)S(1)}) custom-call(f32[1,1,27,1,729]{4,3,2,1,0:T(1,128)} %bitcast.7, f32[1,96,9216]{2,1,0:T(8,128)} %stiff_hbm.1, f32[1,96,9216]{2,1,0:T(8,128)} %volume_hbm.1, f32[4,1,1,729]{3,2,1,0:T(1,128)} %lagrange_hbm.1, f32[4,2,27,2,27]{4,3,2,1,0:T(2,128)} %bitcast.6, s32[6,256]{1,0:T(8,128)} %bitcast.9, ...), custom_call_target="tpu_custom_call" | custom-call | flops 10000000000 | bytes 4000000 | tf_op jit(solution)/shard_map/operator/pallas_call | solution.py:574
  27.0 0.7 %store.1 = (f32[1,1,27,1,729]{4,3,2,1,0:T(1,128)}, f32[4,1,1,729]{3,2,1,0:T(1,128)}) custom-call(f32[27,729]{1,0:T(8,128)S(1)} %get-tuple-element.6.result, f32[4,1,1,729]{3,2,1,0:T(1,128)S(1)} %get-tuple-element.7.jumps), custom_call_target="tpu_custom_call" | custom-call | tf_op jit(solution)/shard_map/store/pallas_call | solution.py:619
